TPU v7x, 32 devices: a whole 2x2x4 slice. The times are simulated.
32 devices in a mesh: rep: 2 (over x), fsdp: 16 (over z, y, core).
Axes of the slice: x: 2, y: 2, z: 4, core: 2. Of those that a mesh axis runs over, the one named last changes fastest.
Arguments:
- x_in: bfloat16 [32, 256, 1536], P(('rep', 'fsdp')), may hold values from -6 to 6
- doc_ids: int32 [32, 256], P(('rep', 'fsdp')), may hold values from 0 to 3, never falling along the last dimension, each value on 1 to 128 neighbouring positions
- w_qkv: bfloat16 [1536, 4608], P('fsdp'), may hold values from -0.15625 to 0.15625
- w_out: bfloat16 [1536, 1536], P('fsdp'), may hold values from -0.15625 to 0.15625
- gain_attn: bfloat16 [1536], P('fsdp'), may hold values from 0.5 to 1.5
- gain_group: bfloat16 [1536], P('fsdp'), may hold values from 0.5 to 1.5
- conv_kernel: float32 [16, 6, 11], replicated, may hold values from -0.8 to 0.8
- head_mix: float32 [16, 2], replicated, may hold values from 0.1 to 1
- gain_ffn: bfloat16 [1536], P('fsdp'), may hold values from 0.5 to 1.5
- w_gate: bfloat16 [1536, 4096], P('fsdp'), may hold values from -0.15625 to 0.15625
- w_up: bfloat16 [1536, 4096], P('fsdp'), may hold values from -0.15625 to 0.15625
- w_down: bfloat16 [4096, 1536], P('fsdp'), may hold values from -0.09375 to 0.09375
- cotangent: bfloat16 [32, 256, 1536], P(('rep', 'fsdp')), may hold values from -6 to 6
Outputs:
- out: bfloat16 [32, 256, 1536], P(('rep', 'fsdp'))
- grad_x: float32 [32, 256, 1536], P(('rep', 'fsdp'))
- grad_qkv: float32 [1536, 4608], P('fsdp')
- grad_out: float32 [1536, 1536], P('fsdp')
- grad_gain_attn: float32 [1536], P('fsdp')
- grad_gain_group: float32 [1536], P('fsdp')
- grad_conv: float32 [16, 6, 11], replicated
- grad_mix: float32 [16, 2], replicated
- grad_gain_ffn: float32 [1536], P('fsdp')
- grad_gate: float32 [1536, 4096], P('fsdp')
- grad_up: float32 [1536, 4096], P('fsdp')
- grad_down: float32 [4096, 1536], P('fsdp')
Inputs may be any that keep to these rules, and one draw needn't show every extreme that they name: `doc_ids`: within each packed row the document ids never fall, and each document holds at most 128 tokens.
All inputs are finite; a program needn't handle non-finite values.
Results may differ from a plain program's by a relative error of at most 0.017.
Values may be sent and summed in bfloat16 or wider, within the bound.
A program may use at most 320 MiB of HBM per device.

v0:
```python
import math

import jax
import jax.numpy as jnp
from jax import lax
from jax.sharding import PartitionSpec as P

MODEL_WIDTH = 1536
H = 16
E = 96
QWIN = 6
KWIN = 11


def rms_scale(values, epsilon):
    return lax.rsqrt(jnp.mean(values * values, axis=1, keepdims=True) + epsilon)


def convolve(zeroed, kernel):
    sequence_length = zeroed.shape[1]
    padded = jnp.pad(zeroed, ((0, 0), (QWIN - 1, 0), (KWIN - 1, 0)))
    total = jnp.zeros_like(zeroed)
    for row_shift in range(QWIN):
        for col_shift in range(KWIN):
            row_start = QWIN - 1 - row_shift
            col_start = KWIN - 1 - col_shift
            window = padded[
                :, row_start : row_start + sequence_length, col_start : col_start + sequence_length
            ]
            total = total + kernel[:, row_shift, col_shift][:, None, None] * window
    return total


def convolve_back(upstream, zeroed, kernel):
    sequence_length = upstream.shape[1]
    padded_up = jnp.pad(upstream, ((0, 0), (0, QWIN - 1), (0, KWIN - 1)))
    padded_zero = jnp.pad(zeroed, ((0, 0), (QWIN - 1, 0), (KWIN - 1, 0)))
    total = jnp.zeros_like(upstream)
    kernel_rows = []
    for row_shift in range(QWIN):
        row_terms = []
        for col_shift in range(KWIN):
            ahead = padded_up[
                :, row_shift : row_shift + sequence_length, col_shift : col_shift + sequence_length
            ]
            total = total + kernel[:, row_shift, col_shift][:, None, None] * ahead
            row_start = QWIN - 1 - row_shift
            col_start = KWIN - 1 - col_shift
            behind = padded_zero[
                :, row_start : row_start + sequence_length, col_start : col_start + sequence_length
            ]
            row_terms.append(jnp.sum(upstream * behind, axis=(1, 2)))
        kernel_rows.append(jnp.stack(row_terms, axis=1))
    return (total, jnp.stack(kernel_rows, axis=1))


def attend_maps(queries, key_rows, allowed, kernel, scale):
    raw_scores = (
        jnp.einsum("ihe,jhe->hij", queries, key_rows, preferred_element_type=jnp.float32) * scale
    )
    zeroed = jnp.where(allowed, raw_scores, 0.0)
    return (zeroed, convolve(zeroed, kernel))


def mix_heads(probs, head_mix):
    heads = probs.shape[0]
    sequence_length = probs.shape[1]
    grouped = probs.reshape(heads // 2, 2, sequence_length, sequence_length)
    table = head_mix.reshape(heads // 2, 2, 2)
    mixed = (
        table[:, :, 0, None, None] * grouped[:, 0:1] + table[:, :, 1, None, None] * grouped[:, 1:2]
    )
    return mixed.reshape(heads, sequence_length, sequence_length)


def per_device(
    x_in,
    doc_ids,
    w_qkv,
    w_out,
    gain_attn,
    gain_group,
    conv_kernel,
    head_mix,
    gain_ffn,
    w_gate,
    w_up,
    w_down,
    cotangent,
):
    sequence_length = x_in.shape[1]
    scale = 1.0 / math.sqrt(E)
    full_qkv, full_out, full_gain_attn, full_gain_group = (
        lax.all_gather(w_qkv, "fsdp", axis=0, tiled=True),
        lax.all_gather(w_out, "fsdp", axis=0, tiled=True),
        lax.all_gather(gain_attn, "fsdp", axis=0, tiled=True),
        lax.all_gather(gain_group, "fsdp", axis=0, tiled=True),
    )
    tokens = x_in[0].astype(jnp.float32)
    positions = jnp.arange(sequence_length)
    documents = doc_ids[0]
    allowed = (positions[None, :] <= positions[:, None]) & (
        documents[:, None] == documents[None, :]
    )
    scale_in = rms_scale(tokens, 1e-06)
    gain_in = full_gain_attn.astype(jnp.float32)
    normed_in = (tokens * scale_in * gain_in).astype(jnp.bfloat16)
    projected = jnp.dot(normed_in, full_qkv, preferred_element_type=jnp.float32).astype(
        jnp.bfloat16
    )
    queries = projected[:, :MODEL_WIDTH].reshape(sequence_length, H, E)
    key_rows = projected[:, MODEL_WIDTH : 2 * MODEL_WIDTH].reshape(sequence_length, H, E)
    value_rows = projected[:, 2 * MODEL_WIDTH :].reshape(sequence_length, H, E)
    zeroed, convolved = attend_maps(queries, key_rows, allowed, conv_kernel, scale)
    masked = jnp.where(allowed, convolved, -jnp.inf)
    top_score = jnp.max(masked, axis=2, keepdims=True)
    exp_scores = jnp.exp(masked - top_score)
    exp_totals = jnp.sum(exp_scores, axis=2, keepdims=True)
    probs = exp_scores / exp_totals
    log_total = top_score + jnp.log(exp_totals)
    mixed = mix_heads(probs, head_mix).astype(jnp.bfloat16)
    heads_out = jnp.einsum("hij,jhe->ihe", mixed, value_rows, preferred_element_type=jnp.float32)
    mean_removed = heads_out - jnp.mean(heads_out, axis=2, keepdims=True)
    inverse_deviation = lax.rsqrt(
        jnp.mean(mean_removed * mean_removed, axis=2, keepdims=True) + 1e-05
    )
    normalized_input = mean_removed * inverse_deviation
    group_scale_factor = full_gain_group.astype(jnp.float32).reshape(H, E)
    head_normalized = (
        (normalized_input * group_scale_factor)
        .reshape(sequence_length, MODEL_WIDTH)
        .astype(jnp.bfloat16)
    )
    resid = tokens + jnp.dot(head_normalized, full_out, preferred_element_type=jnp.float32)
    full_gate, full_up, full_down, full_gain_ffn = (
        lax.all_gather(w_gate, "fsdp", axis=0, tiled=True),
        lax.all_gather(w_up, "fsdp", axis=0, tiled=True),
        lax.all_gather(w_down, "fsdp", axis=0, tiled=True),
        lax.all_gather(gain_ffn, "fsdp", axis=0, tiled=True),
    )
    scale_mid = rms_scale(resid, 1e-06)
    gain_mid = full_gain_ffn.astype(jnp.float32)
    normed_mid = (resid * scale_mid * gain_mid).astype(jnp.bfloat16)
    gate_act = jnp.dot(normed_mid, full_gate, preferred_element_type=jnp.float32)
    up_act = jnp.dot(normed_mid, full_up, preferred_element_type=jnp.float32)
    sigmoid_gate = jax.nn.sigmoid(gate_act)
    silu_gate = gate_act * sigmoid_gate
    hidden = (silu_gate * up_act).astype(jnp.bfloat16)
    output = resid + jnp.dot(hidden, full_down, preferred_element_type=jnp.float32)
    upstream = cotangent[0].astype(jnp.float32)
    full_gate, full_up, full_down, full_gain_ffn = (
        lax.all_gather(w_gate, "fsdp", axis=0, tiled=True),
        lax.all_gather(w_up, "fsdp", axis=0, tiled=True),
        lax.all_gather(w_down, "fsdp", axis=0, tiled=True),
        lax.all_gather(gain_ffn, "fsdp", axis=0, tiled=True),
    )
    gain_mid = full_gain_ffn.astype(jnp.float32)
    back_ffn = upstream.astype(jnp.bfloat16)
    sum_down = jnp.dot(hidden.T, back_ffn, preferred_element_type=jnp.float32)
    back_hidden = jnp.dot(back_ffn, full_down.T, preferred_element_type=jnp.float32)
    back_gate = (
        back_hidden * up_act * sigmoid_gate * (1.0 + gate_act * (1.0 - sigmoid_gate))
    ).astype(jnp.bfloat16)
    back_up = (back_hidden * silu_gate).astype(jnp.bfloat16)
    sum_gate = jnp.dot(normed_mid.T, back_gate, preferred_element_type=jnp.float32)
    sum_up = jnp.dot(normed_mid.T, back_up, preferred_element_type=jnp.float32)
    back_mid = jnp.dot(back_gate, full_gate.T, preferred_element_type=jnp.float32) + jnp.dot(
        back_up, full_up.T, preferred_element_type=jnp.float32
    )
    sum_gain_ffn = jnp.sum(back_mid * resid * scale_mid, axis=0)
    back_norm = back_mid * gain_mid
    back_resid = upstream + scale_mid * (
        back_norm
        - resid * scale_mid * scale_mid * jnp.mean(back_norm * resid, axis=1, keepdims=True)
    )
    part_gate, part_up, part_down, part_gain_ffn = (
        lax.psum_scatter(sum_gate, "fsdp", scatter_dimension=0, tiled=True),
        lax.psum_scatter(sum_up, "fsdp", scatter_dimension=0, tiled=True),
        lax.psum_scatter(sum_down, "fsdp", scatter_dimension=0, tiled=True),
        lax.psum_scatter(sum_gain_ffn, "fsdp", scatter_dimension=0, tiled=True),
    )
    part_gate, part_up, part_down, part_gain_ffn = (
        lax.psum(part_gate.astype(jnp.bfloat16), "rep").astype(jnp.float32),
        lax.psum(part_up.astype(jnp.bfloat16), "rep").astype(jnp.float32),
        lax.psum(part_down.astype(jnp.bfloat16), "rep").astype(jnp.float32),
        lax.psum(part_gain_ffn.astype(jnp.bfloat16), "rep").astype(jnp.float32),
    )
    full_qkv, full_out, full_gain_attn, full_gain_group = (
        lax.all_gather(w_qkv, "fsdp", axis=0, tiled=True),
        lax.all_gather(w_out, "fsdp", axis=0, tiled=True),
        lax.all_gather(gain_attn, "fsdp", axis=0, tiled=True),
        lax.all_gather(gain_group, "fsdp", axis=0, tiled=True),
    )
    gain_in = full_gain_attn.astype(jnp.float32)
    group_scale_factor = full_gain_group.astype(jnp.float32).reshape(H, E)
    back_attn = back_resid.astype(jnp.bfloat16)
    sum_out = jnp.dot(head_normalized.T, back_attn, preferred_element_type=jnp.float32)
    head_gradient = jnp.dot(back_attn, full_out.T, preferred_element_type=jnp.float32).reshape(
        sequence_length, H, E
    )
    group_gain_total = jnp.sum(head_gradient * normalized_input, axis=0).reshape(MODEL_WIDTH)
    centered_gradient = head_gradient * group_scale_factor
    back_out = (
        inverse_deviation
        * (
            centered_gradient
            - jnp.mean(centered_gradient, axis=2, keepdims=True)
            - normalized_input
            * jnp.mean(centered_gradient * normalized_input, axis=2, keepdims=True)
        )
    ).astype(jnp.bfloat16)
    zeroed, convolved = attend_maps(queries, key_rows, allowed, conv_kernel, scale)
    probs = jnp.exp(jnp.where(allowed, convolved, -jnp.inf) - log_total)
    mixed = mix_heads(probs, head_mix).astype(jnp.bfloat16)
    back_mixed = jnp.einsum(
        "ihe,jhe->hij", back_out, value_rows, preferred_element_type=jnp.float32
    )
    back_values = jnp.einsum("hij,ihe->jhe", mixed, back_out, preferred_element_type=jnp.float32)
    grouped_back = back_mixed.reshape(H // 2, 2, sequence_length, sequence_length)
    grouped_probs = probs.reshape(H // 2, 2, sequence_length, sequence_length)
    table = head_mix.reshape(H // 2, 2, 2)
    sum_mix = jnp.sum(grouped_back[:, :, None] * grouped_probs[:, None, :], axis=(3, 4)).reshape(
        H, 2
    )
    back_probs = (
        table[:, 0, :, None, None] * grouped_back[:, 0:1]
        + table[:, 1, :, None, None] * grouped_back[:, 1:2]
    ).reshape(H, sequence_length, sequence_length)
    back_conv = probs * (back_probs - jnp.sum(back_probs * probs, axis=2, keepdims=True))
    back_zeroed, sum_kernel = convolve_back(back_conv, zeroed, conv_kernel)
    back_scores = jnp.where(allowed, back_zeroed, 0.0).astype(jnp.bfloat16)
    back_queries = (
        jnp.einsum("hij,jhe->ihe", back_scores, key_rows, preferred_element_type=jnp.float32)
        * scale
    ).astype(jnp.bfloat16)
    back_keys = (
        jnp.einsum("hij,ihe->jhe", back_scores, queries, preferred_element_type=jnp.float32) * scale
    ).astype(jnp.bfloat16)
    back_proj = jnp.concatenate(
        [
            back_queries.reshape(sequence_length, MODEL_WIDTH),
            back_keys.reshape(sequence_length, MODEL_WIDTH),
            back_values.astype(jnp.bfloat16).reshape(sequence_length, MODEL_WIDTH),
        ],
        axis=1,
    )
    sum_qkv = jnp.dot(normed_in.T, back_proj, preferred_element_type=jnp.float32)
    back_in = jnp.dot(back_proj, full_qkv.T, preferred_element_type=jnp.float32)
    sum_gain_attn = jnp.sum(back_in * tokens * scale_in, axis=0)
    back_norm_in = back_in * gain_in
    grad_tokens = back_resid + scale_in * (
        back_norm_in
        - tokens * scale_in * scale_in * jnp.mean(back_norm_in * tokens, axis=1, keepdims=True)
    )
    kernel_total, mix_total = lax.psum((sum_kernel, sum_mix), ("rep", "fsdp"))
    part_qkv, part_out, part_gain_attn, part_gain_group = (
        lax.psum_scatter(sum_qkv, "fsdp", scatter_dimension=0, tiled=True),
        lax.psum_scatter(sum_out, "fsdp", scatter_dimension=0, tiled=True),
        lax.psum_scatter(sum_gain_attn, "fsdp", scatter_dimension=0, tiled=True),
        lax.psum_scatter(group_gain_total, "fsdp", scatter_dimension=0, tiled=True),
    )
    part_qkv, part_out, part_gain_attn, part_gain_group = (
        lax.psum(part_qkv.astype(jnp.bfloat16), "rep").astype(jnp.float32),
        lax.psum(part_out.astype(jnp.bfloat16), "rep").astype(jnp.float32),
        lax.psum(part_gain_attn.astype(jnp.bfloat16), "rep").astype(jnp.float32),
        lax.psum(part_gain_group.astype(jnp.bfloat16), "rep").astype(jnp.float32),
    )
    return (
        output.astype(jnp.bfloat16)[None],
        grad_tokens[None],
        part_qkv,
        part_out,
        part_gain_attn,
        part_gain_group,
        kernel_total,
        mix_total,
        part_gain_ffn,
        part_gate,
        part_up,
        part_down,
    )


def solution(mesh):
    placed = (
        P(("rep", "fsdp"), None, None),
        P(("rep", "fsdp"), None),
        P("fsdp", None),
        P("fsdp", None),
        P("fsdp"),
        P("fsdp"),
        P(),
        P(),
        P("fsdp"),
        P("fsdp", None),
        P("fsdp", None),
        P("fsdp", None),
        P(("rep", "fsdp"), None, None),
    )
    return jax.shard_map(
        per_device,
        mesh=mesh,
        in_specs=placed,
        out_specs=(
            P(("rep", "fsdp"), None, None),
            P(("rep", "fsdp"), None, None),
            P("fsdp", None),
            P("fsdp", None),
            P("fsdp"),
            P("fsdp"),
            P(),
            P(),
            P("fsdp"),
            P("fsdp", None),
            P("fsdp", None),
            P("fsdp", None),
        ),
        check_vma=False,
    )
```

profile of v0, /device:TPU:16, one launch (start us, length us, event | category | flops | bytes accessed | tf_op | source)
XLA Modules:
  0.0 1776.8 jit_solution(5305259581240575744)
XLA Ops:
  10.6 1.3 fusion.177
  12.6 0.9 dynamic-update-slice
  13.5 0.8 dynamic-update-slice.1
  14.3 0.8 dynamic-update-slice.2
  15.2 52.6 %all-reduce.10 = (bf16[1536]{0:T(1024)(128)(2,1)S(1)}, bf16[1536]{0:T(1024)(128)(2,1)S(1)}, bf16[1536]{0:T(1024)(128)(2,1)S(1)}) all-reduce(bf16[1536]{0:T(1024)(128)(2,1)S(1)} %dynamic-update-slice.1, bf16[1536]{0:T(1024)(128)(2,1)S(1)} %dynamic-update-slice, ...), channel_id=1, replica_groups=mesh['rep'=2,'fsdp'=16] {'fsdp'}, use_global_device_ids=true, to_apply=%add.3 | all-reduce | flops 4608 | bytes 18432
  70.8 50.4 %all-gather.6.cloned.1.call-done = bf16[1536,4608]{1,0:T(8,128)(2,1)} async-done(((bf16[96,4608]{1,0:T(8,128)(2,1)}), bf16[1536,4608]{1,0:T(8,128)(2,1)}) %all-gather.6.cloned.1.call-update) | async-done | bytes 14155792 | tf_op jit(solution)/shard_map/all_gather | solution.py:94
  121.2 9.2 convolution_convert_fusion
  131.6 2.9 multiply_select_fusion
  134.5 204.2 %fusion.173 = (f32[16,256]{1,0:T(8,128)S(1)}, f32[16,256,256]{2,1,0:T(8,128)}) fusion(f32[16]{0:T(128)S(1)} %get-tuple-element.229, f32[16]{0:T(128)S(1)} %get-tuple-element.230, f32[16]{0:T(128)S(1)} %get-tuple-element.166, f32[16]{0:T(128)S(1)} %get-tuple-element.167, f32[16]{0:T(128)S(1)} %get-tuple-element.168, f32[16]{0:T(128)S(1)} %get-tuple-element.169, ...), kind=kLoop, calls=%fused_computation.499 | loop fusion | flops 139456512 | bytes 8474752 | tf_op jit(solution)/shard_map/reduce_max | solution.py:116
  338.7 3.1 fusion.141
  342.3 1.6 fusion.140
  345.3 0.8 bitcast_reduce_fusion
  346.3 1.2 multiply_convert_fusion.7
  347.5 4.4 multiply_reduce_fusion.71
  351.9 1.3 multiply_convert_fusion.6
  353.1 10.7 fusion.179
  363.9 13.3 all-gather.10.cloned.1.call-done
  377.2 10.2 fusion.178
  387.4 90.6 %all-gather.14.cloned.1.call-done = bf16[4096,1536]{1,0:T(8,128)(2,1)} async-done(((bf16[256,1536]{1,0:T(8,128)(2,1)}), bf16[4096,1536]{1,0:T(8,128)(2,1)}) %all-gather.14.cloned.1.call-update) | async-done | bytes 12582928 | tf_op jit(solution)/shard_map/all_gather | solution.py:138
  478.0 10.6 multiply_convert_fusion
  488.6 8.0 fusion.180
  496.6 6.9 multiply_reduce_fusion.67
  504.1 1.1 copy-done.9
  505.2 5.0 fusion.163
  510.3 1.1 copy-done.24
  511.4 14.1 fusion.159
  525.5 1.2 copy-done.15
  526.7 12.1 fusion.183
  538.9 11.9 fusion.182
  552.2 3.8 fusion.165
  556.0 1.0 multiply_reduce_fusion.68
  557.7 0.8 fusion.181
  558.9 1.7 copy-done.4
  560.6 3.1 copy-done.3
  563.7 4.2 fusion.134
  567.9 20.9 %multiply_reduce_fusion.55 = (f32[16]{0:T(128)S(1)}, f32[16]{0:T(128)S(1)}, f32[16]{0:T(128)S(1)}, f32[16]{0:T(128)S(1)}, f32[16]{0:T(128)S(1)}, /*index=5*/f32[...) fusion(f32[16,256,256]{2,1,0:T(8,128)S(1)} %copy-done, ...), kind=kOutput, calls=%fused_computation.331 | output fusion | flops 30412864 | bytes 20972416 | tf_op jit(solution)/shard_map/sub | solution.py:229
  588.8 4.1 slice_bitcast_fusion.1
  593.9 68.6 %select_convert_fusion = bf16[16,256,256]{2,1,0:T(8,128)(2,1)S(1)} fusion(f32[16,256,256]{2,1,0:T(8,128)S(1)} %get-tuple-element.243, f32[16]{0:T(128)S(1)} %get-tuple-element.229, f32[16]{0:T(128)S(1)} %get-tuple-element.230, f32[16]{0:T(128)S(1)} %get-tuple-element.166, f32[16]{0:T(128)S(1)} %get-tuple-element.167, f32[16]{0:T(128)S(1)} %get-tuple-element.168, ...), kind=kLoop, calls=%fused_computation.343 | loop fusion | flops 139460608 | bytes 6361216 | tf_op jit(solution)/shard_map/convert_element_type | solution.py:231
  663.0 0.8 multiply_convert_fusion.4
  665.1 13.3 fusion.157
  679.8 10.2 fusion.155
  690.0 44.1 %multiply_reduce_fusion.37 = (f32[16]{0:T(128)S(1)}, f32[16]{0:T(128)S(1)}, f32[16]{0:T(128)S(1)}, f32[16]{0:T(128)S(1)}, f32[16]{0:T(128)S(1)}, /*index=5*/f32[...) fusion(f32[16,256,256]{2,1,0:T(8,128)} %copy-done.1, ...), kind=kLoop, calls=%fused_computation.313 | loop fusion | flops 37748448 | bytes 8389760 | tf_op jit(solution)/shard_map/reduce_sum | solution.py:52
  734.0 43.6 %multiply_reduce_fusion.19 = (f32[16]{0:T(128)S(1)}, f32[16]{0:T(128)S(1)}, f32[16]{0:T(128)S(1)}, f32[16]{0:T(128)S(1)}, f32[16]{0:T(128)S(1)}, /*index=5*/f32[...) fusion(f32[16,256,256]{2,1,0:T(8,128)} %copy-done.1, ...), kind=kLoop, calls=%fused_computation.295 | loop fusion | flops 37748448 | bytes 8389760 | tf_op jit(solution)/shard_map/reduce_sum | solution.py:52
  777.6 43.8 %multiply_reduce_fusion.1 = (f32[16]{0:T(128)S(1)}, f32[16]{0:T(128)S(1)}, f32[16]{0:T(128)S(1)}, f32[16]{0:T(128)S(1)}, f32[16]{0:T(128)S(1)}, /*index=5*/f32[1...) fusion(f32[16,256,256]{2,1,0:T(8,128)} %copy-done.1, ...), kind=kLoop, calls=%fused_computation.277 | loop fusion | flops 37748448 | bytes 8389760 | tf_op jit(solution)/shard_map/reduce_sum | solution.py:52
  821.4 1.8 convert_element_type.161
  823.2 44.0 %reduce-scatter.14.cloned.1.call-done = f32[256,1536]{1,0:T(8,128)} async-done(((f32[4096,1536]{1,0:T(8,128)}), f32[256,1536]{1,0:T(8,128)}) %reduce-scatter.14.cloned.1.call-update) | async-done | bytes 1572880 | tf_op jit(solution)/shard_map/reduce_scatter | solution.py:179
  867.2 2.4 convert_element_type.173
  869.6 244.4 %reduce-scatter.12.cloned.1.call-done = f32[96,4096]{1,0:T(8,128)} async-done(((f32[1536,4096]{1,0:T(8,128)}), f32[96,4096]{1,0:T(8,128)}) %reduce-scatter.12.cloned.1.call-update) | async-done | bytes 1572880 | tf_op jit(solution)/shard_map/reduce_scatter | solution.py:178
  1114.0 2.4 convert_element_type.171
  1116.3 244.4 %reduce-scatter.10.cloned.1.call-done = f32[96,4096]{1,0:T(8,128)} async-done(((f32[1536,4096]{1,0:T(8,128)}), f32[96,4096]{1,0:T(8,128)}) %reduce-scatter.10.cloned.1.call-update) | async-done | bytes 1572880 | tf_op jit(solution)/shard_map/reduce_scatter | solution.py:177
  1360.7 2.4 convert_element_type.169
  1363.1 272.5 %reduce-scatter.6.cloned.1.call-done = f32[96,4608]{1,0:T(8,128)} async-done(((f32[1536,4608]{1,0:T(8,128)}), f32[96,4608]{1,0:T(8,128)}) %reduce-scatter.6.cloned.1.call-update) | async-done | bytes 1769488 | tf_op jit(solution)/shard_map/reduce_scatter | solution.py:257
  1635.6 2.5 convert_element_type.159
  1638.2 4.3 multiply_reduce_fusion
  1642.6 44.7 %all-reduce.9 = (bf16[1536]{0:T(1024)(128)(2,1)S(1)}, bf16[1536]{0:T(1024)(128)(2,1)S(1)}, bf16[1536]{0:T(1024)(128)(2,1)S(1)}) all-reduce(f32[1536]{0:T(1024)S(1)} %get-tuple-element.130, f32[1536]{0:T(1024)S(1)} %reshape.166, f32[1536]{0:T(1024)S(1)} %get-tuple-element.128), channel_id=4, replica_groups=mesh['rep'=2,'fsdp'=16] {'fsdp'}, use_global_device_ids=true, to_apply=%region_16.17.clone | all-reduce | flops 4608 | bytes 27648
  1687.5 4.9 all-reduce.11
  1694.3 54.9 %all-reduce.8 = (f32[16,6,11]{0,2,1:T(8,128)S(1)}, f32[16,2]{0,1:T(2,128)}) all-reduce(f32[16,6,11]{0,2,1:T(8,128)S(1)} %constant_dynamic-update-slice_fusion, f32[16,2]{0,1:T(2,128)S(1)} %copy.58), channel_id=1, replica_groups=mesh['rep'=2,'fsdp'=16] {'rep','fsdp'}, use_global_device_ids=true, to_apply=%region_87.88 | all-reduce | flops 1088 | bytes 8704 | tf_op jit(solution)/shard_map/psum | solution.py:255
  1749.8 3.2 fusion.151
  1753.1 7.4 fusion.143
  1760.5 1.9 convert_element_type.162
  1762.5 2.5 convert_element_type.160
  1765.0 2.4 convert_element_type.170
  1767.4 1.3 convert_element_type.172
  1768.7 1.3 convert_element_type.174
  (214 shorter events, 18.6 us)
Async XLA Ops:
  7.2 62.6 %copy-start.13 = (bf16[1,256,1536]{2,1,0:T(8,128)(2,1)S(1)}, bf16[1,256,1536]{2,1,0:T(8,128)(2,1)}, u32[]{:S(2)}) copy-start(bf16[1,256,1536]{2,1,0:T(8,128)(2,1)} %param.13) | copy-start | bytes 2359300
  7.2 62.9 %copy-start.33 = (f32[16,6,11]{0,1,2:T(8,128)S(1)}, f32[16,6,11]{0,1,2:T(8,128)}, u32[]{:S(2)}) copy-start(f32[16,6,11]{0,1,2:T(8,128)} %param.19) | copy-start | bytes 12676
  7.2 63.5 %copy-start.60 = (s32[1,256]{1,0:T(1,128)S(1)}, s32[1,256]{1,0:T(1,128)}, u32[]{:S(2)}) copy-start(s32[1,256]{1,0:T(1,128)} %param.14) | copy-start | bytes 3076
  7.2 114.0 %all-gather.6.cloned.1.call-start = ((), (), s32[]{:S(2)}) async-start(), calls=%async_computation.5 | async-start | bytes 15040512 | tf_op jit(solution)/shard_map/all_gather | solution.py:94
  7.9 339.5 %all-gather.8.cloned.1.call-start = ((), (), s32[]{:S(2)}) async-start(), calls=%async_computation.6 | async-start | bytes 5013504 | tf_op jit(solution)/shard_map/all_gather | solution.py:95
  8.7 344.4 %all-gather.12.cloned.1.call-start = ((), (), s32[]{:S(2)}) async-start(), calls=%async_computation.8 | async-start | bytes 13369344 | tf_op jit(solution)/shard_map/all_gather | solution.py:137
  9.4 367.7 %all-gather.10.cloned.1.call-start = ((), (), s32[]{:S(2)}) async-start(), calls=%async_computation.7 | async-start | bytes 13369344 | tf_op jit(solution)/shard_map/all_gather | solution.py:136
  10.0 468.0 %all-gather.14.cloned.1.call-start = ((), (), s32[]{:S(2)}) async-start(), calls=%async_computation.9 | async-start | bytes 13369344 | tf_op jit(solution)/shard_map/all_gather | solution.py:138
  10.6 810.8 %reduce-scatter.8.cloned.1.call-start = ((), (), s32[]{:S(2)}) async-start(), calls=%async_computation.11 | async-start | bytes 10027008 | tf_op jit(solution)/shard_map/reduce_scatter | solution.py:258
  70.6 63.8 %copy-start.34 = (f32[16]{0:T(128)}, f32[16]{0:T(128)S(1)}, u32[]{:S(2)}) copy-start(f32[16]{0:T(128)S(1)} %get-tuple-element.211) | copy-start | bytes 196
  70.6 63.8 %copy-start.36 = (f32[16]{0:T(128)}, f32[16]{0:T(128)S(1)}, u32[]{:S(2)}) copy-start(f32[16]{0:T(128)S(1)} %get-tuple-element.212) | copy-start | bytes 196
  70.6 63.8 %copy-start.38 = (f32[16]{0:T(128)}, f32[16]{0:T(128)S(1)}, u32[]{:S(2)}) copy-start(f32[16]{0:T(128)S(1)} %get-tuple-element.213) | copy-start | bytes 196
  70.6 63.8 %copy-start.40 = (f32[16]{0:T(128)}, f32[16]{0:T(128)S(1)}, u32[]{:S(2)}) copy-start(f32[16]{0:T(128)S(1)} %get-tuple-element.214) | copy-start | bytes 196
  70.7 63.8 %copy-start.42 = (f32[16]{0:T(128)}, f32[16]{0:T(128)S(1)}, u32[]{:S(2)}) copy-start(f32[16]{0:T(128)S(1)} %get-tuple-element.215) | copy-start | bytes 196
  70.7 63.8 %copy-start.44 = (f32[16]{0:T(128)}, f32[16]{0:T(128)S(1)}, u32[]{:S(2)}) copy-start(f32[16]{0:T(128)S(1)} %get-tuple-element.216) | copy-start | bytes 196
  70.7 63.8 %copy-start.46 = (f32[16]{0:T(128)}, f32[16]{0:T(128)S(1)}, u32[]{:S(2)}) copy-start(f32[16]{0:T(128)S(1)} %get-tuple-element.217) | copy-start | bytes 196
  70.7 63.8 %copy-start.48 = (f32[16]{0:T(128)}, f32[16]{0:T(128)S(1)}, u32[]{:S(2)}) copy-start(f32[16]{0:T(128)S(1)} %get-tuple-element.218) | copy-start | bytes 196
  70.7 63.8 %copy-start.50 = (f32[16]{0:T(128)}, f32[16]{0:T(128)S(1)}, u32[]{:S(2)}) copy-start(f32[16]{0:T(128)S(1)} %get-tuple-element.219) | copy-start | bytes 196
  131.0 3.5 copy-start.16
  131.0 3.5 copy-start.52
  131.0 3.5 copy-start.54
  131.3 207.4 %copy-start.18 = (bf16[256,1536]{0,1:T(8,128)(2,1)}, bf16[256,1536]{0,1:T(8,128)(2,1)S(1)}, u32[]{:S(2)}) copy-start(bf16[256,1536]{0,1:T(8,128)(2,1)S(1)} %copy.50) | copy-start | bytes 2359300
  131.6 213.7 %copy-start.20 = (bf16[256,1536]{0,1:T(8,128)(2,1)}, bf16[256,1536]{0,1:T(8,128)(2,1)S(1)}, u32[]{:S(2)}) copy-start(bf16[256,1536]{0,1:T(8,128)(2,1)S(1)} %copy.49) | copy-start | bytes 2359300
  338.7 3.6 copy-start.2
  351.9 151.7 %copy-start.7 = (f32[256,1536]{1,0:T(8,128)}, f32[256,1536]{1,0:T(8,128)S(1)}, u32[]{:S(2)}) copy-start(f32[256,1536]{1,0:T(8,128)S(1)} %get-tuple-element.240) | copy-start | bytes 4718596
  488.6 8.0 copy-start.29
  488.6 8.0 copy-start.30
  496.6 7.0 copy-start.23
  503.5 1.7 copy-start.12
  504.1 1.1 copy-start.9
  510.2 1.1 copy-start.24
  510.2 357.0 %reduce-scatter.14.cloned.1.call-start = ((), (), s32[]{:S(2)}) async-start(), calls=%async_computation.14 | async-start | bytes 26738688 | tf_op jit(solution)/shard_map/reduce_scatter | solution.py:179
  525.5 1.2 copy-start.15
  525.5 588.5 %reduce-scatter.12.cloned.1.call-start = ((), (), s32[]{:S(2)}) async-start(), calls=%async_computation.13 | async-start | bytes 26738688 | tf_op jit(solution)/shard_map/reduce_scatter | solution.py:178
  538.9 821.9 %reduce-scatter.10.cloned.1.call-start = ((), (), s32[]{:S(2)}) async-start(), calls=%async_computation.12 | async-start | bytes 26738688 | tf_op jit(solution)/shard_map/reduce_scatter | solution.py:177
  550.8 1.4 copy-start.10
  550.8 1084.8 %reduce-scatter.6.cloned.1.call-start = ((), (), s32[]{:S(2)}) async-start(), calls=%async_computation.10 | async-start | bytes 30081024 | tf_op jit(solution)/shard_map/reduce_scatter | solution.py:257
  556.0 1.7 copy-start.21
  558.4 2.1 copy-start.4
  558.5 5.2 copy-start.3
  560.6 7.3 copy-start.5
  560.6 7.3 copy-start.6
  563.7 4.2 copy-start
  588.8 4.9 copy-start.1
  588.8 4.2 copy-start.57
  588.8 4.2 copy-start.59
  592.9 0.9 copy-start.35
  593.7 68.7 %copy-start.19 = (bf16[256,1536]{0,1:T(8,128)(2,1)S(1)}, bf16[256,1536]{0,1:T(8,128)(2,1)}, u32[]{:S(2)}) copy-start(bf16[256,1536]{0,1:T(8,128)(2,1)} %copy-done.18) | copy-start | bytes 2359300
  593.9 69.1 %copy-start.17 = (bf16[256,1536]{0,1:T(8,128)(2,1)S(1)}, bf16[256,1536]{0,1:T(8,128)(2,1)}, u32[]{:S(2)}) copy-start(bf16[256,1536]{0,1:T(8,128)(2,1)} %copy-done.16) | copy-start | bytes 2359300
  663.0 2.2 copy-start.14
  663.7 0.9 copy-start.25
  664.2 0.9 copy-start.27
  678.4 1.1 copy-start.26
  678.4 1.4 copy-start.28
  678.4 1082.1 %all-reduce.15.cloned.1.call-start = ((), (), s32[]{:S(2)}) async-start(), calls=%async_computation.15 | async-start | bytes 7077888 | tf_op jit(solution)/shard_map/psum | solution.py:263
  1638.1 55.9 %copy-start.61 = (f32[16]{0:T(128)S(1)}, f32[16]{0:T(128)}, u32[]{:S(2)}) copy-start(f32[16]{0:T(128)} %get-tuple-element.122) | copy-start | bytes 196
  1638.1 55.9 %copy-start.62 = (f32[16]{0:T(128)S(1)}, f32[16]{0:T(128)}, u32[]{:S(2)}) copy-start(f32[16]{0:T(128)} %get-tuple-element.123) | copy-start | bytes 196
  1638.1 55.8 %copy-start.63 = (f32[16]{0:T(128)S(1)}, f32[16]{0:T(128)}, u32[]{:S(2)}) copy-start(f32[16]{0:T(128)} %get-tuple-element.124) | copy-start | bytes 196
  1638.2 55.8 %copy-start.64 = (f32[16]{0:T(128)S(1)}, f32[16]{0:T(128)}, u32[]{:S(2)}) copy-start(f32[16]{0:T(128)} %get-tuple-element.125) | copy-start | bytes 196
  1638.2 111.7 %copy-start.11 = (f32[256,1536]{1,0:T(8,128)S(1)}, f32[256,1536]{1,0:T(8,128)}, u32[]{:S(2)}) copy-start(f32[256,1536]{1,0:T(8,128)} %copy-done.9) | copy-start | bytes 4718596
  1642.5 110.6 %copy-start.8 = (f32[256,1536]{1,0:T(8,128)S(1)}, f32[256,1536]{1,0:T(8,128)}, u32[]{:S(2)}) copy-start(f32[256,1536]{1,0:T(8,128)} %copy-done.7) | copy-start | bytes 4718596
  1749.2 3.9 copy-start.22
  1760.5 6.9 copy-start.32
  1760.5 8.2 copy-start.31
  (12 other events, 9.8 us)
Sparse Core Ops, SparseCore 0:
  10.3 110.8 all-gather.5
  123.5 51.7 all-gather.7
  177.7 98.6 all-gather.11
  278.5 98.6 all-gather.9
  379.3 98.6 all-gather.13
  510.4 110.0 reduce-scatter.7
  624.5 242.6 reduce-scatter.13
  871.3 242.6 reduce-scatter.11
  1118.1 242.6 reduce-scatter.9
  1364.8 270.8 reduce-scatter.5
  1638.8 95.1 all-reduce.14
where the time goes:
time: 1790 us; the launch traced here: 1780 us
  waiting for transfers between devices  963 us (54%)
  other arithmetic  470 us (26%)
  blocking collectives  157 us (9%)
  matrix products  144 us (8%)
  local copies, waits for them, and re-layouts  25.1 us (1%)
    reduce_scatter x1, waiting for transfers between devices, per_device(): lax.psum_scatter(sum_qkv, 'fsdp', scatter_dimension=0, tiled=True)  273 us
    reduce_scatter x1, waiting for transfers between devices, per_device(): lax.psum_scatter(sum_gate, 'fsdp', scatter_dimension=0, tiled=True)  244 us
    reduce_scatter x1, waiting for transfers between devices, per_device(): lax.psum_scatter(sum_up, 'fsdp', scatter_dimension=0, tiled=True)  244 us
    reduce_max x1, other arithmetic, per_device(): top_score = jnp.max(masked, axis=2, keepdims=True)  204 us
    reduce_sum x3, other arithmetic, convolve_back(): row_terms.append(jnp.sum(upstream * behind, axis=(1, 2)))  131 us
    unnamed x2, blocking collectives  97.3 us
    all_gather x1, waiting for transfers between devices, per_device(): lax.all_gather(w_down, 'fsdp', axis=0, tiled=True)  90.6 us
    convert_element_type x1, other arithmetic, per_device(): back_scores = jnp.where(allowed, back_zeroed, 0.0).astype(jnp.bfloat16)  68.6 us
  transfers between devices with their start and end apart: 11, of which 7 were waited for; matrix products, arithmetic and copies ran while one was open for 33% of the time, Pallas kernels for 0%

commit v1 on v0

v1 whole, which is shorter than its diff:
```python
import math

import jax
import jax.numpy as jnp
from jax import lax
from jax.experimental import pallas as pl
from jax.experimental.pallas import tpu as pltpu
from jax.sharding import PartitionSpec as P

MODEL_WIDTH = 1536
H = 16
E = 96
EP = 128
QWIN = 6
KWIN = 11
bf16, f32 = jnp.bfloat16, jnp.float32


def allowed_mask(doc_col, doc_row):
    n = doc_row.shape[-1]
    i = lax.broadcasted_iota(jnp.int32, (n, n), 0)
    j = lax.broadcasted_iota(jnp.int32, (n, n), 1)
    return (j <= i) & (doc_col == doc_row)


def down(v, a):
    if a == 0:
        return v
    i = lax.broadcasted_iota(jnp.int32, v.shape, 0)
    return jnp.where(i >= a, pltpu.roll(v, a, 0), 0.0)


def up(v, a):
    if a == 0:
        return v
    n = v.shape[0]
    i = lax.broadcasted_iota(jnp.int32, v.shape, 0)
    return jnp.where(i < n - a, pltpu.roll(v, n - a, 0), 0.0)


def dot(a, b, ca=1, cb=0):
    return lax.dot_general(a, b, (((ca,), (cb,)), ((), ())), preferred_element_type=f32)


def split(v):
    hi = v.astype(bf16)
    return hi, (v - hi.astype(f32)).astype(bf16)


def fwd_kernel(mix_ref, qkv_ref, dcol_ref, drow_ref, th_ref, tl_ref, gain_ref,
               normed_ref, xhat_ref, s_ref, p_ref, z_ref):
    allowed = allowed_mask(dcol_ref[0], drow_ref[0])
    scale = 1.0 / math.sqrt(E)
    probs = []
    for h in range(2):
        q = qkv_ref[0, :, h * EP:(h + 1) * EP]
        k = qkv_ref[0, :, (2 + h) * EP:(3 + h) * EP]
        zeroed = jnp.where(allowed, dot(q, k, 1, 1) * scale, 0.0)
        z_ref[0, h] = zeroed.astype(bf16)
        his, los = [], []
        for a in range(QWIN):
            hi, lo = split(down(zeroed, a))
            his.append(hi)
            los.append(lo)
        his, los = jnp.concatenate(his, 1), jnp.concatenate(los, 1)
        th, tl = th_ref[h], tl_ref[h]
        conv = dot(his, th) + (dot(his, tl) + dot(los, th))
        masked = jnp.where(allowed, conv, -jnp.inf)
        e = jnp.exp(masked - jnp.max(masked, axis=1, keepdims=True))
        p = e / jnp.sum(e, axis=1, keepdims=True)
        p_ref[0, h] = p
        probs.append(p)
    lane = lax.broadcasted_iota(jnp.int32, (1, EP), 1)
    for h in range(2):
        v = qkv_ref[0, :, (4 + h) * EP:(5 + h) * EP]
        mixed = (mix_ref[h, 0] * probs[0] + mix_ref[h, 1] * probs[1]).astype(bf16)
        ho = dot(mixed, v)
        centered = jnp.where(lane < E, ho - jnp.sum(ho, axis=1, keepdims=True) / E, 0.0)
        s = lax.rsqrt(jnp.sum(centered * centered, axis=1, keepdims=True) / E + 1e-05)
        xhat = centered * s
        cols = slice(h * EP, (h + 1) * EP)
        xhat_ref[0, :, cols] = xhat
        s_ref[0, :, cols] = jnp.broadcast_to(s, xhat.shape)
        normed_ref[0, :, cols] = (xhat * gain_ref[0:1, cols]).astype(bf16)


def attend(mix, qkv, dcol, drow, th, tl, gain):
    n, t, _ = qkv.shape
    row = lambda *s: pl.BlockSpec((1,) + s, lambda i: (i,) + (0,) * len(s))
    full = lambda a: pl.BlockSpec(a.shape, lambda i: (0,) * a.ndim)
    return pl.pallas_call(
        fwd_kernel,
        grid=(n,),
        in_specs=[pl.BlockSpec(memory_space=pltpu.SMEM), row(t, 6 * EP), row(t, 1), row(1, t), full(th), full(tl), full(gain)],
        out_specs=[row(t, 2 * EP), row(t, 2 * EP), row(t, 2 * EP), row(2, t, t), row(2, t, t)],
        out_shape=[
            jax.ShapeDtypeStruct((n, t, 2 * EP), bf16),
            jax.ShapeDtypeStruct((n, t, 2 * EP), f32),
            jax.ShapeDtypeStruct((n, t, 2 * EP), f32),
            jax.ShapeDtypeStruct((n, 2, t, t), f32),
            jax.ShapeDtypeStruct((n, 2, t, t), bf16),
        ],
        cost_estimate=pl.CostEstimate(flops=n * 2 * 3 * 2 * t * t * QWIN * t, bytes_accessed=n * t * t * 20, transcendentals=n * 2 * t * t),
        name="attend",
    )(mix, qkv, dcol, drow, th, tl, gain)


def bwd_kernel(mix_ref, qkv_ref, dcol_ref, drow_ref, tt_ref, gain_ref, dn_ref, xhat_ref, s_ref, p_ref, z_ref,
               dqkv_ref, gconv_ref, gmix_ref, gg_ref, m_ref):
    step, steps = pl.program_id(0), pl.num_programs(0)
    t = p_ref.shape[-1]

    @pl.when(step == 0)
    def _():
        m_ref[...] = jnp.zeros_like(m_ref)
        gmix_ref[...] = jnp.zeros_like(gmix_ref)
        gg_ref[...] = jnp.zeros_like(gg_ref)

    allowed = allowed_mask(dcol_ref[0], drow_ref[0])
    scale = 1.0 / math.sqrt(E)
    lane = lax.broadcasted_iota(jnp.int32, (1, EP), 1)
    p = [p_ref[0, 0], p_ref[0, 1]]
    dmixed = []
    for h in range(2):
        cols = slice(h * EP, (h + 1) * EP)
        dn, xhat = dn_ref[0, :, cols], xhat_ref[0, :, cols]
        gg_ref[0:1, cols] += jnp.sum(dn * xhat, axis=0, keepdims=True)
        dc = dn * gain_ref[0:1, cols]
        m1 = jnp.sum(dc, axis=1, keepdims=True) / E
        m2 = jnp.sum(dc * xhat, axis=1, keepdims=True) / E
        dh = jnp.where(lane < E, s_ref[0, :, cols] * (dc - m1 - xhat * m2), 0.0).astype(bf16)
        v = qkv_ref[0, :, (4 + h) * EP:(5 + h) * EP]
        mixed = (mix_ref[h, 0] * p[0] + mix_ref[h, 1] * p[1]).astype(bf16)
        dmixed.append(dot(dh, v, 1, 1))
        dqkv_ref[0, :, (4 + h) * EP:(5 + h) * EP] = dot(mixed, dh, 0, 0).astype(bf16)
    for h in range(2):
        for c in range(2):
            r = 2 * h + c
            gmix_ref[r:r + 1, :] += jnp.sum(dmixed[h] * p[c], axis=0, keepdims=True)
    for c in range(2):
        dp = mix_ref[0, c] * dmixed[0] + mix_ref[1, c] * dmixed[1]
        dconv = p[c] * (dp - jnp.sum(dp * p[c], axis=1, keepdims=True))
        ahead = jnp.concatenate([up(dconv, a).astype(bf16) for a in range(QWIN)], 1)
        m_ref[c] += dot(z_ref[0, c], ahead, 0, 0)
        ds = jnp.where(allowed, dot(ahead, tt_ref[c]), 0.0).astype(bf16)
        q = qkv_ref[0, :, c * EP:(c + 1) * EP]
        k = qkv_ref[0, :, (2 + c) * EP:(3 + c) * EP]
        dqkv_ref[0, :, c * EP:(c + 1) * EP] = (dot(ds, k) * scale).astype(bf16)
        dqkv_ref[0, :, (2 + c) * EP:(3 + c) * EP] = (dot(ds, q, 0, 0) * scale).astype(bf16)

    @pl.when(step == steps - 1)
    def _():
        lanes = lax.broadcasted_iota(jnp.int32, (8, t), 1)
        for h in range(2):
            for a in range(QWIN):
                total = jnp.zeros((8, t), f32)
                for first in range(0, t, 8):
                    rows = m_ref[h, first:first + 8, a * t:(a + 1) * t]
                    turned = pltpu.roll(rows, t - first, 1) if first else rows
                    total = total + jnp.where(lanes < t - first, turned, 0.0)
                gconv_ref[h, a] = total[:, :EP]


def attend_back(mix, qkv, dcol, drow, tt, gain, dn, xhat, s, p, z):
    n, t, _ = qkv.shape
    row = lambda *sh: pl.BlockSpec((1,) + sh, lambda i: (i,) + (0,) * len(sh))
    full = lambda a: pl.BlockSpec(a.shape, lambda i: (0,) * a.ndim)
    keep = lambda *sh: pl.BlockSpec(sh, lambda i: (0,) * len(sh))
    return pl.pallas_call(
        bwd_kernel,
        grid=(n,),
        in_specs=[pl.BlockSpec(memory_space=pltpu.SMEM), row(t, 6 * EP), row(t, 1), row(1, t), full(tt), full(gain),
                  row(t, 2 * EP), row(t, 2 * EP), row(t, 2 * EP), row(2, t, t), row(2, t, t)],
        out_specs=[row(t, 6 * EP), keep(2, QWIN, 8, EP), keep(8, t), keep(8, 2 * EP)],
        out_shape=[
            jax.ShapeDtypeStruct((n, t, 6 * EP), bf16),
            jax.ShapeDtypeStruct((2, QWIN, 8, EP), f32),
            jax.ShapeDtypeStruct((8, t), f32),
            jax.ShapeDtypeStruct((8, 2 * EP), f32),
        ],
        scratch_shapes=[pltpu.VMEM((2, t, QWIN * t), f32)],
        cost_estimate=pl.CostEstimate(flops=n * 2 * 2 * 2 * t * t * QWIN * t, bytes_accessed=n * t * t * 20, transcendentals=0),
        name="attend_back",
    )(mix, qkv, dcol, drow, tt, gain, dn, xhat, s, p, z)


def bands(kernel, t):
    diff = jnp.arange(t)[None, :] - jnp.arange(t)[:, None]
    band = jnp.zeros((2, QWIN, t, t), f32)
    back = jnp.zeros((2, QWIN, t, t), f32)
    for b in range(KWIN):
        tap = kernel[:, :, b][:, :, None, None]
        band = band + jnp.where(diff == b, tap, 0.0)
        back = back + jnp.where(diff == -b, tap, 0.0)
    th, tl = split(band)
    flat = lambda v: v.reshape(2, QWIN * t, t)
    return flat(th), flat(tl), flat(back.astype(bf16))


def diagonals(tiles):
    return sum(tiles[:, :, i, i:i + KWIN] for i in range(8))


FF = 4096


def rms_scale(values):
    return lax.rsqrt(jnp.mean(values * values, axis=1, keepdims=True) + 1e-06)


class Links:
    def __init__(self, fsdp):
        self.fsdp = fsdp
        index = lax.axis_index("fsdp")
        self.x = lax.axis_index("rep")
        self.z, self.y, self.c = index // 4, (index // 2) % 2, index % 2

    def across(self, flip, v):
        if flip == "x":
            return lax.ppermute(v, "rep", [(0, 1), (1, 0)])
        bit = {"y": 2, "c": 1}[flip]
        return lax.ppermute(v, "fsdp", [(f, f ^ bit) for f in range(self.fsdp)])

    def along(self, v, step):
        pairs = [(f, f + 4 * step) for f in range(self.fsdp) if 0 <= f + 4 * step < self.fsdp]
        return lax.ppermute(v, "fsdp", pairs)

    def ordered(self, bit, mine, other, axis):
        first, second = jnp.where(bit == 0, mine, other), jnp.where(bit == 0, other, mine)
        return jnp.stack([first, second], axis)

    def gather_z(self, v):
        left, right = [], []
        a = b = v
        for _ in range(3):
            a, b = self.along(a, 1), self.along(b, -1)
            left.append(a)
            right.append(b)
        line = jnp.stack(left[::-1] + [v] + right)
        return lax.dynamic_slice_in_dim(line, 3 - self.z, 4, 0)

    def scatter_z(self, parts):
        zero = jnp.zeros((3,) + parts.shape[1:], parts.dtype)
        line = lax.dynamic_slice_in_dim(jnp.concatenate([zero, parts, zero]), self.z, 7, 0)
        low = lambda v: v.astype(bf16)
        a = self.along(low(line[6]), 1)
        b = self.along(low(line[0]), -1)
        for step in (1, 2):
            a = self.along(low(line[6 - step] + a.astype(f32)), 1)
            b = self.along(low(line[step] + b.astype(f32)), -1)
        return line[3] + a.astype(f32) + b.astype(f32)

    def gather_plane(self, v):
        n = v.shape[0] // 2
        vx, vy = self.across("x", v), self.across("y", v)
        vd = jnp.concatenate([self.across("y", vx[:n]), self.across("x", vy[n:])])
        return [jnp.concatenate([u, self.across("c", u)]) for u in (v, vx, vy, vd)]

    def scatter_plane(self, parts):
        low = lambda v: v.astype(bf16)
        n = parts[0].shape[0] // 2
        s = [p[:n] + self.across("c", low(p[n:])).astype(f32) for p in parts]
        m = n // 2
        dx, dy = self.across("x", low(s[3][:m])), self.across("y", low(s[3][m:]))
        to_x = jnp.concatenate([s[1][:m], s[1][m:] + dy.astype(f32)])
        to_y = jnp.concatenate([s[2][:m] + dx.astype(f32), s[2][m:]])
        return s[0] + self.across("x", low(to_x)).astype(f32) + self.across("y", low(to_y)).astype(f32)


class Weights:
    def __init__(self, links):
        self.links = links
        self.line = links.fsdp == 16
        x, y, c = links.x, links.y, links.c
        self.pair = 4 * x + 2 * c + y
        self.slot = 4 * x + 2 * y + c

    def spread(self, shard, dims):
        l = self.links
        ax, ay, ac = dims
        v = lax.dynamic_index_in_dim(shard, l.x, ax, keepdims=True)
        keep = lax.dynamic_index_in_dim(v, l.y, ay, keepdims=True)
        sent = l.across("y", lax.dynamic_index_in_dim(v, 1 - l.y, ay, keepdims=True))
        v = l.ordered(l.y, keep, sent, 0)
        keep = lax.dynamic_index_in_dim(v, l.c, ac + 1, keepdims=True)
        sent = l.across("c", lax.dynamic_index_in_dim(v, 1 - l.c, ac + 1, keepdims=True))
        v = l.ordered(l.c, keep, sent, 1)
        return l.gather_z(v)

    def collect(self, grad, dims):
        l = self.links
        ax, ay, ac = dims
        low = lambda v: v.astype(bf16)
        v = l.scatter_z(grad)
        keep = lax.dynamic_index_in_dim(v, l.c, 1, keepdims=False)
        sent = l.across("c", low(lax.dynamic_index_in_dim(v, 1 - l.c, 1, keepdims=False)))
        v = self.join(l.c, keep, sent.astype(f32), ac + 1)
        keep = lax.dynamic_index_in_dim(v, l.y, 0, keepdims=False)
        sent = l.across("y", low(lax.dynamic_index_in_dim(v, 1 - l.y, 0, keepdims=False)))
        v = low(self.join(l.y, keep, sent.astype(f32), ay))
        return self.join(l.x, v, l.across("x", v), ax).astype(f32)

    def join(self, bit, mine, other, axis):
        first, second = jnp.where(bit == 0, mine, other), jnp.where(bit == 0, other, mine)
        return jnp.concatenate([first, second], axis)

    def whole(self, shard):
        return lax.all_gather(shard, "fsdp", axis=0, tiled=True)

    def owned(self, grad):
        part = lax.psum_scatter(grad, "fsdp", scatter_dimension=0, tiled=True)
        return lax.psum(part.astype(bf16), "rep").astype(f32)

    def qkv(self, shard):
        rows = shard.shape[0]
        if self.line:
            v = self.spread(shard.reshape(rows, 3, 2, 2, 2, 2 * E), (2, 4, 3))
            v = v.reshape(MODEL_WIDTH, 3, 2, E)
        else:
            v = self.whole(shard).reshape(MODEL_WIDTH, 3, 8, 2, E)
            v = lax.dynamic_index_in_dim(v, self.pair, 2, keepdims=False)
        return jnp.pad(v, ((0, 0), (0, 0), (0, 0), (0, EP - E))).reshape(MODEL_WIDTH, 6 * EP)

    def qkv_back(self, grad):
        g = grad.reshape(MODEL_WIDTH, 3, 2, EP)[..., :E]
        if self.line:
            return self.collect(g.reshape(4, 2, 2, -1, 3, 1, 1, 1, 2 * E), (2, 4, 3)).reshape(-1, 3 * MODEL_WIDTH)
        zero = jnp.zeros((MODEL_WIDTH, 3, 8, 2, E), f32)
        return self.owned(lax.dynamic_update_index_in_dim(zero, g, self.pair, 2).reshape(MODEL_WIDTH, 3 * MODEL_WIDTH))

    def out(self, shard):
        l = self.links
        if self.line:
            v = l.gather_z(shard)
            keep = lax.dynamic_index_in_dim(v, 2 * l.x + l.c, 0, keepdims=False)
            sent = l.across("c", lax.dynamic_index_in_dim(v, 2 * l.x + 1 - l.c, 0, keepdims=False))
            v = l.ordered(l.c, keep, sent, 0)
        else:
            v = self.whole(shard).reshape(8, 2, E, MODEL_WIDTH)
            v = lax.dynamic_index_in_dim(v, self.pair, 0, keepdims=False)
        return jnp.pad(v, ((0, 0), (0, EP - E), (0, 0))).reshape(2 * EP, MODEL_WIDTH)

    def out_back(self, grad):
        l = self.links
        g = grad.reshape(2, EP, MODEL_WIDTH)[:, :E]
        if self.line:
            keep = lax.dynamic_index_in_dim(g, l.c, 0, keepdims=False)
            sent = l.across("c", lax.dynamic_index_in_dim(g, 1 - l.c, 0, keepdims=False).astype(bf16)).astype(f32)
            at = jnp.arange(4)[:, None, None]
            parts = jnp.where(at == 2 * l.x + l.c, keep[None], jnp.where(at == 2 * l.x + 1 - l.c, sent[None], 0.0))
            v = l.scatter_z(parts).astype(bf16)
            return (v + l.across("x", v)).astype(f32)
        zero = jnp.zeros((8, 2, E, MODEL_WIDTH), f32)
        return self.owned(lax.dynamic_update_index_in_dim(zero, g, self.pair, 0).reshape(MODEL_WIDTH, MODEL_WIDTH))

    def ffn_in(self, gate, up_):
        rows = gate.shape[0]
        both = jnp.stack([gate, up_], 1)
        if self.line:
            v = self.spread(both.reshape(rows, 2, 4, 2, 2, 2, FF // 32), (5, 3, 4))
            return v.reshape(MODEL_WIDTH, FF // 4)
        v = self.whole(both).reshape(MODEL_WIDTH, 2, 8, FF // 8)
        return lax.dynamic_index_in_dim(v, self.slot, 2, keepdims=False).reshape(MODEL_WIDTH, FF // 4)

    def ffn_in_back(self, grad):
        if self.line:
            v = self.collect(grad.reshape(4, 2, 2, -1, 2, 4, 1, 1, 1, FF // 32), (5, 3, 4)).reshape(-1, 2, FF)
        else:
            zero = jnp.zeros((MODEL_WIDTH, 2, 8, FF // 8), f32)
            g = grad.reshape(MODEL_WIDTH, 2, FF // 8)
            v = self.owned(lax.dynamic_update_index_in_dim(zero, g, self.slot, 2).reshape(MODEL_WIDTH, 2, FF))
        return v[:, 0], v[:, 1]

    def ffn_out(self, shard):
        l = self.links
        if self.line:
            v = lax.dynamic_index_in_dim(shard.reshape(2, FF // 32, MODEL_WIDTH), l.x, 0, keepdims=False)
            return l.gather_z(v).reshape(FF // 8, MODEL_WIDTH)
        v = self.whole(shard).reshape(8, FF // 8, MODEL_WIDTH)
        return lax.dynamic_index_in_dim(v, self.slot, 0, keepdims=False)

    def ffn_out_back(self, grad):
        l = self.links
        if self.line:
            v = l.scatter_z(grad.reshape(4, FF // 32, MODEL_WIDTH)).astype(bf16)
            return self.join(l.x, v, l.across("x", v), 0).astype(f32)
        zero = jnp.zeros((8, FF // 8, MODEL_WIDTH), f32)
        return self.owned(lax.dynamic_update_index_in_dim(zero, grad, self.slot, 0).reshape(FF, MODEL_WIDTH))

    def gains(self, *shards):
        l = self.links
        v = jnp.stack(shards)
        if self.line:
            v = l.ordered(l.c, v, l.across("c", v), 0)
            v = l.ordered(l.y, v, l.across("y", v), 0)
            v = l.gather_z(v)
            v = v.reshape(16, len(shards), -1).transpose(1, 0, 2).reshape(len(shards), MODEL_WIDTH)
        else:
            v = lax.all_gather(v, "fsdp", axis=1, tiled=True)
        return [v[i].astype(f32) for i in range(len(shards))]


def per_device(
    fsdp,
    x_in,
    doc_ids,
    w_qkv,
    w_out,
    gain_attn,
    gain_group,
    conv_kernel,
    head_mix,
    gain_ffn,
    w_gate,
    w_up,
    w_down,
    cotangent,
):
    links = Links(fsdp)
    weights = Weights(links)
    tokens = x_in.shape[1]

    x_all = jnp.concatenate(links.gather_plane(x_in[0]))
    qkv_w = weights.qkv(w_qkv)
    gain_a, gain_g, gain_f = weights.gains(gain_attn, gain_group, gain_ffn)
    docs = doc_ids
    for flip in ("y", "x"):
        docs = jnp.concatenate([docs, links.across(flip, docs)])
    docs = jnp.stack([docs, links.across("c", docs)], 1)
    docs = docs[jnp.array([0, 2, 1, 3])].reshape(8, tokens)
    out_w = weights.out(w_out)
    in_w = weights.ffn_in(w_gate, w_up)
    down_w = weights.ffn_out(w_down)
    upstream_chips = links.gather_plane(cotangent[0])

    kernel = lax.dynamic_slice_in_dim(conv_kernel, 2 * weights.pair, 2, 0)
    mix = lax.dynamic_slice_in_dim(head_mix, 2 * weights.pair, 2, 0)
    th, tl, tt = bands(kernel, tokens)
    group = lax.dynamic_slice_in_dim(gain_g.reshape(8, 2, E), weights.pair, 1, 0)
    group = jnp.pad(group, ((0, 0), (0, 0), (0, EP - E))).reshape(1, 2 * EP)
    doc_col, doc_row = docs[:, :, None], docs[:, None, :]

    xf_all = x_all.astype(f32)
    a1 = (xf_all * rms_scale(xf_all) * gain_a).astype(bf16)
    qkv = dot(a1, qkv_w).astype(bf16).reshape(8, tokens, 6 * EP)
    normed, xhat, s, probs, zeroed = attend(mix, qkv, doc_col, doc_row, th, tl, group)
    normed = normed.reshape(4, 2 * tokens, 2 * EP)
    xf = x_in[0].astype(f32)
    resid = xf + links.scatter_plane([dot(normed[i], out_w) for i in range(4)])

    r2 = rms_scale(resid)
    a2_chips = links.gather_plane((resid * r2 * gain_f).astype(bf16))
    out_parts, back_parts, hiddens, dgus = [], [], [], []
    half = FF // 8
    for a2, dffn in zip(a2_chips, upstream_chips):
        gu = dot(a2, in_w)
        gate, up_act = gu[:, :half], gu[:, half:]
        sig = jax.nn.sigmoid(gate)
        silu = gate * sig
        hidden = (silu * up_act).astype(bf16)
        dhidden = dot(dffn, down_w, 1, 1)
        dgate = (dhidden * up_act * sig * (1.0 + gate * (1.0 - sig))).astype(bf16)
        dup = (dhidden * silu).astype(bf16)
        dgu = jnp.concatenate([dgate, dup], 1)
        hiddens.append(hidden)
        dgus.append(dgu)
        back_parts.append(dot(dgu, in_w, 1, 1))
        out_parts.append(dot(hidden, down_w))
    da2 = links.scatter_plane(back_parts)
    output = (resid + links.scatter_plane(out_parts)).astype(bf16)

    dy = cotangent[0].astype(f32)
    sum_gain_ffn = jnp.sum(da2 * resid * r2, axis=0)
    dn2 = da2 * gain_f
    dresid = dy + r2 * (dn2 - resid * r2 * r2 * jnp.mean(dn2 * resid, axis=1, keepdims=True))
    dattn = jnp.concatenate(links.gather_plane(dresid.astype(bf16)))

    a2_all, dgu_all = jnp.concatenate(a2_chips), jnp.concatenate(dgus)
    hidden_all, dffn_all = jnp.concatenate(hiddens), jnp.concatenate(upstream_chips)
    grad_gate, grad_up = weights.ffn_in_back(dot(a2_all, dgu_all, 0, 0))
    grad_down = weights.ffn_out_back(dot(hidden_all, dffn_all, 0, 0))

    dnormed = dot(dattn, out_w, 1, 1).reshape(8, tokens, 2 * EP)
    dqkv, conv_tiles, mix_sums, group_sums = attend_back(
        mix, qkv, doc_col, doc_row, tt, group, dnormed, xhat, s, probs, zeroed
    )
    dqkv = dqkv.reshape(4, 2 * tokens, 6 * EP)
    da1 = links.scatter_plane([dot(dqkv[i], qkv_w, 1, 1) for i in range(4)])
    grad_out = weights.out_back(dot(normed.reshape(8 * tokens, 2 * EP), dattn, 0, 0))
    grad_qkv = weights.qkv_back(dot(a1, dqkv.reshape(8 * tokens, 6 * EP), 0, 0))

    r1 = rms_scale(xf)
    sum_gain_attn = jnp.sum(da1 * xf * r1, axis=0)
    dn1 = da1 * gain_a
    grad_x = dresid + r1 * (dn1 - xf * r1 * r1 * jnp.mean(dn1 * xf, axis=1, keepdims=True))

    place = lambda v: lax.dynamic_update_index_in_dim(jnp.zeros((8,) + v.shape, f32), v, weights.pair, 0)
    small = [
        sum_gain_attn,
        sum_gain_ffn,
        place(group_sums[0].reshape(2, EP)[:, :E].reshape(-1)),
        place(diagonals(conv_tiles)),
        place(jnp.sum(mix_sums[:4], axis=1)),
    ]
    sizes = [v.size for v in small]
    total = lax.psum(jnp.concatenate([v.reshape(-1) for v in small]), ("rep", "fsdp"))
    cut = [0]
    for size in sizes:
        cut.append(cut[-1] + size)
    gain_a_sum, gain_f_sum, group_sum, conv_sum, mix_sum = (total[cut[i] : cut[i + 1]] for i in range(5))
    rows = gain_attn.shape[0]
    own = lambda v: lax.dynamic_slice_in_dim(v, lax.axis_index("fsdp") * rows, rows, 0)
    return (
        output[None],
        grad_x[None],
        grad_qkv,
        grad_out,
        own(gain_a_sum),
        own(group_sum),
        conv_sum.reshape(H, QWIN, KWIN),
        mix_sum.reshape(H, 2),
        own(gain_f_sum),
        grad_gate,
        grad_up,
        grad_down,
    )


def solution(mesh):
    fsdp = mesh.shape["fsdp"]
    assert mesh.shape["rep"] == 2 and fsdp % 4 == 0
    rows, shard, part = P(("rep", "fsdp"), None, None), P("fsdp", None), P("fsdp")
    placed = (rows, P(("rep", "fsdp"), None), shard, shard, part, part, P(), P(), part, shard, shard, shard, rows)
    return jax.shard_map(
        lambda *args: per_device(fsdp, *args),
        mesh=mesh,
        in_specs=placed,
        out_specs=(rows, rows, shard, shard, part, part, P(), P(), part, shard, shard, shard),
        check_vma=False,
    )
```

time: 1790 us -> 994 us (0.56)
  waiting for transfers between devices: 963 us -> 262 us
  other arithmetic: 470 us -> 119 us
  starting transfers between devices: 0.84 us -> 204 us
  local copies, waits for them, and re-layouts: 25.1 us -> 197 us
  blocking collectives: 157 us -> 54.3 us
  matrix products: 144 us -> 95.8 us
  Pallas kernels: 0 us -> 42 us
    reduce_scatter x5 -> x0, waiting for transfers between devices: 805 us -> none  [the longest x1 273 us: per_device(): lax.psum_scatter(sum_qkv, 'fsdp', scatter_dimension=0, tiled=True)]
    ppermute x0 -> x137, waiting for transfers between devices: none -> 262 us  [the longest x54 153 us: along(): return lax.ppermute(v, 'fsdp', pairs)]
    ppermute x0 -> x137, starting transfers between devices: none -> 204 us  [the longest x54 152 us: along(): return lax.ppermute(v, 'fsdp', pairs)]
    reduce_max x1 -> x0, other arithmetic: 204 us -> none  [per_device(): top_score = jnp.max(masked, axis=2, keepdims=True)]
    all_gather x5 -> x0, waiting for transfers between devices: 154 us -> none  [the longest x1 90.6 us: per_device(): lax.all_gather(w_down, 'fsdp', axis=0, tiled=True)]
    reduce_sum x8 -> x5, other arithmetic: 140 us -> 11.1 us  [the longest x2 4.95 us: rms_scale(): return lax.rsqrt(jnp.mean(values * values, axis=1, keepdims=True) + 1e-06)]
    unnamed x2 -> x0, blocking collectives: 97.3 us -> none
    convert_element_type x21 -> x24, other arithmetic: 95.5 us -> 25.6 us  [the longest x1 6.88 us: split(): return (hi, (v - hi.astype(f32)).astype(bf16))]
  transfers between devices with their start and end apart: 11 -> 137, of which waited for: 7 -> 50; matrix products, arithmetic and copies ran while one was open for 33% -> 40% of each run, Pallas kernels for 0% -> 4%
where the time goes in v1:
time: 994 us; the launch traced here: 979 us
  waiting for transfers between devices  262 us (26%)
  starting transfers between devices  204 us (21%)
  local copies, waits for them, and re-layouts  197 us (20%)
  other arithmetic  119 us (12%)
  matrix products  95.8 us (10%)
  blocking collectives  54.3 us (5%)
  Pallas kernels  42 us (4%)
    ppermute x54, waiting for transfers between devices, along(): return lax.ppermute(v, 'fsdp', pairs)  153 us
    ppermute x54, starting transfers between devices, along(): return lax.ppermute(v, 'fsdp', pairs)  152 us
    dot_general x30, matrix products, dot(): lax.dot_general(a, b, (((ca,), (cb,)), ((), ())), preferred_element_type=...  95.8 us
    ppermute x62, waiting for transfers between devices, across(): return lax.ppermute(v, 'fsdp', [(f, f ^ bit) for f in range(self.fsdp)])  58.7 us
    psum x1, blocking collectives, per_device(): lax.psum(jnp.concatenate([v.reshape(-1) for v in small]), ('rep', 'fsdp'))  54.3 us
    unnamed x348, local copies, waits for them, and re-layouts  52.7 us
    ppermute x21, waiting for transfers between devices, across(): return lax.ppermute(v, 'rep', [(0, 1), (1, 0)])  50.8 us
    ppermute x62, starting transfers between devices, across(): return lax.ppermute(v, 'fsdp', [(f, f ^ bit) for f in range(self.fsdp)])  28.9 us
  transfers between devices with their start and end apart: 137, of which 50 were waited for; matrix products, arithmetic and copies ran while one was open for 40% of the time, Pallas kernels for 4%

profile of v1, /device:TPU:16, one launch (start us, length us, event | category | flops | bytes accessed | tf_op | source)
XLA Modules:
  0.0 979.2 jit_solution(1841412829863502340)
XLA Ops:
  0.7 3.6 collective-permute-start.27
  23.1 3.7 reshape.520
  46.9 6.9 subtract_convert_fusion
  55.1 6.2 fusion.49.tt_ref
  65.8 4.2 collective-permute-start.10
  73.4 3.9 collective-permute-start.11
  81.6 3.6 collective-permute-start.12
  118.2 6.1 collective-permute-done.28
  160.6 7.7 collective-permute-done.53
  172.3 10.6 %collective-permute-done.56 = bf16[128,1536]{1,0:T(8,128)(2,1)S(1)} collective-permute-done((bf16[128,1536]{1,0:T(8,128)(2,1)S(1)}, bf16[128,1536]{1,0:T(8,128)(2,1)S(1)}, u32[]{:S(2)}, u32[]{:S(2)}) %collective-permute-start.56) | collective-permute-done | bytes 393248 | tf_op jit(solution)/shard_map/ppermute | solution.py:226
  185.0 3.9 collective-permute-start.21
  193.0 8.2 collective-permute-done.18
  203.5 4.4 collective-permute-start.19
  209.8 20.4 %collective-permute-done.19 = bf16[2,2,96,3,1,1,1,192]{7,2,3,1,0,6,5,4:T(8,128)(2,1)S(1)} collective-permute-done((bf16[2,2,96,3,1,1,1,192]{7,2,3,1,0,6,5,4:T(8,128)(2,1)S(1)}, bf16[2,2,96,3,1,1,1,192]{7,2,3,1,0,6,5,4:T(8,128)(2,1)S(1)}, u32[]{:S(2)}, u32[]{:S(2)}) %collective-permute-start.19) | collective-permute-done | bytes 442400 | tf_op jit(solution)/shard_map/ppermute | solution.py:226
  238.6 8.3 collective-permute-done.22
  256.0 9.0 collective-permute-done.23
  266.8 6.4 copy.449
  273.3 7.8 reshape.521
  283.8 4.2 fusion
  288.4 6.6 convolution_convert_fusion
  295.0 20.7 %attend.1 = (bf16[8,256,256]{2,1,0:T(8,128)(2,1)}, f32[8,256,256]{2,1,0:T(8,128)}, f32[8,256,256]{2,1,0:T(8,128)}, f32[8,2,256,256]{3,2,1,0:T(8,128)}, bf16[8,2,256,256]{3,2,1,0:T(8,128)(2,1)}) custom-call(f32[2,2]{1,0:T(2,128)} %copy.504.mix_ref, bf16[8,256,768]{2,1,0:T(8,128)(2,1)} %bitcast.608, s32[8,256,1]{2,1,0:T(8,128)} %broadcast_in_dim_reshape.8.dcol_ref, ...), custom_call_target="tpu_custom_call" | custom-call | flops 9663676416 | bytes 10485760 | tf_op jit(solution)/shard_map/attend/pallas_call | solution.py:91
  334.2 4.1 collective-permute-start.50
  341.5 9.0 collective-permute-done.37
  351.9 8.6 collective-permute-done.40
  367.6 10.4 %collective-permute-done.38 = bf16[256,1536]{1,0:T(8,128)(2,1)S(1)} collective-permute-done((bf16[256,1536]{1,0:T(8,128)(2,1)S(1)}, bf16[256,1536]{1,0:T(8,128)(2,1)S(1)}, u32[]{:S(2)}, u32[]{:S(2)}) %collective-permute-start.38) | collective-permute-done | bytes 786464 | tf_op jit(solution)/shard_map/ppermute | solution.py:220
  388.7 6.1 reshape.526
  395.4 6.2 collective-permute-done.58
  406.1 4.2 fusion.98
  455.9 21.2 %fusion.13 = f32[1536,1024]{1,0:T(8,128)} fusion(bf16[2048,1536]{1,0:T(8,128)(2,1)S(1)} %constant_dynamic-update-slice_fusion.25, bf16[512,512]{1,0:T(8,128)(2,1)S(1)} %get-tuple-element.171, bf16[512,512]{1,0:T(8,128)(2,1)S(1)} %get-tuple-element.170, bf16[512,512]{1,0:T(8,128)(2,1)S(1)} %get-tuple-element.173, ...), kind=kOutput, calls=%fused_computation.30 | convolution fusion | flops 6476005376 | bytes 16777216 | tf_op jit(solution)/shard_map/dot_general | solution.py:42
  477.1 8.2 reshape.535
  485.3 3.9 copy.490
  490.9 4.9 fusion.265
  513.2 8.7 collective-permute-done.121
  528.3 3.9 collective-permute-start.125
  534.6 7.6 collective-permute-done.66
  551.8 4.1 collective-permute-start.126
  572.0 5.3 fusion.51
  577.5 6.6 fusion.263
  601.7 3.9 collective-permute-start.134
  615.0 3.9 collective-permute-start.135
  631.5 7.4 collective-permute-done.93
  646.2 4.6 collective-permute-done.136
  652.2 13.9 %collective-permute-done.129 = bf16[96,2,4,2,2,1,128]{6,0,5,4,3,2,1:T(8,128)(2,1)S(1)} collective-permute-done((bf16[96,2,4,2,2,1,128]{6,0,5,4,3,2,1:T(8,128)(2,1)S(1)}, bf16[96,2,4,2,2,1,128]{6,0,5,4,3,2,1:T(8,128)(2,1)S(1)}, u32[]{:S(2)}, u32[]{:S(2)}) %collective-permute-start.129) | collective-permute-done | bytes 786464 | tf_op jit(solution)/shard_map/ppermute | solution.py:220
  666.4 4.1 copy.496
  670.5 5.9 reshape.542
  676.4 3.9 slice_bitcast_fusion
  682.4 6.0 fusion.289.dn_ref
  688.3 21.3 %attend_back.1 = (bf16[8,256,768]{2,1,0:T(8,128)(2,1)}, f32[2,6,8,128]{3,2,1,0:T(8,128)}, f32[8,256]{1,0:T(8,128)}, f32[8,256]{1,0:T(8,128)}) custom-call(f32[2,2]{1,0:T(2,128)} %copy.504.mix_ref, bf16[8,256,768]{2,1,0:T(8,128)(2,1)} %bitcast.609, s32[8,256,1]{2,1,0:T(8,128)} %broadcast_in_dim_reshape.8.dcol_ref, ...), custom_call_target="tpu_custom_call" | custom-call | flops 6442450944 | bytes 10485760 | tf_op jit(solution)/shard_map/attend_back/pallas_call | solution.py:169
  727.8 4.9 copy.480
  732.7 9.5 fusion.7
  742.2 8.7 reshape.529
  750.9 7.7 copy.481
  759.0 6.0 fusion.269
  777.6 3.9 collective-permute-start.107
  787.6 6.4 collective-permute-done.104
  799.4 3.6 collective-permute-done.117
  808.3 3.9 collective-permute-start.118
  812.6 14.8 %collective-permute-done.115 = bf16[96,1536]{1,0:T(8,128)(2,1)S(1)} collective-permute-done((bf16[96,1536]{1,0:T(8,128)(2,1)S(1)}, bf16[96,1536]{1,0:T(8,128)(2,1)S(1)}, u32[]{:S(2)}, u32[]{:S(2)}) %collective-permute-start.115) | collective-permute-done | bytes 294944 | tf_op jit(solution)/shard_map/ppermute | solution.py:226
  837.0 8.5 collective-permute-done.108
  858.8 7.6 collective-permute-done.106
  873.6 22.6 %collective-permute-done.111 = bf16[96,3,1,2,1,192]{5,0,4,3,2,1:T(8,128)(2,1)S(1)} collective-permute-done((bf16[96,3,1,2,1,192]{5,0,4,3,2,1:T(8,128)(2,1)S(1)}, bf16[96,3,1,2,1,192]{5,0,4,3,2,1:T(8,128)(2,1)S(1)}, u32[]{:S(2)}, u32[]{:S(2)}) %collective-permute-start.111) | collective-permute-done | bytes 221216 | tf_op jit(solution)/shard_map/ppermute | solution.py:222
  906.9 54.3 %psum.7 = f32[5696]{0:T(1024)S(1)} all-reduce(f32[5696]{0:T(1024)S(1)} %concatenate.199), channel_id=1, replica_groups=mesh['rep'=2,'fsdp'=16] {'rep','fsdp'}, use_global_device_ids=true, to_apply=%region_8.9 | all-reduce | flops 5696 | bytes 45568 | tf_op jit(solution)/shard_map/psum | solution.py:506
  964.7 5.8 fusion.67
  975.0 3.7 reshape.540
  (877 shorter events, 447.9 us)
Async XLA Ops:
  0.7 105.5 %collective-permute-start.27 = (bf16[96,1536]{1,0:T(8,128)(2,1)}, bf16[96,1536]{1,0:T(8,128)(2,1)}, u32[]{:S(2)}, u32[]{:S(2)}) collective-permute-start(bf16[96,1536]{1,0:T(8,128)(2,1)} %param.17), channel_id=1, source_target_pairs={{0,4},{1,5},{2,6},{3,7},{4,8},{5,9},{6,10},{7,11},{8,12},{9,13},{1... | collective-permute-start | bytes 884744 | tf_op jit(solution)/shard_map/ppermute | solution.py:226
  4.3 106.9 %collective-permute-start.30 = (bf16[96,1536]{1,0:T(8,128)(2,1)}, bf16[96,1536]{1,0:T(8,128)(2,1)}, u32[]{:S(2)}, u32[]{:S(2)}) collective-permute-start(bf16[96,1536]{1,0:T(8,128)(2,1)} %param.17), channel_id=1, source_target_pairs={{4,0},{5,1},{6,2},{7,3},{8,4},{9,5},{10,6},{11,7},{12,8},{13,9},{1... | collective-permute-start | bytes 884744 | tf_op jit(solution)/shard_map/ppermute | solution.py:226
  8.0 53.4 %collective-permute-start.8 = (bf16[3,96]{1,0:T(4,128)(2,1)}, bf16[3,96]{1,0:T(4,128)(2,1)}, u32[]{:S(2)}, u32[]{:S(2)}) collective-permute-start(bf16[3,96]{1,0:T(4,128)(2,1)} %pad_maximum_fusion.18), channel_id=1, source_target_pairs={{0,1},{1,0},{2,3},{3,2},{4,5},{5,4},{6,7},{7,6},{8,9},{9,8},{10,11... | collective-permute-start | bytes 1736 | tf_op jit(solution)/shard_map/ppermute | solution.py:222
  8.0 54.7 %collective-permute-start.24 = (s32[1,256]{1,0:T(1,128)}, s32[1,256]{1,0:T(1,128)}, u32[]{:S(2)}, u32[]{:S(2)}) collective-permute-start(s32[1,256]{1,0:T(1,128)} %param.15), channel_id=1, source_target_pairs={{0,2},{1,3},{2,0},{3,1},{4,6},{5,7},{6,4},{7,5},{8,10},{9,11},{10,... | collective-permute-start | bytes 3080 | tf_op jit(solution)/shard_map/ppermute | solution.py:222
  88.5 25.1 %collective-permute-start = (bf16[256,1536]{1,0:T(8,128)(2,1)S(1)}, bf16[256,1536]{1,0:T(8,128)(2,1)}, u32[]{:S(2)}, u32[]{:S(2)}) collective-permute-start(bf16[256,1536]{1,0:T(8,128)(2,1)S(1)} %bitcast.514), channel_id=1, source_target_pairs={{0,1},{1,0},{2,3},{3,2},{4,5},{5,4},{6,7},{7,6},{8,9},{9,8},{10,11... | collective-permute-start | bytes 2359304 | tf_op jit(solution)/shard_map/ppermute | solution.py:222
  108.8 20.4 %collective-permute-start.1 = (bf16[256,1536]{1,0:T(8,128)(2,1)S(1)}, bf16[256,1536]{1,0:T(8,128)(2,1)S(1)}, u32[]{:S(2)}, u32[]{:S(2)}) collective-permute-start(bf16[256,1536]{1,0:T(8,128)(2,1)S(1)} %bitcast.515), channel_id=1, source_target_pairs={{0,16},{16,0},{1,17},{17,1},{2,18},{18,2},{3,19},{19,3},{4,20},{20... | collective-permute-start | bytes 2359304 | tf_op jit(solution)/shard_map/ppermute | solution.py:220
  111.2 20.5 %collective-permute-start.3 = (bf16[256,1536]{1,0:T(8,128)(2,1)S(1)}, bf16[256,1536]{1,0:T(8,128)(2,1)S(1)}, u32[]{:S(2)}, u32[]{:S(2)}) collective-permute-start(bf16[256,1536]{1,0:T(8,128)(2,1)S(1)} %bitcast.516), channel_id=1, source_target_pairs={{0,2},{1,3},{2,0},{3,1},{4,6},{5,7},{6,4},{7,5},{8,10},{9,11},{10,... | collective-permute-start | bytes 2359304 | tf_op jit(solution)/shard_map/ppermute | solution.py:222
  112.9 32.3 %collective-permute-start.74 = (bf16[256,1536]{1,0:T(8,128)(2,1)}, bf16[256,1536]{1,0:T(8,128)(2,1)}, u32[]{:S(2)}, u32[]{:S(2)}) collective-permute-start(bf16[256,1536]{1,0:T(8,128)(2,1)} %bitcast.99), channel_id=1, source_target_pairs={{0,16},{16,0},{1,17},{17,1},{2,18},{18,2},{3,19},{19,3},{4,20},{20... | collective-permute-start | bytes 2359304 | tf_op jit(solution)/shard_map/ppermute | solution.py:220
  113.7 34.8 %collective-permute-start.78 = (bf16[256,1536]{1,0:T(8,128)(2,1)}, bf16[256,1536]{1,0:T(8,128)(2,1)S(1)}, u32[]{:S(2)}, u32[]{:S(2)}) collective-permute-start(bf16[256,1536]{1,0:T(8,128)(2,1)} %bitcast.99), channel_id=1, source_target_pairs={{0,2},{1,3},{2,0},{3,1},{4,6},{5,7},{6,4},{7,5},{8,10},{9,11},{10,... | collective-permute-start | bytes 2359304 | tf_op jit(solution)/shard_map/ppermute | solution.py:222
  131.7 19.2 %collective-permute-start.29 = (bf16[96,1536]{1,0:T(8,128)(2,1)S(1)}, bf16[96,1536]{1,0:T(8,128)(2,1)S(1)}, u32[]{:S(2)}, u32[]{:S(2)}) collective-permute-start(bf16[96,1536]{1,0:T(8,128)(2,1)S(1)} %collective-permute-done.28), channel_id=1, source_target_pairs={{0,4},{1,5},{2,6},{3,7},{4,8},{5,9},{6,10},{7,11},{8,12},{9,13},{1... | collective-permute-start | bytes 884744 | tf_op jit(solution)/shard_map/ppermute | solution.py:226
  141.9 26.6 %collective-permute-start.55 = (bf16[128,1536]{1,0:T(8,128)(2,1)S(1)}, bf16[128,1536]{1,0:T(8,128)(2,1)S(1)}, u32[]{:S(2)}, u32[]{:S(2)}) collective-permute-start(bf16[128,1536]{1,0:T(8,128)(2,1)S(1)} %collective-permute-done.54), channel_id=1, source_target_pairs={{4,0},{5,1},{6,2},{7,3},{8,4},{9,5},{10,6},{11,7},{12,8},{13,9},{1... | collective-permute-start | bytes 1179656 | tf_op jit(solution)/shard_map/ppermute | solution.py:226
  148.5 34.6 %collective-permute-start.5 = (bf16[128,1536]{1,0:T(8,128)(2,1)S(1)}, bf16[128,1536]{1,0:T(8,128)(2,1)S(1)}, u32[]{:S(2)}, u32[]{:S(2)}) collective-permute-start(bf16[128,1536]{1,0:T(8,128)(2,1)S(1)} %slice.631), channel_id=1, source_target_pairs={{0,2},{1,3},{2,0},{3,1},{4,6},{5,7},{6,4},{7,5},{8,10},{9,11},{10,... | collective-permute-start | bytes 1179656 | tf_op jit(solution)/shard_map/ppermute | solution.py:222
  150.9 34.1 %collective-permute-start.6 = (bf16[128,1536]{1,0:T(8,128)(2,1)S(1)}, bf16[128,1536]{1,0:T(8,128)(2,1)S(1)}, u32[]{:S(2)}, u32[]{:S(2)}) collective-permute-start(bf16[128,1536]{1,0:T(8,128)(2,1)S(1)} %slice.632), channel_id=1, source_target_pairs={{0,16},{16,0},{1,17},{17,1},{2,18},{18,2},{3,19},{19,3},{4,20},{20... | collective-permute-start | bytes 1179656 | tf_op jit(solution)/shard_map/ppermute | solution.py:220
  154.6 35.3 %collective-permute-start.77 = (bf16[128,1536]{1,0:T(8,128)(2,1)S(1)}, bf16[128,1536]{1,0:T(8,128)(2,1)S(1)}, u32[]{:S(2)}, u32[]{:S(2)}) collective-permute-start(bf16[128,1536]{1,0:T(8,128)(2,1)S(1)} %slice.680), channel_id=1, source_target_pairs={{0,2},{1,3},{2,0},{3,1},{4,6},{5,7},{6,4},{7,5},{8,10},{9,11},{10,... | collective-permute-start | bytes 1179656 | tf_op jit(solution)/shard_map/ppermute | solution.py:222
  168.5 23.3 %collective-permute-start.79 = (bf16[128,1536]{1,0:T(8,128)(2,1)S(1)}, bf16[128,1536]{1,0:T(8,128)(2,1)S(1)}, u32[]{:S(2)}, u32[]{:S(2)}) collective-permute-start(bf16[128,1536]{1,0:T(8,128)(2,1)S(1)} %slice.681), channel_id=1, source_target_pairs={{0,16},{16,0},{1,17},{17,1},{2,18},{18,2},{3,19},{19,3},{4,20},{20... | collective-permute-start | bytes 1179656 | tf_op jit(solution)/shard_map/ppermute | solution.py:220
  182.9 20.6 %collective-permute-start.2 = (bf16[256,1536]{1,0:T(8,128)(2,1)S(1)}, bf16[256,1536]{1,0:T(8,128)(2,1)S(1)}, u32[]{:S(2)}, u32[]{:S(2)}) collective-permute-start(bf16[256,1536]{1,0:T(8,128)(2,1)S(1)} %collective-permute-done.1), channel_id=1, source_target_pairs={{0,1},{1,0},{2,3},{3,2},{4,5},{5,4},{6,7},{7,6},{8,9},{9,8},{10,11... | collective-permute-start | bytes 2359304 | tf_op jit(solution)/shard_map/ppermute | solution.py:222
  185.0 24.8 %collective-permute-start.21 = (bf16[2,2,96,3,1,1,1,192]{7,2,6,5,4,3,1,0:T(8,128)(2,1)S(1)}, bf16[2,2,96,3,1,1,1,192]{7,2,6,5,4,3,1,0:T(8,128)(2,1)S(1)}, u32[]{:S(2)}, u32[]{:S(2)}) collective-permute-start(bf16[2,2,96,3,1,1,1,192]{7,2,6,5,4,3,1,0:T(8,128)(2,1)S(1)} %get-tuple-element.224), channel_id=1, source_target_pairs={{4,0},{5,1},{6,2},{7,3},{8,4},{9,5},{10,6},{11,7},{12,8},{13,9},{1... | collective-permute-start | bytes 1327112 | tf_op jit(solution)/shard_map/ppermute | solution.py:226
  189.9 57.1 %collective-permute-start.45 = (bf16[2,2,96,2,4,1,1,1,128]{8,2,4,3,0,1,7,6,5:T(8,128)(2,1)S(1)}, bf16[2,2,96,2,4,1,1,1,128]{8,2,4,3,0,1,7,6,5:T(8,128)(2,1)}, u32[]{:S(2)}, u32[]{:S(2)}) collective-permute-start(bf16[2,2,96,2,4,1,1,1,128]{8,2,4,3,0,1,7,6,5:T(8,128)(2,1)S(1)} %get-tuple-element.217), channel_id=1, source_target_pairs={{0,4},{1,5},{2,6},{3,7},{4,8},{5,9},{6,10},{7,11},{8,12},{9,13},{1... | collective-permute-start | bytes 2359304 | tf_op jit(solution)/shard_map/ppermute | solution.py:226
  191.8 40.7 %collective-permute-start.4 = (bf16[256,1536]{1,0:T(8,128)(2,1)S(1)}, bf16[256,1536]{1,0:T(8,128)(2,1)S(1)}, u32[]{:S(2)}, u32[]{:S(2)}) collective-permute-start(bf16[256,1536]{1,0:T(8,128)(2,1)S(1)} %collective-permute-done.3), channel_id=1, source_target_pairs={{0,1},{1,0},{2,3},{3,2},{4,5},{5,4},{6,7},{7,6},{8,9},{9,8},{10,11... | collective-permute-start | bytes 2359304 | tf_op jit(solution)/shard_map/ppermute | solution.py:222
  201.1 48.2 %collective-permute-start.48 = (bf16[2,2,96,2,4,1,1,1,128]{8,2,4,3,0,7,6,5,1:T(8,128)(2,1)S(1)}, bf16[2,2,96,2,4,1,1,1,128]{8,2,4,3,0,7,6,5,1:T(8,128)(2,1)}, u32[]{:S(2)}, u32[]{:S(2)}) collective-permute-start(bf16[2,2,96,2,4,1,1,1,128]{8,2,4,3,0,7,6,5,1:T(8,128)(2,1)S(1)} %get-tuple-element.216), channel_id=1, source_target_pairs={{4,0},{5,1},{6,2},{7,3},{8,4},{9,5},{10,6},{11,7},{12,8},{13,9},{1... | collective-permute-start | bytes 2359304 | tf_op jit(solution)/shard_map/ppermute | solution.py:226
  203.5 26.7 %collective-permute-start.19 = (bf16[2,2,96,3,1,1,1,192]{7,2,3,1,0,6,5,4:T(8,128)(2,1)S(1)}, bf16[2,2,96,3,1,1,1,192]{7,2,3,1,0,6,5,4:T(8,128)(2,1)S(1)}, u32[]{:S(2)}, u32[]{:S(2)}) collective-permute-start(bf16[2,2,96,3,1,1,1,192]{7,2,3,1,0,6,5,4:T(8,128)(2,1)S(1)} %collective-permute-done.18), channel_id=1, source_target_pairs={{0,4},{1,5},{2,6},{3,7},{4,8},{5,9},{6,10},{7,11},{8,12},{9,13},{1... | collective-permute-start | bytes 1327112 | tf_op jit(solution)/shard_map/ppermute | solution.py:226
  209.8 200.4 %collective-permute-start.72 = (bf16[256,1536]{1,0:T(8,128)(2,1)}, bf16[256,1536]{1,0:T(8,128)(2,1)}, u32[]{:S(2)}, u32[]{:S(2)}) collective-permute-start(bf16[256,1536]{1,0:T(8,128)(2,1)} %bitcast.99), channel_id=1, source_target_pairs={{0,1},{1,0},{2,3},{3,2},{4,5},{5,4},{6,7},{7,6},{8,9},{9,8},{10,11... | collective-permute-start | bytes 2359304 | tf_op jit(solution)/shard_map/ppermute | solution.py:222
  232.5 20.3 %collective-permute-start.20 = (bf16[2,2,96,3,1,1,1,192]{7,2,3,1,0,6,5,4:T(8,128)(2,1)S(1)}, bf16[2,2,96,3,1,1,1,192]{7,2,3,1,0,6,5,4:T(8,128)(2,1)S(1)}, u32[]{:S(2)}, u32[]{:S(2)}) collective-permute-start(bf16[2,2,96,3,1,1,1,192]{7,2,3,1,0,6,5,4:T(8,128)(2,1)S(1)} %collective-permute-done.19), channel_id=1, source_target_pairs={{0,4},{1,5},{2,6},{3,7},{4,8},{5,9},{6,10},{7,11},{8,12},{9,13},{1... | collective-permute-start | bytes 1327112 | tf_op jit(solution)/shard_map/ppermute | solution.py:226
  246.9 35.8 %collective-permute-start.7 = (bf16[256,1536]{1,0:T(8,128)(2,1)}, bf16[256,1536]{1,0:T(8,128)(2,1)S(1)}, u32[]{:S(2)}, u32[]{:S(2)}) collective-permute-start(bf16[256,1536]{1,0:T(8,128)(2,1)} %pad_maximum_fusion), channel_id=1, source_target_pairs={{0,1},{1,0},{2,3},{3,2},{4,5},{5,4},{6,7},{7,6},{8,9},{9,8},{10,11... | collective-permute-start | bytes 2359304 | tf_op jit(solution)/shard_map/ppermute | solution.py:222
  249.3 82.5 %collective-permute-start.46 = (bf16[2,2,96,2,4,1,1,1,128]{8,2,4,3,0,1,7,6,5:T(8,128)(2,1)}, bf16[2,2,96,2,4,1,1,1,128]{8,2,4,3,0,1,7,6,5:T(8,128)(2,1)}, u32[]{:S(2)}, u32[]{:S(2)}) collective-permute-start(bf16[2,2,96,2,4,1,1,1,128]{8,2,4,3,0,1,7,6,5:T(8,128)(2,1)} %collective-permute-done.45), channel_id=1, source_target_pairs={{0,4},{1,5},{2,6},{3,7},{4,8},{5,9},{6,10},{7,11},{8,12},{9,13},{1... | collective-permute-start | bytes 2359304 | tf_op jit(solution)/shard_map/ppermute | solution.py:226
  252.8 79.1 %collective-permute-start.49 = (bf16[2,2,96,2,4,1,1,1,128]{8,2,4,3,0,7,6,5,1:T(8,128)(2,1)}, bf16[2,2,96,2,4,1,1,1,128]{8,2,4,3,0,7,6,5,1:T(8,128)(2,1)}, u32[]{:S(2)}, u32[]{:S(2)}) collective-permute-start(bf16[2,2,96,2,4,1,1,1,128]{8,2,4,3,0,7,6,5,1:T(8,128)(2,1)} %collective-permute-done.48), channel_id=1, source_target_pairs={{4,0},{5,1},{6,2},{7,3},{8,4},{9,5},{10,6},{11,7},{12,8},{13,9},{1... | collective-permute-start | bytes 2359304 | tf_op jit(solution)/shard_map/ppermute | solution.py:226
  329.1 38.4 %collective-permute-start.34 = (bf16[256,1536]{1,0:T(8,128)(2,1)S(1)}, bf16[256,1536]{1,0:T(8,128)(2,1)S(1)}, u32[]{:S(2)}, u32[]{:S(2)}) collective-permute-start(bf16[256,1536]{1,0:T(8,128)(2,1)S(1)} %copy-done.61), channel_id=1, source_target_pairs={{0,1},{1,0},{2,3},{3,2},{4,5},{5,4},{6,7},{7,6},{8,9},{9,8},{10,11... | collective-permute-start | bytes 2359304 | tf_op jit(solution)/shard_map/ppermute | solution.py:222
  332.0 29.9 %collective-permute-start.47 = (bf16[2,2,96,2,4,1,1,1,128]{8,2,4,3,0,1,7,6,5:T(8,128)(2,1)}, bf16[2,2,96,2,4,1,1,1,128]{8,2,4,3,0,1,7,6,5:T(8,128)(2,1)S(1)}, u32[]{:S(2)}, u32[]{:S(2)}) collective-permute-start(bf16[2,2,96,2,4,1,1,1,128]{8,2,4,3,0,1,7,6,5:T(8,128)(2,1)} %collective-permute-done.46), channel_id=1, source_target_pairs={{0,4},{1,5},{2,6},{3,7},{4,8},{5,9},{6,10},{7,11},{8,12},{9,13},{1... | collective-permute-start | bytes 2359304 | tf_op jit(solution)/shard_map/ppermute | solution.py:226
  334.2 50.7 %collective-permute-start.50 = (bf16[2,2,96,2,4,1,1,1,128]{8,2,4,3,0,7,6,5,1:T(8,128)(2,1)}, bf16[2,2,96,2,4,1,1,1,128]{8,2,4,3,0,7,6,5,1:T(8,128)(2,1)S(1)}, u32[]{:S(2)}, u32[]{:S(2)}) collective-permute-start(bf16[2,2,96,2,4,1,1,1,128]{8,2,4,3,0,7,6,5,1:T(8,128)(2,1)} %collective-permute-done.49), channel_id=1, source_target_pairs={{4,0},{5,1},{6,2},{7,3},{8,4},{9,5},{10,6},{11,7},{12,8},{13,9},{1... | collective-permute-start | bytes 2359304 | tf_op jit(solution)/shard_map/ppermute | solution.py:226
  381.3 23.9 %collective-permute-start.42 = (bf16[256,1536]{1,0:T(8,128)(2,1)}, bf16[256,1536]{1,0:T(8,128)(2,1)}, u32[]{:S(2)}, u32[]{:S(2)}) collective-permute-start(bf16[256,1536]{1,0:T(8,128)(2,1)} %get-tuple-element.135), channel_id=1, source_target_pairs={{0,1},{1,0},{2,3},{3,2},{4,5},{5,4},{6,7},{7,6},{8,9},{9,8},{10,11... | collective-permute-start | bytes 2359304 | tf_op jit(solution)/shard_map/ppermute | solution.py:222
  381.3 20.3 %collective-permute-start.58 = (bf16[256,1536]{1,0:T(8,128)(2,1)}, bf16[256,1536]{1,0:T(8,128)(2,1)}, u32[]{:S(2)}, u32[]{:S(2)}) collective-permute-start(bf16[256,1536]{1,0:T(8,128)(2,1)} %get-tuple-element.135), channel_id=1, source_target_pairs={{0,16},{16,0},{1,17},{17,1},{2,18},{18,2},{3,19},{19,3},{4,20},{20... | collective-permute-start | bytes 2359304 | tf_op jit(solution)/shard_map/ppermute | solution.py:220
  382.1 20.5 %collective-permute-start.62 = (bf16[256,1536]{1,0:T(8,128)(2,1)}, bf16[256,1536]{1,0:T(8,128)(2,1)}, u32[]{:S(2)}, u32[]{:S(2)}) collective-permute-start(bf16[256,1536]{1,0:T(8,128)(2,1)} %get-tuple-element.135), channel_id=1, source_target_pairs={{0,2},{1,3},{2,0},{3,1},{4,6},{5,7},{6,4},{7,5},{8,10},{9,11},{10,... | collective-permute-start | bytes 2359304 | tf_op jit(solution)/shard_map/ppermute | solution.py:222
  384.9 40.6 %collective-permute-start.75 = (bf16[256,1536]{1,0:T(8,128)(2,1)}, bf16[256,1536]{1,0:T(8,128)(2,1)}, u32[]{:S(2)}, u32[]{:S(2)}) collective-permute-start(bf16[256,1536]{1,0:T(8,128)(2,1)} %collective-permute-done.74), channel_id=1, source_target_pairs={{0,1},{1,0},{2,3},{3,2},{4,5},{5,4},{6,7},{7,6},{8,9},{9,8},{10,11... | collective-permute-start | bytes 2359304 | tf_op jit(solution)/shard_map/ppermute | solution.py:222
  401.5 33.4 %collective-permute-start.84 = (bf16[256,1536]{1,0:T(8,128)(2,1)}, bf16[256,1536]{1,0:T(8,128)(2,1)S(1)}, u32[]{:S(2)}, u32[]{:S(2)}) collective-permute-start(bf16[256,1536]{1,0:T(8,128)(2,1)} %copy-done.32), channel_id=1, source_target_pairs={{0,1},{1,0},{2,3},{3,2},{4,5},{5,4},{6,7},{7,6},{8,9},{9,8},{10,11... | collective-permute-start | bytes 2359304 | tf_op jit(solution)/shard_map/ppermute | solution.py:222
  421.7 27.2 %collective-permute-start.80 = (bf16[256,1536]{1,0:T(8,128)(2,1)S(1)}, bf16[256,1536]{1,0:T(8,128)(2,1)S(1)}, u32[]{:S(2)}, u32[]{:S(2)}) collective-permute-start(bf16[256,1536]{1,0:T(8,128)(2,1)S(1)} %copy-done.55), channel_id=1, source_target_pairs={{0,1},{1,0},{2,3},{3,2},{4,5},{5,4},{6,7},{7,6},{8,9},{9,8},{10,11... | collective-permute-start | bytes 2359304 | tf_op jit(solution)/shard_map/ppermute | solution.py:222
  421.8 130.0 %collective-permute-start.73 = (bf16[256,1536]{1,0:T(8,128)(2,1)}, bf16[256,1536]{1,0:T(8,128)(2,1)}, u32[]{:S(2)}, u32[]{:S(2)}) collective-permute-start(bf16[256,1536]{1,0:T(8,128)(2,1)} %slice.1011), channel_id=1, source_target_pairs={{0,1},{1,0},{2,3},{3,2},{4,5},{5,4},{6,7},{7,6},{8,9},{9,8},{10,11... | collective-permute-start | bytes 2359304 | tf_op jit(solution)/shard_map/ppermute | solution.py:222
  425.4 21.3 %collective-permute-start.64 = (bf16[256,1536]{1,0:T(8,128)(2,1)S(1)}, bf16[256,1536]{1,0:T(8,128)(2,1)S(1)}, u32[]{:S(2)}, u32[]{:S(2)}) collective-permute-start(bf16[256,1536]{1,0:T(8,128)(2,1)S(1)} %pad_maximum_fusion.4), channel_id=1, source_target_pairs={{0,1},{1,0},{2,3},{3,2},{4,5},{5,4},{6,7},{7,6},{8,9},{9,8},{10,11... | collective-permute-start | bytes 2359304 | tf_op jit(solution)/shard_map/ppermute | solution.py:222
  431.6 65.9 %collective-permute-start.76 = (bf16[256,1536]{1,0:T(8,128)(2,1)}, bf16[256,1536]{1,0:T(8,128)(2,1)}, u32[]{:S(2)}, u32[]{:S(2)}) collective-permute-start(bf16[256,1536]{1,0:T(8,128)(2,1)} %slice.1010), channel_id=1, source_target_pairs={{0,1},{1,0},{2,3},{3,2},{4,5},{5,4},{6,7},{7,6},{8,9},{9,8},{10,11... | collective-permute-start | bytes 2359304 | tf_op jit(solution)/shard_map/ppermute | solution.py:222
  439.7 60.6 %collective-permute-start.85 = (bf16[256,1536]{1,0:T(8,128)(2,1)}, bf16[256,1536]{1,0:T(8,128)(2,1)}, u32[]{:S(2)}, u32[]{:S(2)}) collective-permute-start(bf16[256,1536]{1,0:T(8,128)(2,1)} %slice.1008), channel_id=1, source_target_pairs={{0,1},{1,0},{2,3},{3,2},{4,5},{5,4},{6,7},{7,6},{8,9},{9,8},{10,11... | collective-permute-start | bytes 2359304 | tf_op jit(solution)/shard_map/ppermute | solution.py:222
  446.7 57.7 %collective-permute-start.60 = (bf16[256,1536]{1,0:T(8,128)(2,1)}, bf16[256,1536]{1,0:T(8,128)(2,1)}, u32[]{:S(2)}, u32[]{:S(2)}) collective-permute-start(bf16[256,1536]{1,0:T(8,128)(2,1)} %slice.1014), channel_id=1, source_target_pairs={{0,1},{1,0},{2,3},{3,2},{4,5},{5,4},{6,7},{7,6},{8,9},{9,8},{10,11... | collective-permute-start | bytes 2359304 | tf_op jit(solution)/shard_map/ppermute | solution.py:222
  449.0 61.1 %collective-permute-start.69 = (bf16[256,1536]{1,0:T(8,128)(2,1)}, bf16[256,1536]{1,0:T(8,128)(2,1)}, u32[]{:S(2)}, u32[]{:S(2)}) collective-permute-start(bf16[256,1536]{1,0:T(8,128)(2,1)} %slice.1012), channel_id=1, source_target_pairs={{0,1},{1,0},{2,3},{3,2},{4,5},{5,4},{6,7},{7,6},{8,9},{9,8},{10,11... | collective-permute-start | bytes 2359304 | tf_op jit(solution)/shard_map/ppermute | solution.py:222
  500.3 21.6 %collective-permute-start.121 = (bf16[2,2,96,2,4,1,1,1,128]{8,2,4,3,0,1,7,6,5:T(8,128)(2,1)S(1)}, bf16[2,2,96,2,4,1,1,1,128]{8,2,4,3,0,1,7,6,5:T(8,128)(2,1)S(1)}, u32[]{:S(2)}, u32[]{:S(2)}) collective-permute-start(bf16[2,2,96,2,4,1,1,1,128]{8,2,4,3,0,1,7,6,5:T(8,128)(2,1)S(1)} %get-tuple-element.152), channel_id=1, source_target_pairs={{0,4},{1,5},{2,6},{3,7},{4,8},{5,9},{6,10},{7,11},{8,12},{9,13},{1... | collective-permute-start | bytes 2359304 | tf_op jit(solution)/shard_map/ppermute | solution.py:226
  504.5 21.6 %collective-permute-start.124 = (bf16[2,2,96,2,4,1,1,1,128]{8,2,4,3,0,7,6,5,1:T(8,128)(2,1)S(1)}, bf16[2,2,96,2,4,1,1,1,128]{8,2,4,3,0,7,6,5,1:T(8,128)(2,1)S(1)}, u32[]{:S(2)}, u32[]{:S(2)}) collective-permute-start(bf16[2,2,96,2,4,1,1,1,128]{8,2,4,3,0,7,6,5,1:T(8,128)(2,1)S(1)} %get-tuple-element.153), channel_id=1, source_target_pairs={{4,0},{5,1},{6,2},{7,3},{8,4},{9,5},{10,6},{11,7},{12,8},{13,9},{1... | collective-permute-start | bytes 2359304 | tf_op jit(solution)/shard_map/ppermute | solution.py:226
  512.6 19.9 %collective-permute-start.82 = (bf16[128,1536]{1,0:T(8,128)(2,1)S(1)}, bf16[128,1536]{1,0:T(8,128)(2,1)S(1)}, u32[]{:S(2)}, u32[]{:S(2)}) collective-permute-start(bf16[128,1536]{1,0:T(8,128)(2,1)S(1)} %get-tuple-element.211), channel_id=1, source_target_pairs={{0,2},{1,3},{2,0},{3,1},{4,6},{5,7},{6,4},{7,5},{8,10},{9,11},{10,... | collective-permute-start | bytes 1179656 | tf_op jit(solution)/shard_map/ppermute | solution.py:222
  526.1 20.5 %collective-permute-start.122 = (bf16[2,2,96,2,4,1,1,1,128]{8,2,4,3,0,1,7,6,5:T(8,128)(2,1)S(1)}, bf16[2,2,96,2,4,1,1,1,128]{8,2,4,3,0,1,7,6,5:T(8,128)(2,1)S(1)}, u32[]{:S(2)}, u32[]{:S(2)}) collective-permute-start(bf16[2,2,96,2,4,1,1,1,128]{8,2,4,3,0,1,7,6,5:T(8,128)(2,1)S(1)} %fusion.76), channel_id=1, source_target_pairs={{0,4},{1,5},{2,6},{3,7},{4,8},{5,9},{6,10},{7,11},{8,12},{9,13},{1... | collective-permute-start | bytes 2359304 | tf_op jit(solution)/shard_map/ppermute | solution.py:226
  528.3 20.5 %collective-permute-start.125 = (bf16[2,2,96,2,4,1,1,1,128]{8,2,4,3,0,7,6,5,1:T(8,128)(2,1)S(1)}, bf16[2,2,96,2,4,1,1,1,128]{8,2,4,3,0,7,6,5,1:T(8,128)(2,1)S(1)}, u32[]{:S(2)}, u32[]{:S(2)}) collective-permute-start(bf16[2,2,96,2,4,1,1,1,128]{8,2,4,3,0,7,6,5,1:T(8,128)(2,1)S(1)} %fusion.72), channel_id=1, source_target_pairs={{4,0},{5,1},{6,2},{7,3},{8,4},{9,5},{10,6},{11,7},{12,8},{13,9},{1... | collective-permute-start | bytes 2359304 | tf_op jit(solution)/shard_map/ppermute | solution.py:226
  546.6 418.1 %collective-permute-start.57 = (bf16[256,1536]{1,0:T(8,128)(2,1)}, bf16[256,1536]{1,0:T(8,128)(2,1)}, u32[]{:S(2)}, u32[]{:S(2)}) collective-permute-start(bf16[256,1536]{1,0:T(8,128)(2,1)} %slice.1015), channel_id=1, source_target_pairs={{0,1},{1,0},{2,3},{3,2},{4,5},{5,4},{6,7},{7,6},{8,9},{9,8},{10,11... | collective-permute-start | bytes 2359304 | tf_op jit(solution)/shard_map/ppermute | solution.py:222
  548.8 51.0 %collective-permute-start.123 = (bf16[2,2,96,2,4,1,1,1,128]{8,2,4,3,0,1,7,6,5:T(8,128)(2,1)}, bf16[2,2,96,2,4,1,1,1,128]{8,2,4,3,0,1,7,6,5:T(8,128)(2,1)}, u32[]{:S(2)}, u32[]{:S(2)}) collective-permute-start(bf16[2,2,96,2,4,1,1,1,128]{8,2,4,3,0,1,7,6,5:T(8,128)(2,1)} %fusion.78), channel_id=1, source_target_pairs={{0,4},{1,5},{2,6},{3,7},{4,8},{5,9},{6,10},{7,11},{8,12},{9,13},{1... | collective-permute-start | bytes 2359304 | tf_op jit(solution)/shard_map/ppermute | solution.py:226
  551.8 49.9 %collective-permute-start.126 = (bf16[2,2,96,2,4,1,1,1,128]{8,2,4,3,0,7,6,5,1:T(8,128)(2,1)}, bf16[2,2,96,2,4,1,1,1,128]{8,2,4,3,0,7,6,5,1:T(8,128)(2,1)}, u32[]{:S(2)}, u32[]{:S(2)}) collective-permute-start(bf16[2,2,96,2,4,1,1,1,128]{8,2,4,3,0,7,6,5,1:T(8,128)(2,1)} %fusion.74), channel_id=1, source_target_pairs={{4,0},{5,1},{6,2},{7,3},{8,4},{9,5},{10,6},{11,7},{12,8},{13,9},{1... | collective-permute-start | bytes 2359304 | tf_op jit(solution)/shard_map/ppermute | solution.py:226
  597.6 21.5 %collective-permute-start.91 = (bf16[256,1536]{1,0:T(8,128)(2,1)S(1)}, bf16[256,1536]{1,0:T(8,128)(2,1)S(1)}, u32[]{:S(2)}, u32[]{:S(2)}) collective-permute-start(bf16[256,1536]{1,0:T(8,128)(2,1)S(1)} %copy-done.66), channel_id=1, source_target_pairs={{0,2},{1,3},{2,0},{3,1},{4,6},{5,7},{6,4},{7,5},{8,10},{9,11},{10,... | collective-permute-start | bytes 2359304 | tf_op jit(solution)/shard_map/ppermute | solution.py:222
  640.0 26.1 %collective-permute-start.129 = (bf16[96,2,4,2,2,1,128]{6,0,5,4,3,2,1:T(8,128)(2,1)S(1)}, bf16[96,2,4,2,2,1,128]{6,0,5,4,3,2,1:T(8,128)(2,1)S(1)}, u32[]{:S(2)}, u32[]{:S(2)}) collective-permute-start(bf16[96,2,4,2,2,1,128]{6,0,5,4,3,2,1:T(8,128)(2,1)S(1)} %pad_maximum_fusion.13), channel_id=1, source_target_pairs={{0,16},{16,0},{1,17},{17,1},{2,18},{18,2},{3,19},{19,3},{4,20},{20... | collective-permute-start | bytes 2359304 | tf_op jit(solution)/shard_map/ppermute | solution.py:220
  641.8 38.5 %collective-permute-start.95 = (bf16[256,1536]{1,0:T(8,128)(2,1)}, bf16[256,1536]{1,0:T(8,128)(2,1)}, u32[]{:S(2)}, u32[]{:S(2)}) collective-permute-start(bf16[256,1536]{1,0:T(8,128)(2,1)} %pad_maximum_fusion.10), channel_id=1, source_target_pairs={{0,1},{1,0},{2,3},{3,2},{4,5},{5,4},{6,7},{7,6},{8,9},{9,8},{10,11... | collective-permute-start | bytes 2359304 | tf_op jit(solution)/shard_map/ppermute | solution.py:222
  714.7 186.7 %collective-permute-start.96 = (bf16[256,1536]{1,0:T(8,128)(2,1)}, bf16[256,1536]{1,0:T(8,128)(2,1)}, u32[]{:S(2)}, u32[]{:S(2)}) collective-permute-start(bf16[256,1536]{1,0:T(8,128)(2,1)} %slice.1007), channel_id=1, source_target_pairs={{0,1},{1,0},{2,3},{3,2},{4,5},{5,4},{6,7},{7,6},{8,9},{9,8},{10,11... | collective-permute-start | bytes 2359304 | tf_op jit(solution)/shard_map/ppermute | solution.py:222
  727.3 55.4 %collective-permute-start.113 = (bf16[96,1536]{1,0:T(8,128)(2,1)}, bf16[96,1536]{1,0:T(8,128)(2,1)S(1)}, u32[]{:S(2)}, u32[]{:S(2)}) collective-permute-start(bf16[96,1536]{1,0:T(8,128)(2,1)} %fusion.217), channel_id=1, source_target_pairs={{0,1},{1,0},{2,3},{3,2},{4,5},{5,4},{6,7},{7,6},{8,9},{9,8},{10,11... | collective-permute-start | bytes 884744 | tf_op jit(solution)/shard_map/ppermute | solution.py:222
  777.6 20.0 %collective-permute-start.107 = (bf16[2,2,96,3,1,1,1,192]{7,2,6,5,4,3,1,0:T(8,128)(2,1)}, bf16[2,2,96,3,1,1,1,192]{7,2,6,5,4,3,1,0:T(8,128)(2,1)S(1)}, u32[]{:S(2)}, u32[]{:S(2)}) collective-permute-start(bf16[2,2,96,3,1,1,1,192]{7,2,6,5,4,3,1,0:T(8,128)(2,1)} %get-tuple-element.159), channel_id=1, source_target_pairs={{4,0},{5,1},{6,2},{7,3},{8,4},{9,5},{10,6},{11,7},{12,8},{13,9},{1... | collective-permute-start | bytes 1327112 | tf_op jit(solution)/shard_map/ppermute | solution.py:226
  803.2 30.2 %collective-permute-start.105 = (bf16[2,2,96,3,1,1,1,192]{7,2,3,1,0,6,5,4:T(8,128)(2,1)S(1)}, bf16[2,2,96,3,1,1,1,192]{7,2,3,1,0,6,5,4:T(8,128)(2,1)S(1)}, u32[]{:S(2)}, u32[]{:S(2)}) collective-permute-start(bf16[2,2,96,3,1,1,1,192]{7,2,3,1,0,6,5,4:T(8,128)(2,1)S(1)} %fusion.139), channel_id=1, source_target_pairs={{0,4},{1,5},{2,6},{3,7},{4,8},{5,9},{6,10},{7,11},{8,12},{9,13},{1... | collective-permute-start | bytes 1327112 | tf_op jit(solution)/shard_map/ppermute | solution.py:226
  805.9 21.5 %collective-permute-start.115 = (bf16[96,1536]{1,0:T(8,128)(2,1)S(1)}, bf16[96,1536]{1,0:T(8,128)(2,1)S(1)}, u32[]{:S(2)}, u32[]{:S(2)}) collective-permute-start(bf16[96,1536]{1,0:T(8,128)(2,1)S(1)} %get-tuple-element.156), channel_id=1, source_target_pairs={{0,4},{1,5},{2,6},{3,7},{4,8},{5,9},{6,10},{7,11},{8,12},{9,13},{1... | collective-permute-start | bytes 884744 | tf_op jit(solution)/shard_map/ppermute | solution.py:226
  808.3 22.4 %collective-permute-start.118 = (bf16[96,1536]{1,0:T(8,128)(2,1)S(1)}, bf16[96,1536]{1,0:T(8,128)(2,1)S(1)}, u32[]{:S(2)}, u32[]{:S(2)}) collective-permute-start(bf16[96,1536]{1,0:T(8,128)(2,1)S(1)} %get-tuple-element.157), channel_id=1, source_target_pairs={{4,0},{5,1},{6,2},{7,3},{8,4},{9,5},{10,6},{11,7},{12,8},{13,9},{1... | collective-permute-start | bytes 884744 | tf_op jit(solution)/shard_map/ppermute | solution.py:226
  866.4 36.2 %collective-permute-start.100 = (bf16[256,1536]{1,0:T(8,128)(2,1)S(1)}, bf16[256,1536]{1,0:T(8,128)(2,1)S(1)}, u32[]{:S(2)}, u32[]{:S(2)}) collective-permute-start(bf16[256,1536]{1,0:T(8,128)(2,1)S(1)} %pad_maximum_fusion.11), channel_id=1, source_target_pairs={{0,16},{16,0},{1,17},{17,1},{2,18},{18,2},{3,19},{19,3},{4,20},{20... | collective-permute-start | bytes 2359304 | tf_op jit(solution)/shard_map/ppermute | solution.py:220
  870.3 33.4 %collective-permute-start.103 = (bf16[256,1536]{1,0:T(8,128)(2,1)S(1)}, bf16[256,1536]{1,0:T(8,128)(2,1)S(1)}, u32[]{:S(2)}, u32[]{:S(2)}) collective-permute-start(bf16[256,1536]{1,0:T(8,128)(2,1)S(1)} %pad_maximum_fusion.12), channel_id=1, source_target_pairs={{0,2},{1,3},{2,0},{3,1},{4,6},{5,7},{6,4},{7,5},{8,10},{9,11},{10,... | collective-permute-start | bytes 2359304 | tf_op jit(solution)/shard_map/ppermute | solution.py:222
  872.1 24.2 %collective-permute-start.111 = (bf16[96,3,1,2,1,192]{5,0,4,3,2,1:T(8,128)(2,1)S(1)}, bf16[96,3,1,2,1,192]{5,0,4,3,2,1:T(8,128)(2,1)S(1)}, u32[]{:S(2)}, u32[]{:S(2)}) collective-permute-start(bf16[96,3,1,2,1,192]{5,0,4,3,2,1:T(8,128)(2,1)S(1)} %get-tuple-element.223), channel_id=1, source_target_pairs={{0,2},{1,3},{2,0},{3,1},{4,6},{5,7},{6,4},{7,5},{8,10},{9,11},{10,... | collective-permute-start | bytes 663560 | tf_op jit(solution)/shard_map/ppermute | solution.py:222
  896.3 68.4 %collective-permute-start.67 = (bf16[256,1536]{1,0:T(8,128)(2,1)}, bf16[256,1536]{1,0:T(8,128)(2,1)}, u32[]{:S(2)}, u32[]{:S(2)}) collective-permute-start(bf16[256,1536]{1,0:T(8,128)(2,1)} %pad_maximum_fusion.5), channel_id=1, source_target_pairs={{0,16},{16,0},{1,17},{17,1},{2,18},{18,2},{3,19},{19,3},{4,20},{20... | collective-permute-start | bytes 2359304 | tf_op jit(solution)/shard_map/ppermute | solution.py:220
  901.4 63.3 %collective-permute-start.71 = (bf16[256,1536]{1,0:T(8,128)(2,1)}, bf16[256,1536]{1,0:T(8,128)(2,1)}, u32[]{:S(2)}, u32[]{:S(2)}) collective-permute-start(bf16[256,1536]{1,0:T(8,128)(2,1)} %pad_maximum_fusion.6), channel_id=1, source_target_pairs={{0,2},{1,3},{2,0},{3,1},{4,6},{5,7},{6,4},{7,5},{8,10},{9,11},{10,... | collective-permute-start | bytes 2359304 | tf_op jit(solution)/shard_map/ppermute | solution.py:222
  902.5 68.0 %collective-permute-start.112 = (bf16[96,3,1,2,2,192]{5,4,3,2,1,0:T(2,128)(2,1)}, bf16[96,3,1,2,2,192]{5,4,3,2,1,0:T(2,128)(2,1)}, u32[]{:S(2)}, u32[]{:S(2)}) collective-permute-start(bf16[96,3,1,2,2,192]{5,4,3,2,1,0:T(2,128)(2,1)} %pad_maximum_fusion.15), channel_id=1, source_target_pairs={{0,16},{16,0},{1,17},{17,1},{2,18},{18,2},{3,19},{19,3},{4,20},{20... | collective-permute-start | bytes 1327112 | tf_op jit(solution)/shard_map/ppermute | solution.py:220
  (206 other events, 2098.7 us)

commit v2 on v1

--- a/solution.py
+++ b/solution.py
@@ -202,6 +202,676 @@
 
 
 FF = 4096
+MESH = pl.DeviceIdType.MESH
+
+
+class Net:
+    def __init__(self):
+        self.x, self.f = lax.axis_index("rep"), lax.axis_index("fsdp")
+        self.z, self.y, self.c = self.f // 4, (self.f // 2) % 2, self.f % 2
+        self.k = self.f % 4
+        nx, fy, fc = 1 - self.x, 2 - 4 * self.y, 1 - 2 * self.c
+        self.to = {
+            "x": (nx, self.f),
+            "y": (self.x, self.f + fy),
+            "c": (self.x, self.f + fc),
+            "xy": (nx, self.f + fy),
+            "xc": (nx, self.f + fc),
+            "yc": (self.x, self.f + fy + fc),
+            "xyc": (nx, self.f + fy + fc),
+            "up": (self.x, self.f + 4),
+            "down": (self.x, self.f - 4),
+        }
+
+    def greet(self, names, line=True):
+        barrier = pltpu.get_barrier_semaphore()
+        for name in names:
+            pl.semaphore_signal(barrier, inc=1, device_id=self.to[name], device_id_type=MESH)
+        count = len(names)
+        if line:
+
+            @pl.when(self.z < 3)
+            def _():
+                pl.semaphore_signal(barrier, inc=1, device_id=self.to["up"], device_id_type=MESH)
+
+            @pl.when(self.z > 0)
+            def _():
+                pl.semaphore_signal(barrier, inc=1, device_id=self.to["down"], device_id_type=MESH)
+
+            count = count + (self.z + 3) // 4 + (6 - self.z) // 4
+        pl.semaphore_wait(barrier, count)
+
+    def copy(self, src, dst, sems, i, name):
+        return pltpu.make_async_remote_copy(
+            src_ref=src, dst_ref=dst, send_sem=sems[0].at[i], recv_sem=sems[1].at[i],
+            device_id=self.to[name], device_id_type=MESH,
+        )
+
+    def send(self, src, dst, sems, i, name):
+        copy = self.copy(src, dst, sems, i, name)
+        copy.start()
+        return copy
+
+
+def tiles(start, size, body, step=32):
+    def one(i, _):
+        body(pl.ds(pl.multiple_of(start + i * step, step), step))
+        return 0
+
+    lax.fori_loop(0, size // step, one, 0)
+
+
+def wide(v):
+    return v.astype(f32)
+
+
+class GatherLine:
+    def __init__(self, net, src, out, sems, base, keep=None):
+        self.net, self.src, self.out, self.sems, self.base = net, src, out, sems, base
+        self.keep = keep or (lambda slot: net.z >= 0)
+
+    def go(self, d, way, act):
+        net = self.net
+        slot = net.z - d if way == "up" else net.z + d
+        inside = (net.z >= d) & (net.z < 3) if way == "up" else (net.z < 4 - d) & (net.z > 0)
+        i = self.base + d + (0 if way == "up" else 3)
+
+        @pl.when(inside & self.keep(slot))
+        def _():
+            src = self.src if d == 0 else self.out.at[slot]
+            act(net.copy(src, self.out.at[slot], self.sems, i, way))
+
+    def came(self, d, way):
+        net = self.net
+        slot = net.z - d if way == "up" else net.z + d
+        inside = net.z >= d if way == "up" else net.z < 4 - d
+        i = self.base + d - 1 + (0 if way == "up" else 3)
+
+        @pl.when(inside & self.keep(slot))
+        def _():
+            net.copy(self.out.at[slot], self.out.at[slot], self.sems, i, way).wait_recv()
+
+    def step(self, d):
+        for way in ("up", "down"):
+            if d > 0:
+                self.came(d, way)
+            if d < 3:
+                self.go(d, way, lambda copy: copy.start())
+
+    def finish(self):
+        for d in range(3):
+            for way in ("up", "down"):
+                self.go(d, way, lambda copy: copy.wait_send())
+
+
+class ScatterLine:
+    def __init__(self, net, parts, got, made, sems, base):
+        self.net, self.parts, self.got, self.made, self.sems, self.base = net, parts, got, made, sems, base
+        self.n = parts.shape[1]
+
+    def each(self, d, way):
+        net = self.net
+        t = net.z + (3 - d) if way == 0 else net.z - (3 - d)
+        inside = (t < 4) if way == 0 else (t >= 0)
+        first = (net.z == 0) if way == 0 else (net.z == 3)
+        return t, inside, first, self.base + d + 3 * way, ("up", "down")[way]
+
+    def step(self, d):
+        for way in range(2):
+            t, inside, first, i, name = self.each(d, way)
+
+            @pl.when(inside & first)
+            def _():
+                self.net.copy(self.parts.at[t], self.got.at[way, d], self.sems, i, name).start()
+
+            if d == 0:
+                continue
+
+            @pl.when(inside & jnp.logical_not(first))
+            def _():
+                self.net.copy(self.got.at[way, d - 1], self.got.at[way, d - 1], self.sems, i - 1, name).wait_recv()
+
+                def body(rows):
+                    self.made[way, d - 1, rows] = (wide(self.parts[t, rows]) + wide(self.got[way, d - 1, rows])).astype(bf16)
+
+                tiles(0, self.n, body)
+                self.net.copy(self.made.at[way, d - 1], self.got.at[way, d], self.sems, i, name).start()
+
+    def finish(self, store):
+        net = self.net
+        below, above = net.z > 0, net.z < 3
+
+        @pl.when(below)
+        def _():
+            net.copy(self.got.at[0, 2], self.got.at[0, 2], self.sems, self.base + 2, "up").wait_recv()
+
+        @pl.when(above)
+        def _():
+            net.copy(self.got.at[1, 2], self.got.at[1, 2], self.sems, self.base + 5, "down").wait_recv()
+
+        def put(low, high):
+            def body(rows):
+                total = wide(self.parts[net.z, rows])
+                if low:
+                    total = total + wide(self.got[0, 2, rows])
+                if high:
+                    total = total + wide(self.got[1, 2, rows])
+                store(rows, total)
+
+            tiles(0, self.n, body)
+
+        @pl.when(below & above)
+        def _():
+            put(True, True)
+
+        @pl.when(jnp.logical_not(below))
+        def _():
+            put(False, True)
+
+        @pl.when(jnp.logical_not(above))
+        def _():
+            put(True, False)
+
+        for d in range(3):
+            for way in range(2):
+                t, inside, first, i, name = self.each(d, way)
+
+                @pl.when(inside & first)
+                def _():
+                    net.copy(self.parts.at[t], self.got.at[way, d], self.sems, i, name).wait_send()
+
+                if d > 0:
+
+                    @pl.when(inside & jnp.logical_not(first))
+                    def _():
+                        net.copy(self.made.at[way, d - 1], self.got.at[way, d], self.sems, i, name).wait_send()
+
+
+def line_scratch(n, w):
+    return [pltpu.VMEM((2, 3, n, w), bf16), pltpu.VMEM((2, 2, n, w), bf16)]
+
+
+LINE_COPIES = 6
+
+
+def gather_rows(net, v, out, sems, base, ready, poll):
+    n = v.shape[0]
+    A, B = pl.ds(0, n // 2), pl.ds(n // 2, n // 2)
+    go = {}
+    ready(0)
+    go["xA"] = net.send(v.at[A], out.at[1, 0, A], sems, base + 0, "x")
+    go["yA"] = net.send(v.at[A], out.at[2, 0, A], sems, base + 3, "y")
+    go["0A"] = net.send(v.at[A], out.at[0, 1, A], sems, base + 4, "c")
+    ready(1)
+    go["yB"] = net.send(v.at[B], out.at[2, 0, B], sems, base + 2, "y")
+    go["xB"] = net.send(v.at[B], out.at[1, 0, B], sems, base + 1, "x")
+    go["0B"] = net.send(v.at[B], out.at[0, 1, B], sems, base + 5, "c")
+    poll()
+    go["xA"].wait_recv()
+    go["dA"] = net.send(out.at[1, 0, A], out.at[3, 0, A], sems, base + 6, "y")
+    go["1A"] = net.send(out.at[1, 0, A], out.at[1, 1, A], sems, base + 8, "c")
+    go["yA"].wait_recv()
+    go["2A"] = net.send(out.at[2, 0, A], out.at[2, 1, A], sems, base + 10, "c")
+    poll()
+    go["yB"].wait_recv()
+    go["dB"] = net.send(out.at[2, 0, B], out.at[3, 0, B], sems, base + 7, "x")
+    go["2B"] = net.send(out.at[2, 0, B], out.at[2, 1, B], sems, base + 9, "c")
+    go["xB"].wait_recv()
+    go["1B"] = net.send(out.at[1, 0, B], out.at[1, 1, B], sems, base + 11, "c")
+    poll()
+    go["dA"].wait_recv()
+    go["3A"] = net.send(out.at[3, 0, A], out.at[3, 1, A], sems, base + 12, "c")
+    go["dB"].wait_recv()
+    go["3B"] = net.send(out.at[3, 0, B], out.at[3, 1, B], sems, base + 13, "c")
+    poll()
+    for name in ("0A", "0B", "1A", "2B", "2A", "1B", "3A", "3B"):
+        go[name].wait_recv()
+    for copy in go.values():
+        copy.wait_send()
+
+
+GATHER_COPIES = 14
+SCATTER_COPIES = 10
+
+
+def scatter_rows(net, parts, rc, rd, rx, ry, td, tx, ty, sems, base, poll):
+    n = parts.shape[2]
+    A, B = pl.ds(0, n // 2), pl.ds(n // 2, n // 2)
+    go = {}
+    for i, chip in enumerate((3, 1, 2, 0)):
+        go[chip] = net.send(parts.at[chip, 1], rc.at[chip], sems, base + i, "c")
+
+    def add(dst, chip, start, more=None):
+        def body(rows):
+            total = wide(parts[chip, 0, rows]) + wide(rc[chip, rows])
+            if more is not None:
+                total = total + wide(more[rows])
+            dst[rows] = total.astype(bf16)
+
+        tiles(start, n // 2, body)
+
+    go[3].wait_recv()
+    add(td, 3, 0)
+    go["dA"] = net.send(td.at[A], rd.at[A], sems, base + 4, "x")
+    add(td, 3, n // 2)
+    go["dB"] = net.send(td.at[B], rd.at[B], sems, base + 5, "y")
+    go[1].wait_recv()
+    add(tx, 1, 0)
+    go["xA"] = net.send(tx.at[A], rx.at[A], sems, base + 6, "x")
+    go[2].wait_recv()
+    add(ty, 2, n // 2)
+    go["yB"] = net.send(ty.at[B], ry.at[B], sems, base + 7, "y")
+    poll()
+    go["dA"].wait_recv()
+    add(ty, 2, 0, rd)
+    go["yA"] = net.send(ty.at[A], ry.at[A], sems, base + 8, "y")
+    go["dB"].wait_recv()
+    add(tx, 1, n // 2, rd)
+    go["xB"] = net.send(tx.at[B], rx.at[B], sems, base + 9, "x")
+    go[0].wait_recv()
+
+    def done(half):
+        for name in (("xA", "yA"), ("xB", "yB"))[half]:
+            go[name].wait_recv()
+        if half == 1:
+            for copy in go.values():
+                copy.wait_send()
+
+    return done
+
+
+def scatter_scratch(n, w):
+    return [pltpu.VMEM((4, n, w), bf16)] + [pltpu.VMEM((n, w), bf16)] * 6
+
+
+def dma_sems(count):
+    return [pltpu.SemaphoreType.DMA((count,)), pltpu.SemaphoreType.DMA((count,))]
+
+
+VM = pl.BlockSpec(memory_space=pltpu.VMEM)
+ANY = pl.BlockSpec(memory_space=pl.ANY)
+
+
+def polls(*acts):
+    left = list(acts)
+
+    def poll():
+        if left:
+            left.pop(0)()
+
+    def drain():
+        while left:
+            poll()
+
+    return poll, drain
+
+
+def comm_call(body, name, ident, ins, in_specs, outs, out_specs, scratch):
+    return pl.pallas_call(
+        body,
+        in_specs=in_specs,
+        out_specs=out_specs,
+        out_shape=outs,
+        scratch_shapes=scratch,
+        compiler_params=pltpu.CompilerParams(collective_id=ident, has_side_effects=True, vmem_limit_bytes=60 << 20),
+        name=name,
+    )(*ins)
+
+
+def shape(dims, dtype):
+    return jax.ShapeDtypeStruct(dims, dtype)
+
+
+PLANE = ("x", "y", "c", "xy", "xc", "yc", "xyc")
+PLACES = {"c": (0, 1), "x": (1, 0), "xc": (1, 1), "y": (2, 0), "yc": (2, 1), "xy": (3, 0), "xyc": (3, 1)}
+
+
+def start_call(x, dy, docs, gains, w_qkv, w_gate, w_up, w_out, ident):
+    n, w = x.shape
+    rows = w_qkv.shape[0]
+
+    def body(x_ref, dy_ref, docs_ref, g_ref, wq_ref, gate_ref, up_ref, wo_ref,
+             xs_ref, dys_ref, docs_out, gains_out, qkv_out, gu_out, wo_out, slots, gus, local, send, recv):
+        net = Net()
+        sems = (send, recv)
+        base = 2 * GATHER_COPIES
+        line_q = GatherLine(net, qkv_out.at[net.z], qkv_out, sems, base)
+        line_o = GatherLine(net, wo_ref, wo_out, sems, base + 6, lambda slot: slot // 2 == net.x)
+        line_g = GatherLine(net, gains_out.at[net.z], gains_out, sems, base + 12)
+        base += 18
+        slots[...] = jnp.zeros_like(slots)
+        for half in range(2):
+
+            @pl.when(net.x == half)
+            def _():
+                for k in range(4):
+                    pair = 4 * half + 2 * (k % 2) + k // 2
+                    for m in range(6):
+                        col = (m // 2) * MODEL_WIDTH + (2 * pair + m % 2) * E
+                        slots[k, :, m * EP : m * EP + E] = wq_ref[:, col : col + E]
+                    for m in range(8):
+                        src = gate_ref if m < 4 else up_ref
+                        col = 256 * (4 * (m % 4) + k) + 128 * half
+                        gus[k, :, m * 128 : (m + 1) * 128] = src[:, col : col + 128]
+
+        net.greet(PLANE)
+        own = [
+            pltpu.make_async_copy(x_ref, xs_ref.at[0, 0], local.at[0]),
+            pltpu.make_async_copy(dy_ref, dys_ref.at[0, 0], local.at[1]),
+            pltpu.make_async_copy(slots.at[net.k], qkv_out.at[net.z, net.k], local.at[2]),
+            pltpu.make_async_copy(gus.at[net.k], gu_out.at[net.k], local.at[3]),
+            pltpu.make_async_copy(g_ref, gains_out.at[net.z, net.k], local.at[4]),
+            pltpu.make_async_copy(docs_ref, docs_out.at[0, 0], local.at[5]),
+            pltpu.make_async_copy(wo_ref, wo_out.at[net.z], local.at[6]),
+        ]
+        for copy in own:
+            copy.start()
+        shares, small = [], []
+        flips = {"c": net.k + 1 - 2 * net.c, "y": net.k + 2 - 4 * net.y, "yc": net.k + 1 - 2 * net.c + 2 - 4 * net.y}
+        for j, name in enumerate(("y", "yc", "c")):
+            other = flips[name]
+            shares.append(net.send(slots.at[other], qkv_out.at[net.z, net.k], sems, base + j, name))
+            small.append(net.send(g_ref, gains_out.at[net.z, net.k], sems, base + 6 + j, name))
+        for j, (name, (chip, core)) in enumerate(PLACES.items()):
+            small.append(net.send(docs_ref, docs_out.at[chip, core], sems, base + 9 + j, name))
+
+        def rest():
+            for j, name in enumerate(("y", "yc", "c")):
+                small.append(net.send(gus.at[flips[name]], gu_out.at[net.k], sems, base + 3 + j, name))
+
+        def line0():
+            own[2].wait()
+            own[4].wait()
+            for copy in shares:
+                copy.wait_recv()
+            for copy in small[:3]:
+                copy.wait_recv()
+            line_q.step(0)
+            line_g.step(0)
+            line_o.step(0)
+
+        def both(d):
+            def act():
+                line_q.step(d)
+                line_g.step(d)
+
+            return act
+
+        first, _ = polls(line0, both(1))
+        gather_rows(net, x_ref, xs_ref, sems, 0, lambda half: None, first)
+        rest()
+        second, drain = polls(both(2), lambda: line_o.step(1), both(3), lambda: line_o.step(2))
+        gather_rows(net, dy_ref, dys_ref, sems, GATHER_COPIES, lambda half: None, second)
+        drain()
+        line_o.step(3)
+        for line in (line_q, line_g, line_o):
+            line.finish()
+        for copy in own[:2] + [own[3]] + own[5:]:
+            copy.wait()
+        for copy in small[3:]:
+            copy.wait_recv()
+        for copy in shares + small:
+            copy.wait_send()
+
+    return comm_call(
+        body, "start", ident, (x, dy, docs, gains, w_qkv, w_gate, w_up, w_out), [VM] * 7 + [ANY],
+        [shape((4, 2, n, w), bf16), shape((4, 2, n, w), bf16), shape((4, 2) + docs.shape, docs.dtype), shape((4, 4) + gains.shape, bf16),
+         shape((4, 4, rows, 6 * EP), bf16), shape((4, rows, FF // 4), bf16), shape((4, rows, MODEL_WIDTH), bf16)],
+        [ANY] * 7,
+        [pltpu.VMEM((4, rows, 6 * EP), bf16), pltpu.VMEM((4, rows, FF // 4), bf16), pltpu.SemaphoreType.DMA((7,))]
+        + dma_sems(2 * GATHER_COPIES + 18 + 16),
+    )
+
+
+def mid_call(parts, x, gain, gu, w_down, ident):
+    n, w = parts.shape[2:]
+    down = w_down.shape[0] // 2
+
+    def body(p_ref, x_ref, g_ref, gu_ref, wd_ref, resid_ref, out_ref, gu_out, wd_out, v, local, rc, rd, rx, ry, td, tx, ty, send, recv):
+        net = Net()
+        sems = (send, recv)
+        net.greet("xyc")
+        base = SCATTER_COPIES + GATHER_COPIES
+        mine = wd_ref.at[pl.ds(pl.multiple_of(down * net.x, down), down)]
+        line_g = GatherLine(net, gu_ref, gu_out, sems, base)
+        line_d = GatherLine(net, mine, wd_out, sems, base + LINE_COPIES)
+        lines = (line_g, line_d)
+        own = [pltpu.make_async_copy(gu_ref, gu_out.at[net.z], local.at[1]), pltpu.make_async_copy(mine, wd_out.at[net.z], local.at[2])]
+        for copy in own:
+            copy.start()
+        for line in lines:
+            line.step(0)
+        poll, drain = polls(*[lambda d=d, line=line: line.step(d) for d in (1, 2, 3) for line in lines])
+        done = scatter_rows(net, p_ref, rc, rd, rx, ry, td, tx, ty, sems, 0, poll)
+        poll()
+
+        def ready(half):
+            done(half)
+
+            def rows_of(rows):
+                total = wide(p_ref[0, 0, rows]) + wide(rc[0, rows]) + wide(rx[rows]) + wide(ry[rows])
+                resid = wide(x_ref[rows]) + total
+                resid_ref[rows] = resid
+                r = lax.rsqrt(jnp.mean(resid * resid, axis=1, keepdims=True) + 1e-06)
+                v[rows] = (resid * r * g_ref[...]).astype(bf16)
+
+            tiles(half * (n // 2), n // 2, rows_of)
+
+        gather_rows(net, v, out_ref, sems, SCATTER_COPIES, ready, poll)
+        drain()
+        last = pltpu.make_async_copy(v, out_ref.at[0, 0], local.at[0])
+        last.start()
+        for line in lines:
+            line.finish()
+        for copy in own:
+            copy.wait()
+        last.wait()
+
+    return comm_call(
+        body, "mid", ident, (parts, x, gain, gu, w_down), [VM] * 3 + [ANY] * 2,
+        [shape((n, w), f32), shape((4, 2, n, w), bf16), shape((4,) + gu.shape, bf16), shape((4, down, w), bf16)], [VM, ANY, ANY, ANY],
+        [pltpu.VMEM((n, w), bf16), pltpu.SemaphoreType.DMA((3,))] + scatter_scratch(n, w)
+        + dma_sems(SCATTER_COPIES + GATHER_COPIES + 2 * LINE_COPIES),
+    )
+
+
+def mid_back_call(parts, dy, resid, gain, gu, down, ident):
+    n, w = parts.shape[2:]
+
+    def body(p_ref, dy_ref, r_ref, g_ref, gu_ref, down_ref, dresid_ref, out_ref, sum_ref, gu_out, down_out,
+             v, local, rc, rd, rx, ry, td, tx, ty, g_got, g_made, d_got, d_made, send, recv):
+        net = Net()
+        sems = (send, recv)
+        net.greet("xyc")
+        base = SCATTER_COPIES + GATHER_COPIES
+        line_g = ScatterLine(net, gu_ref, g_got, g_made, sems, base)
+        line_d = ScatterLine(net, down_ref, d_got, d_made, sems, base + LINE_COPIES)
+        lines = (line_g, line_d)
+        for line in lines:
+            line.step(0)
+        acts = [lambda d=d, line=line: line.step(d) for d in (1, 2) for line in lines]
+        poll, drain = polls(acts[0], acts[1], lambda: None, acts[2], acts[3])
+        sum_ref[...] = jnp.zeros_like(sum_ref)
+        done = scatter_rows(net, p_ref, rc, rd, rx, ry, td, tx, ty, sems, 0, poll)
+        poll()
+
+        def ready(half):
+            done(half)
+
+            def rows_of(rows):
+                da2 = wide(p_ref[0, 0, rows]) + wide(rc[0, rows]) + wide(rx[rows]) + wide(ry[rows])
+                res = r_ref[rows]
+                r = lax.rsqrt(jnp.mean(res * res, axis=1, keepdims=True) + 1e-06)
+                unit = res * r
+                sum_ref[0:1] += jnp.sum(da2 * unit, axis=0, keepdims=True)
+                dn = da2 * g_ref[...]
+                dresid = wide(dy_ref[rows]) + r * (dn - unit * r * jnp.mean(dn * res, axis=1, keepdims=True))
+                dresid_ref[rows] = dresid
+                v[rows] = dresid.astype(bf16)
+
+            tiles(half * (n // 2), n // 2, rows_of)
+
+        gather_rows(net, v, out_ref, sems, SCATTER_COPIES, ready, poll)
+        drain()
+        last = pltpu.make_async_copy(v, out_ref.at[0, 0], local)
+        last.start()
+
+        def put(ref):
+            def store(rows, total):
+                ref[rows] = total.astype(bf16)
+
+            return store
+
+        line_g.finish(put(gu_out))
+        line_d.finish(put(down_out))
+        last.wait()
+
+    return comm_call(
+        body, "mid_back", ident, (parts, dy, resid, gain, gu, down), [VM] * 6,
+        [shape((n, w), f32), shape((4, 2, n, w), bf16), shape((8, w), f32), shape(gu.shape[1:], bf16), shape(down.shape[1:], bf16)],
+        [VM, ANY, VM, VM, VM],
+        [pltpu.VMEM((n, w), bf16), pltpu.SemaphoreType.DMA] + scatter_scratch(n, w) + line_scratch(*gu.shape[1:]) + line_scratch(*down.shape[1:])
+        + dma_sems(SCATTER_COPIES + GATHER_COPIES + 2 * LINE_COPIES),
+    )
+
+
+def end_call(da_parts, out_parts, qkv, wo, small, x, resid, dresid, gain, ident):
+    n, w = da_parts.shape[2:]
+    rows_q = qkv.shape[1] // 4
+    rows_o = wo.shape[1]
+
+    def body(da_ref, op_ref, q_ref, wo_ref, small_ref, x_ref, resid_ref, dresid_ref, g_ref,
+             out_ref, gx_ref, gq_ref, go_ref, total_ref,
+             rc, rd, rx, ry, td, tx, ty, rc2, rd2, rx2, ry2, td2, tx2, ty2,
+             q_got, q_made, o_got, o_made, zq, cq, fq, po, ro, s_got, s_sum, s_line, send, recv):
+        net = Net()
+        sems = (send, recv)
+        net.greet("xyc")
+        z, x, y, c = net.z, net.x, net.y, net.c
+        base = 2 * SCATTER_COPIES
+        line_q = ScatterLine(net, q_ref, q_got, q_made, sems, base)
+        line_o = ScatterLine(net, po, o_got, o_made, sems, base + 6)
+        line_s = GatherLine(net, s_sum.at[2], s_line, sems, base + 12)
+        base += 18
+        line_q.step(0)
+        to_c = net.send(wo_ref.at[1 - c], po.at[2 * x + c], sems, base, "c")
+        hop = net.send(small_ref, s_got.at[0], sems, base + 1, "c")
+        hops = [hop]
+        po[2 * (1 - x)] = jnp.zeros((rows_o, w), bf16)
+        po[2 * (1 - x) + 1] = jnp.zeros((rows_o, w), bf16)
+        po[2 * x + c] = wo_ref[c]
+
+        def small_step(i):
+            hops[i].wait_recv()
+            s_sum[i] = (small_ref[...] if i == 0 else s_sum[i - 1]) + s_got[i]
+            if i < 2:
+                hops.append(net.send(s_sum.at[i], s_got.at[i + 1], sems, base + 2 + i, "yx"[i]))
+            else:
+                line_s.step(0)
+
+        def begin():
+            small_step(0)
+            to_c.wait_recv()
+            line_o.step(0)
+
+        poll, _ = polls(begin)
+        done = scatter_rows(net, da_ref, rc, rd, rx, ry, td, tx, ty, sems, 0, poll)
+        line_q.step(1)
+        small_step(1)
+        line_o.step(1)
+
+        def later():
+            line_q.step(2)
+            small_step(2)
+
+        poll, _ = polls(later)
+        done2 = scatter_rows(net, op_ref, rc2, rd2, rx2, ry2, td2, tx2, ty2, sems, SCATTER_COPIES, poll)
+        line_o.step(2)
+        line_s.step(1)
+        for half in range(2):
+            done(half)
+
+            def rows_of(rows):
+                da = wide(da_ref[0, 0, rows]) + wide(rc[0, rows]) + wide(rx[rows]) + wide(ry[rows])
+                xf = wide(x_ref[rows])
+                r = lax.rsqrt(jnp.mean(xf * xf, axis=1, keepdims=True) + 1e-06)
+                dn = da * g_ref[...]
+                gx_ref[rows] = dresid_ref[rows] + r * (dn - xf * r * r * jnp.mean(dn * xf, axis=1, keepdims=True))
+
+            tiles(half * (n // 2), n // 2, rows_of)
+
+        def put_q(rows, total):
+            zq[rows] = total.astype(bf16)
+
+        def put_o(rows, total):
+            ro[0, rows] = total.astype(bf16)
+
+        line_q.finish(put_q)
+        block = lambda i, j: pl.ds(pl.multiple_of((2 * i + j) * rows_q, rows_q), rows_q)
+        swaps = [net.send(zq.at[block(i, 1 - c)], cq.at[i, c], sems, base + 4 + i, "c") for i in range(2)]
+        for i in range(2):
+            cq[i, c] = zq[block(i, c)]
+        for copy in swaps:
+            copy.wait_recv()
+        swaps.append(net.send(cq.at[1 - y], fq.at[x, y], sems, base + 6, "y"))
+        fq[x, y] = cq[y]
+        line_s.step(2)
+        line_o.finish(put_o)
+        swaps.append(net.send(ro.at[0], ro.at[1], sems, base + 7, "x"))
+        swaps[2].wait_recv()
+        swaps.append(net.send(fq.at[x], fq.at[x], sems, base + 8, "x"))
+        line_s.step(3)
+        s_line[z] = s_sum[2]
+        total_ref[...] = (s_line[0] + s_line[1]) + (s_line[2] + s_line[3])
+        for half in range(2):
+            done2(half)
+
+            def sum_of(rows):
+                total = wide(op_ref[0, 0, rows]) + wide(rc2[0, rows]) + wide(rx2[rows]) + wide(ry2[rows])
+                out_ref[rows] = (resid_ref[rows] + total).astype(bf16)
+
+            tiles(half * (n // 2), n // 2, sum_of)
+        swaps[3].wait_recv()
+        go_ref[...] = wide(ro[0]) + wide(ro[1])
+        swaps[4].wait_recv()
+        for i in range(2):
+            for k in range(4):
+                pair = 4 * i + 2 * (k % 2) + k // 2
+                for m in range(6):
+                    col = (m // 2) * MODEL_WIDTH + (2 * pair + m % 2) * E
+                    gq_ref[:, col : col + E] = wide(fq[i, k // 2, k % 2, :, m * EP : m * EP + E])
+        line_s.finish()
+        for copy in swaps + hops + [to_c]:
+            copy.wait_send()
+
+    stages = [pltpu.VMEM((2, rows_o, w), bf16), pltpu.VMEM((3,) + small.shape, f32), pltpu.VMEM((3,) + small.shape, f32),
+              pltpu.VMEM((4,) + small.shape, f32)]
+    return comm_call(
+        body, "end", ident, (da_parts, out_parts, qkv, wo, small, x, resid, dresid, gain), [VM] * 9,
+        [shape((n, w), bf16), shape((n, w), f32), shape((rows_q, 3 * MODEL_WIDTH), f32), shape((rows_o, w), f32), shape(small.shape, f32)],
+        [VM] * 5,
+        scatter_scratch(n, w) * 2 + line_scratch(*qkv.shape[1:]) + line_scratch(rows_o, w)
+        + [pltpu.VMEM(qkv.shape[1:], bf16), pltpu.VMEM((2, 2, rows_q, 6 * EP), bf16), pltpu.VMEM((2, 2, 2, rows_q, 6 * EP), bf16),
+           pltpu.VMEM((4, rows_o, w), bf16)]
+        + stages + dma_sems(2 * SCATTER_COPIES + 18 + 9),
+    )
+
+
+def place_gu(pieces):
+    rows = pieces.shape[3]
+
+    def body(p_ref, gate_ref, up_ref):
+        for i in range(2):
+            for k in range(4):
+                for m in range(8):
+                    col = 256 * (4 * (m % 4) + k) + 128 * i
+                    dst = gate_ref if m < 4 else up_ref
+                    dst[:, col : col + 128] = wide(p_ref[i, k // 2, k % 2, :, m * 128 : (m + 1) * 128])
+
+    return pl.pallas_call(
+        body, in_specs=[VM], out_specs=[VM] * 2, out_shape=[shape((rows, FF), f32)] * 2, name="place_gu",
+        compiler_params=pltpu.CompilerParams(vmem_limit_bytes=16 << 20),
+    )(pieces)
 
 
 def rms_scale(values):
@@ -526,13 +1196,147 @@
     )
 
 
+def join(bit, mine, other, axis):
+    first, second = jnp.where(bit == 0, mine, other), jnp.where(bit == 0, other, mine)
+    return jnp.stack([first, second], axis)
+
+
+def fast(
+    x_in,
+    doc_ids,
+    w_qkv,
+    w_out,
+    gain_attn,
+    gain_group,
+    conv_kernel,
+    head_mix,
+    gain_ffn,
+    w_gate,
+    w_up,
+    w_down,
+    cotangent,
+):
+    links = Links(16)
+    pair = 4 * links.x + 2 * links.c + links.y
+    tokens = x_in.shape[1]
+    x, dy = x_in[0], cotangent[0]
+    rows = w_qkv.shape[0]
+
+    gains = jnp.pad(jnp.stack([gain_attn, gain_group, gain_ffn]), ((0, 13), (0, 128 - rows)))
+    docs = jnp.broadcast_to(doc_ids, (8, tokens))
+    x_all, dffn_all, docs, gains, qkv_w, gu_plane, out_w = start_call(x, dy, docs, gains, w_qkv, w_gate, w_up, w_out, 1)
+    docs = docs.reshape(8, 8, tokens)[:, 0]
+    gains = gains.reshape(16, 16, 128)[:, :3, :rows].astype(f32).transpose(1, 0, 2).reshape(3, MODEL_WIDTH)
+    gain_a, gain_g, gain_f = gains[0:1], gains[1], gains[2:3]
+    qkv_w = qkv_w.reshape(MODEL_WIDTH, 6 * EP)
+    keep = lax.dynamic_index_in_dim(out_w, 2 * links.x + links.c, 0, keepdims=False)
+    other = links.across("c", lax.dynamic_index_in_dim(out_w, 2 * links.x + 1 - links.c, 0, keepdims=False))
+    out_w = jnp.pad(join(links.c, keep, other, 0), ((0, 0), (0, EP - E), (0, 0))).reshape(2 * EP, MODEL_WIDTH)
+
+    kernel = lax.dynamic_slice_in_dim(conv_kernel, 2 * pair, 2, 0)
+    mix = lax.dynamic_slice_in_dim(head_mix, 2 * pair, 2, 0)
+    th, tl, tt = bands(kernel, tokens)
+    group = lax.dynamic_slice_in_dim(gain_g.reshape(8, 2, E), pair, 1, 0)
+    group = jnp.pad(group, ((0, 0), (0, 0), (0, EP - E))).reshape(1, 2 * EP)
+    doc_col, doc_row = docs[:, :, None], docs[:, None, :]
+
+    x_all = x_all.reshape(8 * tokens, MODEL_WIDTH)
+    dffn_all = dffn_all.reshape(8 * tokens, MODEL_WIDTH)
+    xf_all = x_all.astype(f32)
+    a1 = (xf_all * rms_scale(xf_all) * gain_a).astype(bf16)
+    qkv = dot(a1, qkv_w).astype(bf16).reshape(8, tokens, 6 * EP)
+    normed, xhat, s, probs, zeroed = attend(mix, qkv, doc_col, doc_row, th, tl, group)
+    normed = normed.reshape(8 * tokens, 2 * EP)
+    by_chip = lambda v: v.astype(bf16).reshape(4, 2, tokens, MODEL_WIDTH)
+    resid, a2, gu_w, down_w = mid_call(by_chip(dot(normed, out_w)), x, gain_f, gu_plane, w_down, 2)
+
+    a2 = a2.reshape(8 * tokens, MODEL_WIDTH)
+    gu_w = gu_w.reshape(MODEL_WIDTH, FF // 4)
+    down_w = down_w.reshape(FF // 8, MODEL_WIDTH)
+    half = FF // 8
+    gu = dot(a2, gu_w)
+    gate, up_act = gu[:, :half], gu[:, half:]
+    sig = jax.nn.sigmoid(gate)
+    silu = gate * sig
+    hidden = (silu * up_act).astype(bf16)
+    dhidden = dot(dffn_all, down_w, 1, 1)
+    dgate = (dhidden * up_act * sig * (1.0 + gate * (1.0 - sig))).astype(bf16)
+    dup = (dhidden * silu).astype(bf16)
+    dgu = jnp.concatenate([dgate, dup], 1)
+    grad_gu = dot(a2, dgu, 0, 0).astype(bf16).reshape(4, 4 * rows, FF // 4)
+    grad_down = dot(hidden, dffn_all, 0, 0).astype(bf16).reshape(4, FF // 32, MODEL_WIDTH)
+    out_parts = by_chip(dot(hidden, down_w))
+    dresid, dattn, sum_f, grad_gu, grad_down = mid_back_call(
+        by_chip(dot(dgu, gu_w, 1, 1)), dy, resid, gain_f, grad_gu, grad_down, 3
+    )
+    v = grad_gu.reshape(2, 2, rows, FF // 4)
+    sent = links.across("c", lax.dynamic_index_in_dim(v, 1 - links.c, 1, keepdims=False))
+    v = join(links.c, lax.dynamic_index_in_dim(v, links.c, 1, keepdims=False), sent, 1)
+    sent = links.across("y", lax.dynamic_index_in_dim(v, 1 - links.y, 0, keepdims=False))
+    v = join(links.y, lax.dynamic_index_in_dim(v, links.y, 0, keepdims=False), sent, 0)
+    grad_gate, grad_up = place_gu(join(links.x, v, links.across("x", v), 0))
+    grad_down = join(links.x, grad_down, links.across("x", grad_down), 0).reshape(-1, MODEL_WIDTH).astype(f32)
+
+    dattn = dattn.reshape(8 * tokens, MODEL_WIDTH)
+    dnormed = dot(dattn, out_w, 1, 1).reshape(8, tokens, 2 * EP)
+    dqkv, conv_tiles, mix_sums, group_sums = attend_back(
+        mix, qkv, doc_col, doc_row, tt, group, dnormed, xhat, s, probs, zeroed
+    )
+    dqkv = dqkv.reshape(8 * tokens, 6 * EP)
+    grad_qkv = dot(a1, dqkv, 0, 0)
+    sum_a = jnp.sum(grad_qkv * qkv_w.astype(f32), axis=1) / gain_a[0]
+    grad_out = dot(normed, dattn, 0, 0).astype(bf16).reshape(2, EP, MODEL_WIDTH)[:, :rows]
+    place = lambda v: lax.dynamic_update_index_in_dim(jnp.zeros((8,) + v.shape, f32), v, pair, 0)
+    small = [
+        sum_a,
+        sum_f[0],
+        place(group_sums[0].reshape(2, EP)[:, :E].reshape(-1)),
+        place(diagonals(conv_tiles)),
+        place(jnp.sum(mix_sums[:4], axis=1)),
+    ]
+    cut = [0]
+    for v in small:
+        cut.append(cut[-1] + v.size)
+    room = 48 * 128
+    flat = jnp.concatenate([v.reshape(-1) for v in small] + [jnp.zeros((room - cut[-1],), f32)]).reshape(48, 128)
+    out, grad_x, grad_qkv, grad_out, total = end_call(
+        by_chip(dot(dqkv, qkv_w, 1, 1)),
+        out_parts,
+        grad_qkv.astype(bf16).reshape(4, 4 * rows, 6 * EP),
+        grad_out,
+        flat,
+        x,
+        resid,
+        dresid,
+        gain_a,
+        4,
+    )
+    total = total.reshape(-1)
+    gain_a_sum, gain_f_sum, group_sum, conv_sum, mix_sum = (total[cut[i] : cut[i + 1]] for i in range(5))
+    own = lambda v: lax.dynamic_slice_in_dim(v, lax.axis_index("fsdp") * rows, rows, 0)
+    return (
+        out[None],
+        grad_x[None],
+        grad_qkv,
+        grad_out,
+        own(gain_a_sum),
+        own(group_sum),
+        conv_sum.reshape(H, QWIN, KWIN),
+        mix_sum.reshape(H, 2),
+        own(gain_f_sum),
+        grad_gate,
+        grad_up,
+        grad_down,
+    )
+
+
 def solution(mesh):
     fsdp = mesh.shape["fsdp"]
     assert mesh.shape["rep"] == 2 and fsdp % 4 == 0
     rows, shard, part = P(("rep", "fsdp"), None, None), P("fsdp", None), P("fsdp")
     placed = (rows, P(("rep", "fsdp"), None), shard, shard, part, part, P(), P(), part, shard, shard, shard, rows)
     return jax.shard_map(
-        lambda *args: per_device(fsdp, *args),
+        fast if fsdp == 16 else (lambda *args: per_device(fsdp, *args)),
         mesh=mesh,
         in_specs=placed,
         out_specs=(rows, rows, shard, shard, part, part, P(), P(), part, shard, shard, shard),

time: 994 us -> 566 us (0.57)
  Pallas kernels: 42 us -> 396 us
  waiting for transfers between devices: 262 us -> 17.7 us
  starting transfers between devices: 204 us -> 1.3 us
  local copies, waits for them, and re-layouts: 197 us -> 30.3 us
  other arithmetic: 119 us -> 27.7 us
  blocking collectives: 54.3 us -> 0 us
  matrix products: 95.8 us -> 85.5 us
    pallas_call x0 -> x5, Pallas kernels: none -> 354 us  [the longest x4 352 us: comm_call(): pl.pallas_call(body, in_specs=in_specs, out_specs=out_specs, out_shape=ou...]
    ppermute x54 -> x0, waiting for transfers between devices: 153 us -> none  [along(): return lax.ppermute(v, 'fsdp', pairs)]
    ppermute x54 -> x0, starting transfers between devices: 152 us -> none  [along(): return lax.ppermute(v, 'fsdp', pairs)]
    ppermute x62 -> x3, waiting for transfers between devices: 58.7 us -> 0.01 us  [across(): return lax.ppermute(v, 'fsdp', [(f, f ^ bit) for f in range(self.fsdp)])]
    psum x1 -> x0, blocking collectives: 54.3 us -> none  [per_device(): lax.psum(jnp.concatenate([v.reshape(-1) for v in small]), ('rep', 'fsdp'))]
    reshape x12 -> x4, local copies, waits for them, and re-layouts: 46.7 us -> 0.49 us  [the longest x3 0.32 us: fast(): v.reshape(-1)]
    unnamed x348 -> x83, local copies, waits for them, and re-layouts: 52.7 us -> 7.13 us
    ppermute x21 -> x2, waiting for transfers between devices: 50.8 us -> 17.7 us  [across(): return lax.ppermute(v, 'rep', [(0, 1), (1, 0)])]
  transfers between devices with their start and end apart: 137 -> 5, of which waited for: 50 -> 1; matrix products, arithmetic and copies ran while one was open for 40% -> 10% of each run, Pallas kernels for 4% -> 20%
where the time goes in v2:
time: 566 us; the launch traced here: 560 us
  Pallas kernels  396 us (70%)
  matrix products  85.5 us (15%)
  local copies, waits for them, and re-layouts  30.3 us (5%)
  other arithmetic  27.7 us (5%)
  waiting for transfers between devices  17.7 us (3%)
    pallas_call x4, Pallas kernels, comm_call(): pl.pallas_call(body, in_specs=in_specs, out_specs=out_specs, out_shape=ou...  352 us
    dot_general x12, matrix products, dot(): lax.dot_general(a, b, (((ca,), (cb,)), ((), ())), preferred_element_type=...  85.5 us
    pallas_call x1, Pallas kernels, attend_back(): pl.pallas_call(bwd_kernel, grid=(n,), in_specs=[pl.BlockSpec(memory_space...  21.6 us
    pallas_call x1, Pallas kernels, attend(): pl.pallas_call(fwd_kernel, grid=(n,), in_specs=[pl.BlockSpec(memory_space...  20.7 us
    ppermute x2, waiting for transfers between devices, across(): return lax.ppermute(v, 'rep', [(0, 1), (1, 0)])  17.7 us
  transfers between devices with their start and end apart: 5, of which 1 were waited for; matrix products, arithmetic and copies ran while one was open for 10% of the time, Pallas kernels for 20%

profile of v2, /device:TPU:16, one launch (start us, length us, event | category | flops | bytes accessed | tf_op | source)
XLA Modules:
  0.0 560.2 jit_solution(9787436041895802049)
XLA Ops:
  0.7 1.3 fusion.63.g_ref
  2.0 1.3 broadcast_in_dim.370.docs_ref
  3.3 88.5 %start.1 = (bf16[4,2,256,1536]{3,2,1,0:T(8,128)(2,1)}, bf16[4,2,256,1536]{3,2,1,0:T(8,128)(2,1)}, s32[4,2,8,256]{3,2,1,0:T(8,128)}, bf16[4,4,16,128]{3,2,1,0:T(8...) custom-call(bf16[256,1536]{1,0:T(8,128)(2,1)} %bitcast.198, ...), custom_call_target="tpu_custom_call" | custom-call | tf_op jit(solution)/shard_map/start/pallas_call | solution.py:510
  91.8 1.0 dynamic-slice_bitcast_fusion.1
  93.7 0.8 slice.169
  96.7 0.7 copy.61.mix_ref
  97.4 4.1 fusion
  101.5 1.4 fusion.66
  103.0 1.3 copy.56.dcol_ref
  104.3 0.6 pad.13
  104.9 4.4 fusion.2
  109.3 6.6 %convolution_convert_fusion.5 = bf16[2048,768]{1,0:T(8,128)(2,1)} fusion(bf16[2048,1536]{1,0:T(8,128)(2,1)S(1)} %bitcast.201, bf16[1536,768]{1,0:T(8,128)(2,1)S(1)} %bitcast.296), kind=kOutput, calls=%fused_computation.19 | convolution fusion | flops 4833411072 | bytes 11796480 | tf_op jit(solution)/shard_map/dot_general | solution.py:42
  116.1 0.1 broadcast_in_dim.452
  116.3 0.1 broadcast_in_dim.455
  117.1 6.9 %subtract_convert_fusion = (bf16[2,1536,256]{2,1,0:T(8,128)(2,1)}, bf16[2,1536,256]{2,1,0:T(8,128)(2,1)}) fusion(f32[2,1536]{1,0:T(2,128)S(1)} %bitcast.259, pred[1536,256]{1,0:T(8,128)(4,1)S(1)} %bitcast.224, f32[2,1536]{1,0:T(2,128)S(1)} %bitcast.257, pred[1536,256]{1,0:T(8,128)(4,1)S(1)} %bitcast.223, f32[2,1536]{1,0:T(2,128)S(1)} %bitcast.255, ...), kind=kLoop, calls=%fused_computation.39 | loop fusion | flops 19660800 | bytes 7606272 | tf_op jit(solution)/shard_map/convert_element_type | solution.py:47
  125.1 6.2 %fusion.13.tt_ref = bf16[2,1536,256]{2,1,0:T(8,128)(2,1)} fusion(f32[2,1536]{1,0:T(2,128)S(1)} %bitcast.260, f32[2,1536]{1,0:T(2,128)S(1)} %bitcast.258, f32[2,1536]{1,0:T(2,128)S(1)} %bitcast.256, f32[2,1536]{1,0:T(2,128)S(1)} %bitcast.254, f32[2,1536]{1,0:T(2,128)S(1)} %bitcast.252, f32[2,1536]{1,0:T(2,128)S(1)} %bitcast.250, f32[2,1536]{1,0:T(2,128)S(1)} %bitcast.248, ...), kind=kLoop, calls=%fused_computation.29 | loop fusion | flops 17301504 | bytes 6033408 | tf_op jit(solution)/shard_map/convert_element_type | solution.py:197
  131.4 20.7 %attend.1 = (bf16[8,256,256]{2,1,0:T(8,128)(2,1)}, f32[8,256,256]{2,1,0:T(8,128)}, f32[8,256,256]{2,1,0:T(8,128)}, f32[8,2,256,256]{3,2,1,0:T(8,128)}, bf16[8,2,256,256]{3,2,1,0:T(8,128)(2,1)}) custom-call(f32[2,2]{1,0:T(2,128)} %copy.61.mix_ref, bf16[8,256,768]{2,1,0:T(8,128)(2,1)} %bitcast.300, s32[8,256,1]{2,1,0:T(8,128)} %copy.56.dcol_ref, ...), custom_call_target="tpu_custom_call" | custom-call | flops 9663676416 | bytes 10485760 | tf_op jit(solution)/shard_map/attend/pallas_call | solution.py:91
  152.1 0.7 slice.159.g_ref
  152.8 0.7 slice.143.g_ref
  153.4 1.0 fusion.32
  154.5 4.5 convolution_convert_fusion.1
  159.0 84.1 %mid.1 = (f32[256,1536]{1,0:T(8,128)}, bf16[4,2,256,1536]{3,2,1,0:T(8,128)(2,1)}, bf16[4,4,96,1024]{3,2,1,0:T(8,128)(2,1)}, bf16[4,128,1536]{2,1,0:T(8,128)(2,1)}) custom-call(bf16[4,2,256,1536]{3,2,1,0:T(8,128)(2,1)} %bitcast.191, bf16[256,1536]{1,0:T(8,128)(2,1)} %bitcast.199, f32[1,1536]{1,0:T(1,128)} %slice.143.g_ref, ...), custom_call_target="tpu_custom_call" | custom-call | tf_op jit(solution)/shard_map/mid/pallas_call | solution.py:510
  243.1 11.9 %fusion.68 = f32[2048,1024]{0,1:T(8,128)} fusion(bf16[2048,1536]{1,0:T(8,128)(2,1)} %bitcast.290, bf16[1536,1024]{1,0:T(8,128)(2,1)} %bitcast.294), kind=kOutput, calls=%fused_computation.145 | convolution fusion | flops 6442450944 | bytes 17825792 | tf_op jit(solution)/shard_map/dot_general | solution.py:42
  255.1 9.1 %multiply_convert_fusion.2 = (bf16[2048,512]{0,1:T(8,128)(2,1)S(1)}, bf16[2048,512]{0,1:T(8,128)(2,1)S(1)}, bf16[2048,512]{0,1:T(8,128)(2,1)S(1)}) fusion(f32[2048,1024]{0,1:T(8,128)} %fusion.68, bf16[2048,1536]{1,0:T(8,128)(2,1)} %bitcast.286, bf16[512,1536]{1,0:T(8,128)(2,1)S(1)} %bitcast.298), kind=kOutput, calls=%fused_computation.15 | convolution fusion | flops 3236954112 | bytes 22544384 | tf_op jit(solution)/shard_map/dot_general | solution.py:42
  264.2 9.5 %convolution_convert_fusion.4 = bf16[1536,1024]{1,0:T(8,128)(2,1)} fusion(bf16[2048,1536]{1,0:T(8,128)(2,1)S(1)} %bitcast.293, bf16[2048,512]{0,1:T(8,128)(2,1)S(1)} %get-tuple-element.91, bf16[2048,512]{0,1:T(8,128)(2,1)S(1)} %get-tuple-element.90), kind=kOutput, calls=%fused_computation.18 | convolution fusion | flops 6452412416 | bytes 13631488 | tf_op jit(solution)/shard_map/dot_general | solution.py:42
  273.7 9.5 %convolution_convert_fusion.3 = bf16[2048,1536]{1,0:T(8,128)(2,1)} fusion(bf16[1536,1024]{1,0:T(8,128)(2,1)S(1)} %bitcast.295, bf16[2048,512]{0,1:T(8,128)(2,1)S(1)} %get-tuple-element.91, bf16[2048,512]{0,1:T(8,128)(2,1)S(1)} %get-tuple-element.90), kind=kOutput, calls=%fused_computation.8 | convolution fusion | flops 6453985280 | bytes 13631488 | tf_op jit(solution)/shard_map/dot_general | solution.py:42
  283.2 4.5 convolution_convert_fusion.6
  287.7 5.3 convolution_convert_fusion.2
  293.1 87.8 %mid_back.1 = (f32[256,1536]{1,0:T(8,128)}, bf16[4,2,256,1536]{3,2,1,0:T(8,128)(2,1)}, f32[8,1536]{1,0:T(8,128)}, bf16[384,1024]{1,0:T(8,128)(2,1)}, bf16[128,1536]{1,0:T(8,128)(2,1)}) custom-call(bf16[4,2,256,1536]{3,2,1,0:T(8,128)(2,1)} %bitcast.205, bf16[256,1536]{1,0:T(8,128)(2,1)} %bitcast.212, f32[256,1536]{1,0:T(8,128)} %get-tuple-element.55.r_ref.resid_ref, ...), custom_call_target="tpu_custom_call" | custom-call | tf_op jit(solution)/shard_map/mid_back/pallas_call | solution.py:510
  380.9 5.9 %fusion.69.dn_ref = f32[8,256,256]{2,1,0:T(8,128)} fusion(bf16[8,256,1536]{2,1,0:T(8,128)(2,1)} %bitcast.192, bf16[256,1536,1]{1,0,2:T(8,128)(2,1)S(1)} %bitcast.209), kind=kOutput, calls=%fused_computation.146 | convolution fusion | flops 1610612736 | bytes 9175040 | tf_op jit(solution)/shard_map/dot_general | solution.py:42
  386.8 21.6 %attend_back.1 = (bf16[8,256,768]{2,1,0:T(8,128)(2,1)}, f32[2,6,8,128]{3,2,1,0:T(8,128)}, f32[8,256]{1,0:T(8,128)}, f32[8,256]{1,0:T(8,128)}) custom-call(f32[2,2]{1,0:T(2,128)} %copy.61.mix_ref, bf16[8,256,768]{2,1,0:T(8,128)(2,1)} %bitcast.301, s32[8,256,1]{2,1,0:T(8,128)} %copy.56.dcol_ref, s32[8,1,256]{2,1,0:T(1,128)} %get-tuple-element.105.drow_ref, ...), custom_call_target="tpu_custom_call" | custom-call | flops 6442450944 | bytes 10485760 | tf_op jit(solution)/shard_map/attend_back/pallas_call | solution.py:169
  408.5 9.5 %multiply_reduce_fusion = (f32[1536]{0:T(1024)S(1)}, bf16[1536,768]{1,0:T(8,128)(2,1)}) fusion(bf16[4,4,96,768]{3,2,1,0:T(8,128)(2,1)S(1)} %copy-done.17, bf16[2048,1536]{1,0:T(8,128)(2,1)} %bitcast.202, bf16[2048,768]{1,0:T(8,128)(2,1)} %bitcast.302), kind=kOutput, calls=%fused_computation.9 | convolution fusion | flops 4836555264 | bytes 14161920 | tf_op jit(solution)/shard_map/dot_general | solution.py:42
  418.1 7.3 %convolution_convert_fusion = bf16[2048,1536]{1,0:T(8,128)(2,1)} fusion(bf16[2048,768]{1,0:T(8,128)(2,1)S(1)} %bitcast.303, bf16[1536,768]{1,0:T(8,128)(2,1)S(1)} %bitcast.297), kind=kOutput, calls=%fused_computation.5 | convolution fusion | flops 4834983936 | bytes 11796480 | tf_op jit(solution)/shard_map/dot_general | solution.py:42
  425.3 0.7 collective-permute-start.4
  426.2 1.8 convolution_convert_fusion.7
  428.0 0.2 add_bitcast_fusion
  428.3 0.8 fusion.27
  429.1 0.3 collective-permute-start.2
  429.4 0.1 slice_reduce_fusion.1
  429.5 0.2 reshape.346
  429.7 0.7 slice.148
  430.7 0.9 slice.176.wo_ref
  431.5 0.8 slice_reduce_fusion
  432.4 0.7 concatenate.7
  433.1 91.2 %end.1 = (bf16[256,1536]{1,0:T(8,128)(2,1)}, f32[256,1536]{1,0:T(8,128)}, f32[96,4608]{1,0:T(8,128)}, f32[96,1536]{1,0:T(8,128)}, f32[48,128]{1,0:T(8,128)}) custom-call(bf16[4,2,256,1536]{3,2,1,0:T(8,128)(2,1)} %bitcast.204, bf16[4,2,256,1536]{3,2,1,0:T(8,128)(2,1)} %bitcast.203, bf16[4,384,768]{2,1,0:T(8,128)(2,1)} %bitcast.214, ...), custom_call_target="tpu_custom_call" | custom-call | tf_op jit(solution)/shard_map/end/pallas_call | solution.py:510
  524.2 1.4 slice_bitcast_fusion
  525.6 2.3 slice.165
  527.9 0.6 copy.60
  528.6 0.7 slice.177
  529.3 0.2 reshape.350
  529.4 0.8 copy.59
  530.2 1.3 dynamic_slice.44
  531.5 1.3 dynamic_slice.45
  532.7 1.3 dynamic_slice.46
  534.2 0.2 collective-permute-start.3
  534.5 1.4 bitcast_convert_fusion
  535.9 17.7 %collective-permute-done.3 = bf16[2,2,96,1024]{3,2,1,0:T(8,128)(2,1)S(1)} collective-permute-done((bf16[2,2,96,1024]{3,2,1,0:T(8,128)(2,1)S(1)}, bf16[2,2,96,1024]{3,2,1,0:T(8,128)(2,1)S(1)}, u32[]{:S(2)}, u32[]{:S(2)}) %collective-permute-start.3) | collective-permute-done | bytes 786464 | tf_op jit(solution)/shard_map/ppermute | solution.py:890
  553.5 0.1 select_bitcast_fusion.1
  553.7 0.1 pad_maximum_fusion.3.p_ref
  553.8 2.0 place_gu.1
  555.9 0.9 copy.83
  556.8 1.1 copy.84
  557.9 1.2 copy.85
  559.1 0.8 copy.86
  (162 shorter events, 5.9 us)
Async XLA Ops:
  0.6 96.0 %copy-start = (f32[16,2]{0,1:T(2,128)S(1)}, f32[16,2]{0,1:T(2,128)}, u32[]{:S(2)}) copy-start(f32[16,2]{0,1:T(2,128)} %param.20) | copy-start | bytes 388
  3.3 91.3 %copy-start.13 = (f32[16,6,11]{0,1,2:T(8,128)S(1)}, f32[16,6,11]{0,1,2:T(8,128)}, u32[]{:S(2)}) copy-start(f32[16,6,11]{0,1,2:T(8,128)} %param.19) | copy-start | bytes 12676
  92.8 60.7 %collective-permute-start = (bf16[96,1536]{1,0:T(8,128)(2,1)S(1)}, bf16[96,1536]{1,0:T(8,128)(2,1)S(1)}, u32[]{:S(2)}, u32[]{:S(2)}) collective-permute-start(bf16[96,1536]{1,0:T(8,128)(2,1)S(1)} %dynamic-slice_bitcast_fusion.1), channel_id=1, source_target_pairs={{0,1},{1,0},{2,3},{3,2},{4,5},{5,4},{6,7},{7,6},{8,9},{9,8},{10,11... | collective-permute-start | bytes 884744 | tf_op jit(solution)/shard_map/ppermute | solution.py:892
  97.4 7.5 %copy-start.10 = (f32[1536]{0:T(1024)}, f32[1536]{0:T(1024)S(1)}, u32[]{:S(2)}) copy-start(f32[1536]{0:T(1024)S(1)} %mul.75) | copy-start | bytes 18436
  104.9 4.4 copy-start.16
  109.3 6.6 %copy-start.3 = (bf16[4,2,256,1536]{3,2,1,0:T(8,128)(2,1)}, bf16[4,2,256,1536]{3,2,1,0:T(8,128)(2,1)S(1)}, u32[]{:S(2)}) copy-start(bf16[4,2,256,1536]{3,2,1,0:T(8,128)(2,1)S(1)} %fusion.2) | copy-start | bytes 18874372
  152.1 2.5 copy-start.2
  243.1 12.0 %copy-start.19 = (bf16[4,128,1536]{2,1,0:T(8,128)(2,1)S(1)}, bf16[4,128,1536]{2,1,0:T(8,128)(2,1)}, u32[]{:S(2)}) copy-start(bf16[4,128,1536]{2,1,0:T(8,128)(2,1)} %get-tuple-element.52) | copy-start | bytes 4718596
  243.1 21.0 %slice-start.4 = ((s8[6291456]{0:T(1024)(128)(4,1)}), s8[4194304]{0:T(1024)(128)(4,1)S(1)}, s32[]{:S(2)}) async-start(s8[6291456]{0:T(1024)(128)(4,1)} %bitcast.291), calls=%async_computation.4 | async-start | bytes 8388608
  255.1 9.1 %slice-start.5 = ((s8[6291456]{0:T(1024)(128)(4,1)}), s8[2097152]{0:T(1024)(128)(4,1)S(1)}, s32[]{:S(2)}) async-start(s8[6291456]{0:T(1024)(128)(4,1)} %bitcast.291), calls=%async_computation.5 | async-start | bytes 4194304
  255.1 28.1 %slice-start.2 = ((s8[6291456]{0:T(1024)(128)(4,1)}), s8[4194304]{0:T(1024)(128)(4,1)S(1)}, s32[]{:S(2)}) async-start(s8[6291456]{0:T(1024)(128)(4,1)} %bitcast.287), calls=%async_computation.2 | async-start | bytes 8388608
  264.2 9.5 %copy-start.15 = (bf16[4,4,96,1024]{3,2,1,0:T(8,128)(2,1)S(1)}, bf16[4,4,96,1024]{3,2,1,0:T(8,128)(2,1)}, u32[]{:S(2)}) copy-start(bf16[4,4,96,1024]{3,2,1,0:T(8,128)(2,1)} %get-tuple-element.54) | copy-start | bytes 9437188
  264.2 19.0 %slice-start.3 = ((s8[6291456]{0:T(1024)(128)(4,1)}), s8[2097152]{0:T(1024)(128)(4,1)S(1)}, s32[]{:S(2)}) async-start(s8[6291456]{0:T(1024)(128)(4,1)} %bitcast.287), calls=%async_computation.3 | async-start | bytes 4194304
  386.8 21.6 %copy-start.17 = (bf16[4,4,96,768]{3,2,1,0:T(8,128)(2,1)S(1)}, bf16[4,4,96,768]{3,2,1,0:T(8,128)(2,1)}, u32[]{:S(2)}) copy-start(bf16[4,4,96,768]{3,2,1,0:T(8,128)(2,1)} %get-tuple-element.46) | copy-start | bytes 7077892
  408.4 9.6 %copy-start.18 = (bf16[4,4,96,768]{3,2,1,0:T(8,128)(2,1)S(1)}, bf16[4,4,96,768]{3,2,1,0:T(8,128)(2,1)}, u32[]{:S(2)}) copy-start(bf16[4,4,96,768]{3,2,1,0:T(8,128)(2,1)} %get-tuple-element.46) | copy-start | bytes 7077892
  408.5 9.6 %copy-start.20 = (bf16[8,256,768]{2,1,0:T(8,128)(2,1)S(1)}, bf16[8,256,768]{2,1,0:T(8,128)(2,1)}, u32[]{:S(2)}) copy-start(bf16[8,256,768]{2,1,0:T(8,128)(2,1)} %get-tuple-element.61) | copy-start | bytes 9437188
  408.5 17.7 %slice-start = ((s8[6291456]{0:T(1024)(128)(4,1)}), s8[4194304]{0:T(1024)(128)(4,1)S(1)}, s32[]{:S(2)}) async-start(s8[6291456]{0:T(1024)(128)(4,1)} %bitcast.193), calls=%async_computation | async-start | bytes 8388608
  418.0 7.3 %copy-start.9 = (bf16[128,1536]{1,0:T(8,128)(2,1)S(1)}, bf16[128,1536]{1,0:T(8,128)(2,1)}, u32[]{:S(2)}) copy-start(bf16[128,1536]{1,0:T(8,128)(2,1)} %get-tuple-element.75) | copy-start | bytes 1179652
  418.0 8.0 %copy-start.7 = (bf16[384,1024]{1,0:T(8,128)(2,1)S(1)}, bf16[384,1024]{1,0:T(8,128)(2,1)}, u32[]{:S(2)}) copy-start(bf16[384,1024]{1,0:T(8,128)(2,1)} %get-tuple-element.72) | copy-start | bytes 2359300
  418.0 8.1 %slice-start.1 = ((s8[6291456]{0:T(1024)(128)(4,1)}), s8[2097152]{0:T(1024)(128)(4,1)S(1)}, s32[]{:S(2)}) async-start(s8[6291456]{0:T(1024)(128)(4,1)} %bitcast.193), calls=%async_computation.1 | async-start | bytes 4194304
  425.3 109.0 %collective-permute-start.4 = (bf16[128,1536]{1,0:T(8,128)(2,1)S(1)}, bf16[128,1536]{1,0:T(8,128)(2,1)S(1)}, u32[]{:S(2)}, u32[]{:S(2)}) collective-permute-start(bf16[128,1536]{1,0:T(8,128)(2,1)S(1)} %copy-done.9), channel_id=1, source_target_pairs={{0,16},{16,0},{1,17},{17,1},{2,18},{18,2},{3,19},{19,3},{4,20},{20... | collective-permute-start | bytes 1179656 | tf_op jit(solution)/shard_map/ppermute | solution.py:890
  426.1 2.1 collective-permute-start.1
  426.2 1.8 copy-start.12
  426.2 3.2 copy-start.14
  426.2 3.3 copy-start.11
  429.1 104.9 %collective-permute-start.2 = (bf16[2,96,1024]{2,1,0:T(8,128)(2,1)}, bf16[2,96,1024]{2,1,0:T(8,128)(2,1)S(1)}, u32[]{:S(2)}, u32[]{:S(2)}) collective-permute-start(bf16[2,96,1024]{2,1,0:T(8,128)(2,1)} %fusion.27), channel_id=1, source_target_pairs={{0,2},{1,3},{2,0},{3,1},{4,6},{5,7},{6,4},{7,5},{8,10},{9,11},{10,... | collective-permute-start | bytes 1179656 | tf_op jit(solution)/shard_map/ppermute | solution.py:892
  534.2 19.4 %collective-permute-start.3 = (bf16[2,2,96,1024]{3,2,1,0:T(8,128)(2,1)S(1)}, bf16[2,2,96,1024]{3,2,1,0:T(8,128)(2,1)S(1)}, u32[]{:S(2)}, u32[]{:S(2)}) collective-permute-start(bf16[2,2,96,1024]{3,2,1,0:T(8,128)(2,1)S(1)} %pad_maximum_fusion.4), channel_id=1, source_target_pairs={{0,16},{16,0},{1,17},{17,1},{2,18},{18,2},{3,19},{19,3},{4,20},{20... | collective-permute-start | bytes 2359304 | tf_op jit(solution)/shard_map/ppermute | solution.py:890
  553.6 2.2 copy-start.6
  553.7 3.1 copy-start.5
  553.8 4.1 copy-start.4
  556.8 2.4 copy-start.8
  556.8 3.2 copy-start.1

commit v3 on v2

--- a/solution.py
+++ b/solution.py
@@ -394,7 +394,7 @@
 LINE_COPIES = 6
 
 
-def gather_rows(net, v, out, sems, base, ready, poll):
+def gather_steps(net, v, out, sems, base, ready):
     n = v.shape[0]
     A, B = pl.ds(0, n // 2), pl.ds(n // 2, n // 2)
     go = {}
@@ -406,40 +406,57 @@
     go["yB"] = net.send(v.at[B], out.at[2, 0, B], sems, base + 2, "y")
     go["xB"] = net.send(v.at[B], out.at[1, 0, B], sems, base + 1, "x")
     go["0B"] = net.send(v.at[B], out.at[0, 1, B], sems, base + 5, "c")
-    poll()
+    yield
     go["xA"].wait_recv()
     go["dA"] = net.send(out.at[1, 0, A], out.at[3, 0, A], sems, base + 6, "y")
     go["1A"] = net.send(out.at[1, 0, A], out.at[1, 1, A], sems, base + 8, "c")
     go["yA"].wait_recv()
     go["2A"] = net.send(out.at[2, 0, A], out.at[2, 1, A], sems, base + 10, "c")
-    poll()
+    yield
     go["yB"].wait_recv()
     go["dB"] = net.send(out.at[2, 0, B], out.at[3, 0, B], sems, base + 7, "x")
     go["2B"] = net.send(out.at[2, 0, B], out.at[2, 1, B], sems, base + 9, "c")
     go["xB"].wait_recv()
     go["1B"] = net.send(out.at[1, 0, B], out.at[1, 1, B], sems, base + 11, "c")
-    poll()
+    yield
     go["dA"].wait_recv()
     go["3A"] = net.send(out.at[3, 0, A], out.at[3, 1, A], sems, base + 12, "c")
     go["dB"].wait_recv()
     go["3B"] = net.send(out.at[3, 0, B], out.at[3, 1, B], sems, base + 13, "c")
-    poll()
+    yield
     for name in ("0A", "0B", "1A", "2B", "2A", "1B", "3A", "3B"):
         go[name].wait_recv()
     for copy in go.values():
         copy.wait_send()
 
 
+def gather_rows(net, v, out, sems, base, ready, poll):
+    for _ in gather_steps(net, v, out, sems, base, ready):
+        poll()
+
+
 GATHER_COPIES = 14
 SCATTER_COPIES = 10
 
 
-def scatter_rows(net, parts, rc, rd, rx, ry, td, tx, ty, sems, base, poll):
+class Later:
+    def __init__(self, make):
+        self.make = make
+        make().start()
+
+    def wait_recv(self):
+        self.make().wait_recv()
+
+    def wait_send(self):
+        self.make().wait_send()
+
+
+def scatter_steps(net, parts, rc, rd, rx, ry, td, tx, ty, sems, base):
     n = parts.shape[2]
     A, B = pl.ds(0, n // 2), pl.ds(n // 2, n // 2)
     go = {}
     for i, chip in enumerate((3, 1, 2, 0)):
-        go[chip] = net.send(parts.at[chip, 1], rc.at[chip], sems, base + i, "c")
+        go[chip] = Later(lambda i=i, chip=chip: net.copy(parts.at[chip, 1], rc.at[chip], sems, base + i, "c"))
 
     def add(dst, chip, start, more=None):
         def body(rows):
@@ -450,24 +467,25 @@
 
         tiles(start, n // 2, body)
 
+    yield None
     go[3].wait_recv()
     add(td, 3, 0)
-    go["dA"] = net.send(td.at[A], rd.at[A], sems, base + 4, "x")
+    go["dA"] = Later(lambda: net.copy(td.at[A], rd.at[A], sems, base + 4, "x"))
     add(td, 3, n // 2)
-    go["dB"] = net.send(td.at[B], rd.at[B], sems, base + 5, "y")
+    go["dB"] = Later(lambda: net.copy(td.at[B], rd.at[B], sems, base + 5, "y"))
     go[1].wait_recv()
     add(tx, 1, 0)
-    go["xA"] = net.send(tx.at[A], rx.at[A], sems, base + 6, "x")
+    go["xA"] = Later(lambda: net.copy(tx.at[A], rx.at[A], sems, base + 6, "x"))
     go[2].wait_recv()
     add(ty, 2, n // 2)
-    go["yB"] = net.send(ty.at[B], ry.at[B], sems, base + 7, "y")
-    poll()
+    go["yB"] = Later(lambda: net.copy(ty.at[B], ry.at[B], sems, base + 7, "y"))
+    yield None
     go["dA"].wait_recv()
     add(ty, 2, 0, rd)
-    go["yA"] = net.send(ty.at[A], ry.at[A], sems, base + 8, "y")
+    go["yA"] = Later(lambda: net.copy(ty.at[A], ry.at[A], sems, base + 8, "y"))
     go["dB"].wait_recv()
     add(tx, 1, n // 2, rd)
-    go["xB"] = net.send(tx.at[B], rx.at[B], sems, base + 9, "x")
+    go["xB"] = Later(lambda: net.copy(tx.at[B], rx.at[B], sems, base + 9, "x"))
     go[0].wait_recv()
 
     def done(half):
@@ -477,7 +495,15 @@
             for copy in go.values():
                 copy.wait_send()
 
-    return done
+    yield done
+
+
+def scatter_rows(net, parts, rc, rd, rx, ry, td, tx, ty, sems, base, poll):
+    steps = scatter_steps(net, parts, rc, rd, rx, ry, td, tx, ty, sems, base)
+    next(steps)
+    next(steps)
+    poll()
+    return next(steps)
 
 
 def scatter_scratch(n, w):
@@ -526,12 +552,13 @@
 PLACES = {"c": (0, 1), "x": (1, 0), "xc": (1, 1), "y": (2, 0), "yc": (2, 1), "xy": (3, 0), "xyc": (3, 1)}
 
 
-def start_call(x, dy, docs, gains, w_qkv, w_gate, w_up, w_out, ident):
+def start_call(x, dy, docs, gains, taps, w_qkv, w_gate, w_up, w_out, ident):
     n, w = x.shape
     rows = w_qkv.shape[0]
 
-    def body(x_ref, dy_ref, docs_ref, g_ref, wq_ref, gate_ref, up_ref, wo_ref,
-             xs_ref, dys_ref, docs_out, gains_out, qkv_out, gu_out, wo_out, slots, gus, local, send, recv):
+    def body(x_ref, dy_ref, docs_ref, g_ref, taps_ref, wq_ref, gate_ref, up_ref, wo_ref,
+             a1_ref, dys_ref, docs_out, gains_ref, qkv_out, gu_out, wo_out, th_ref, tl_ref, tt_ref,
+             xs, gains_out, slots, gus, local, send, recv):
         net = Net()
         sems = (send, recv)
         base = 2 * GATHER_COPIES
@@ -539,6 +566,7 @@
         line_o = GatherLine(net, wo_ref, wo_out, sems, base + 6, lambda slot: slot // 2 == net.x)
         line_g = GatherLine(net, gains_out.at[net.z], gains_out, sems, base + 12)
         base += 18
+        gains_out[net.z, net.k] = g_ref[...]
         slots[...] = jnp.zeros_like(slots)
         for half in range(2):
 
@@ -556,69 +584,109 @@
 
         net.greet(PLANE)
         own = [
-            pltpu.make_async_copy(x_ref, xs_ref.at[0, 0], local.at[0]),
+            pltpu.make_async_copy(slots.at[net.k], qkv_out.at[net.z, net.k], local.at[0]),
             pltpu.make_async_copy(dy_ref, dys_ref.at[0, 0], local.at[1]),
-            pltpu.make_async_copy(slots.at[net.k], qkv_out.at[net.z, net.k], local.at[2]),
-            pltpu.make_async_copy(gus.at[net.k], gu_out.at[net.k], local.at[3]),
-            pltpu.make_async_copy(g_ref, gains_out.at[net.z, net.k], local.at[4]),
-            pltpu.make_async_copy(docs_ref, docs_out.at[0, 0], local.at[5]),
-            pltpu.make_async_copy(wo_ref, wo_out.at[net.z], local.at[6]),
+            pltpu.make_async_copy(gus.at[net.k], gu_out.at[net.k], local.at[2]),
+            pltpu.make_async_copy(docs_ref, docs_out.at[0, 0], local.at[3]),
+            pltpu.make_async_copy(wo_ref, wo_out.at[net.z], local.at[4]),
         ]
         for copy in own:
             copy.start()
-        shares, small = [], []
+        qkv_parts, gain_parts, small = [], [], []
         flips = {"c": net.k + 1 - 2 * net.c, "y": net.k + 2 - 4 * net.y, "yc": net.k + 1 - 2 * net.c + 2 - 4 * net.y}
         for j, name in enumerate(("y", "yc", "c")):
-            other = flips[name]
-            shares.append(net.send(slots.at[other], qkv_out.at[net.z, net.k], sems, base + j, name))
-            small.append(net.send(g_ref, gains_out.at[net.z, net.k], sems, base + 6 + j, name))
+            gain_parts.append(net.send(g_ref, gains_out.at[net.z, net.k], sems, base + 6 + j, name))
+            qkv_parts.append(net.send(slots.at[flips[name]], qkv_out.at[net.z, net.k], sems, base + j, name))
+        line_o.step(0)
         for j, (name, (chip, core)) in enumerate(PLACES.items()):
             small.append(net.send(docs_ref, docs_out.at[chip, core], sems, base + 9 + j, name))
-
-        def rest():
-            for j, name in enumerate(("y", "yc", "c")):
-                small.append(net.send(gus.at[flips[name]], gu_out.at[net.k], sems, base + 3 + j, name))
-
-        def line0():
-            own[2].wait()
-            own[4].wait()
-            for copy in shares:
-                copy.wait_recv()
-            for copy in small[:3]:
-                copy.wait_recv()
-            line_q.step(0)
-            line_g.step(0)
-            line_o.step(0)
-
-        def both(d):
-            def act():
-                line_q.step(d)
-                line_g.step(d)
-
-            return act
-
-        first, _ = polls(line0, both(1))
-        gather_rows(net, x_ref, xs_ref, sems, 0, lambda half: None, first)
-        rest()
-        second, drain = polls(both(2), lambda: line_o.step(1), both(3), lambda: line_o.step(2))
-        gather_rows(net, dy_ref, dys_ref, sems, GATHER_COPIES, lambda half: None, second)
-        drain()
+        gather_x = gather_steps(net, x_ref, xs, sems, 0, lambda half: None)
+        next(gather_x)
+        gather_dy = gather_steps(net, dy_ref, dys_ref, sems, GATHER_COPIES, lambda half: None)
+        next(gather_dy)
+        for copy in gain_parts:
+            copy.wait_recv()
+        line_g.step(0)
+        own[0].wait()
+        for copy in qkv_parts:
+            copy.wait_recv()
+        line_q.step(0)
+        line_g.step(1)
+
+        diff = lax.broadcasted_iota(jnp.int32, (n, n), 1) - lax.broadcasted_iota(jnp.int32, (n, n), 0)
+
+        def bands_of(first, count):
+            def one(i, _):
+                band = jnp.zeros((n, n), f32)
+                back = jnp.zeros((n, n), f32)
+                for b in range(KWIN):
+                    tap = taps_ref[(first + i) * KWIN + b]
+                    band = jnp.where(diff == b, tap, band)
+                    back = jnp.where(diff == -b, tap, back)
+                h, a = (first + i) // QWIN, (first + i) % QWIN
+                at = pl.ds(pl.multiple_of(a * n, n), n)
+                th_ref[h, at], tl_ref[h, at] = split(band)
+                tt_ref[h, at] = back.astype(bf16)
+                return 0
+
+            lax.fori_loop(0, count, one, 0)
+
+        bands_of(0, QWIN)
+        line_g.step(2)
+        next(gather_x)
+        line_q.step(1)
+        line_g.step(3)
+        line_o.step(1)
+        for i in range(16):
+            gains_ref[:, i * rows : (i + 1) * rows] = wide(gains_out[i // 4, i % 4, 0:8, 0:rows])
+        bands_of(QWIN, QWIN)
+        next(gather_x)
+        next(gather_dy)
+        for j, name in enumerate(("y", "yc", "c")):
+            small.append(net.send(gus.at[flips[name]], gu_out.at[net.k], sems, base + 3 + j, name))
+        next(gather_dy)
+        gain = gains_ref[0:1]
+
+        def norm(chip, core, src):
+            def body(at):
+                xf = wide(src[at])
+                r = lax.rsqrt(jnp.mean(xf * xf, axis=1, keepdims=True) + 1e-06)
+                a1_ref[chip, core, at] = (xf * r * gain).astype(bf16)
+
+            tiles(0, n, body)
+
+        norm(0, 0, x_ref)
+        line_q.step(2)
+        line_o.step(2)
+        for _ in gather_x:
+            pass
+        next(gather_dy)
+        for chip in range(4):
+            for core in range(2):
+                if (chip, core) != (0, 0):
+                    norm(chip, core, xs.at[chip, core])
+        line_q.step(3)
         line_o.step(3)
+        for _ in gather_dy:
+            pass
         for line in (line_q, line_g, line_o):
             line.finish()
-        for copy in own[:2] + [own[3]] + own[5:]:
+        for copy in own[1:]:
             copy.wait()
-        for copy in small[3:]:
+        for copy in small:
             copy.wait_recv()
-        for copy in shares + small:
+        for copy in qkv_parts + gain_parts + small:
             copy.wait_send()
 
     return comm_call(
-        body, "start", ident, (x, dy, docs, gains, w_qkv, w_gate, w_up, w_out), [VM] * 7 + [ANY],
-        [shape((4, 2, n, w), bf16), shape((4, 2, n, w), bf16), shape((4, 2) + docs.shape, docs.dtype), shape((4, 4) + gains.shape, bf16),
-         shape((4, 4, rows, 6 * EP), bf16), shape((4, rows, FF // 4), bf16), shape((4, rows, MODEL_WIDTH), bf16)],
-        [ANY] * 7,
-        [pltpu.VMEM((4, rows, 6 * EP), bf16), pltpu.VMEM((4, rows, FF // 4), bf16), pltpu.SemaphoreType.DMA((7,))]
+        body, "start", ident, (x, dy, docs, gains, taps, w_qkv, w_gate, w_up, w_out),
+        [VM] * 4 + [pl.BlockSpec(memory_space=pltpu.SMEM)] + [VM] * 4,
+        [shape((4, 2, n, w), bf16), shape((4, 2, n, w), bf16), shape((4, 2) + docs.shape, docs.dtype), shape((8, w), f32),
+         shape((4, 4, rows, 6 * EP), bf16), shape((4, rows, FF // 4), bf16), shape((4, rows, MODEL_WIDTH), bf16)]
+        + [shape((2, QWIN * n, n), bf16)] * 3,
+        [VM, ANY, ANY, VM, ANY, ANY, ANY, VM, VM, VM],
+        [pltpu.VMEM((4, 2, n, w), bf16), pltpu.VMEM((4, 4) + gains.shape, bf16),
+         pltpu.VMEM((4, rows, 6 * EP), bf16), pltpu.VMEM((4, rows, FF // 4), bf16), pltpu.SemaphoreType.DMA((5,))]
         + dma_sems(2 * GATHER_COPIES + 18 + 16),
     )
 
@@ -668,29 +736,25 @@
         last.wait()
 
     return comm_call(
-        body, "mid", ident, (parts, x, gain, gu, w_down), [VM] * 3 + [ANY] * 2,
+        body, "mid", ident, (parts, x, gain, gu, w_down), [VM] * 5,
         [shape((n, w), f32), shape((4, 2, n, w), bf16), shape((4,) + gu.shape, bf16), shape((4, down, w), bf16)], [VM, ANY, ANY, ANY],
         [pltpu.VMEM((n, w), bf16), pltpu.SemaphoreType.DMA((3,))] + scatter_scratch(n, w)
         + dma_sems(SCATTER_COPIES + GATHER_COPIES + 2 * LINE_COPIES),
     )
 
 
-def mid_back_call(parts, dy, resid, gain, gu, down, ident):
+def mid_back_call(parts, dy, resid, gain, down, ident):
     n, w = parts.shape[2:]
 
-    def body(p_ref, dy_ref, r_ref, g_ref, gu_ref, down_ref, dresid_ref, out_ref, sum_ref, gu_out, down_out,
-             v, local, rc, rd, rx, ry, td, tx, ty, g_got, g_made, d_got, d_made, send, recv):
+    def body(p_ref, dy_ref, r_ref, g_ref, down_ref, dresid_ref, out_ref, sum_ref, down_out,
+             v, local, rc, rd, rx, ry, td, tx, ty, d_got, d_made, send, recv):
         net = Net()
         sems = (send, recv)
         net.greet("xyc")
         base = SCATTER_COPIES + GATHER_COPIES
-        line_g = ScatterLine(net, gu_ref, g_got, g_made, sems, base)
-        line_d = ScatterLine(net, down_ref, d_got, d_made, sems, base + LINE_COPIES)
-        lines = (line_g, line_d)
-        for line in lines:
-            line.step(0)
-        acts = [lambda d=d, line=line: line.step(d) for d in (1, 2) for line in lines]
-        poll, drain = polls(acts[0], acts[1], lambda: None, acts[2], acts[3])
+        line_d = ScatterLine(net, down_ref, d_got, d_made, sems, base)
+        line_d.step(0)
+        poll, drain = polls(lambda: line_d.step(1), lambda: None, lambda: line_d.step(2))
         sum_ref[...] = jnp.zeros_like(sum_ref)
         done = scatter_rows(net, p_ref, rc, rd, rx, ry, td, tx, ty, sems, 0, poll)
         poll()
@@ -722,33 +786,32 @@
 
             return store
 
-        line_g.finish(put(gu_out))
         line_d.finish(put(down_out))
         last.wait()
 
     return comm_call(
-        body, "mid_back", ident, (parts, dy, resid, gain, gu, down), [VM] * 6,
-        [shape((n, w), f32), shape((4, 2, n, w), bf16), shape((8, w), f32), shape(gu.shape[1:], bf16), shape(down.shape[1:], bf16)],
-        [VM, ANY, VM, VM, VM],
-        [pltpu.VMEM((n, w), bf16), pltpu.SemaphoreType.DMA] + scatter_scratch(n, w) + line_scratch(*gu.shape[1:]) + line_scratch(*down.shape[1:])
-        + dma_sems(SCATTER_COPIES + GATHER_COPIES + 2 * LINE_COPIES),
+        body, "mid_back", ident, (parts, dy, resid, gain, down), [VM] * 5,
+        [shape((n, w), f32), shape((4, 2, n, w), bf16), shape((8, w), f32), shape(down.shape[1:], bf16)],
+        [VM, ANY, VM, VM],
+        [pltpu.VMEM((n, w), bf16), pltpu.SemaphoreType.DMA] + scatter_scratch(n, w) + line_scratch(*down.shape[1:])
+        + dma_sems(SCATTER_COPIES + GATHER_COPIES + LINE_COPIES),
     )
 
 
-def end_call(da_parts, out_parts, qkv, wo, small, x, resid, dresid, gain, ident):
+def end_call(da_parts, qkv, wo, gu, down, small, x, dresid, gain, ident):
     n, w = da_parts.shape[2:]
     rows_q = qkv.shape[1] // 4
     rows_o = wo.shape[1]
 
-    def body(da_ref, op_ref, q_ref, wo_ref, small_ref, x_ref, resid_ref, dresid_ref, g_ref,
-             out_ref, gx_ref, gq_ref, go_ref, total_ref,
-             rc, rd, rx, ry, td, tx, ty, rc2, rd2, rx2, ry2, td2, tx2, ty2,
-             q_got, q_made, o_got, o_made, zq, cq, fq, po, ro, s_got, s_sum, s_line, send, recv):
+    def body(da_ref, q_ref, wo_ref, zg, down_ref, small_ref, x_ref, dresid_ref, g_ref,
+             gx_ref, gq_ref, go_ref, gate_ref, up_ref, gd_ref, total_ref,
+             rc, rd, rx, ry, td, tx, ty,
+             q_got, q_made, o_got, o_made, zq, cq, fq, cg, fg, fd, po, ro, s_got, s_sum, s_line, send, recv):
         net = Net()
         sems = (send, recv)
         net.greet("xyc")
         z, x, y, c = net.z, net.x, net.y, net.c
-        base = 2 * SCATTER_COPIES
+        base = SCATTER_COPIES
         line_q = ScatterLine(net, q_ref, q_got, q_made, sems, base)
         line_o = ScatterLine(net, po, o_got, o_made, sems, base + 6)
         line_s = GatherLine(net, s_sum.at[2], s_line, sems, base + 12)
@@ -760,6 +823,11 @@
         po[2 * (1 - x)] = jnp.zeros((rows_o, w), bf16)
         po[2 * (1 - x) + 1] = jnp.zeros((rows_o, w), bf16)
         po[2 * x + c] = wo_ref[c]
+        block = lambda i, j: pl.ds(pl.multiple_of((2 * i + j) * rows_q, rows_q), rows_q)
+        gu_swaps = [net.send(zg.at[block(i, 1 - c)], cg.at[i, c], sems, base + 9 + i, "c") for i in range(2)]
+        for i in range(2):
+            cg[i, c] = zg[block(i, c)]
+        fd[x] = down_ref[...]
 
         def small_step(i):
             hops[i].wait_recv()
@@ -779,15 +847,18 @@
         line_q.step(1)
         small_step(1)
         line_o.step(1)
-
-        def later():
-            line_q.step(2)
-            small_step(2)
-
-        poll, _ = polls(later)
-        done2 = scatter_rows(net, op_ref, rc2, rd2, rx2, ry2, td2, tx2, ty2, sems, SCATTER_COPIES, poll)
+        down_swap = net.send(down_ref, fd.at[x], sems, base + 13, "x")
+        for copy in gu_swaps:
+            copy.wait_recv()
+        gu_swaps.append(net.send(cg.at[1 - y], fg.at[x, y], sems, base + 11, "y"))
+        fg[x, y] = cg[y]
+
+        line_q.step(2)
+        small_step(2)
         line_o.step(2)
         line_s.step(1)
+        gu_swaps[2].wait_recv()
+        gu_swaps.append(net.send(fg.at[x], fg.at[x], sems, base + 12, "x"))
         for half in range(2):
             done(half)
 
@@ -807,7 +878,6 @@
             ro[0, rows] = total.astype(bf16)
 
         line_q.finish(put_q)
-        block = lambda i, j: pl.ds(pl.multiple_of((2 * i + j) * rows_q, rows_q), rows_q)
         swaps = [net.send(zq.at[block(i, 1 - c)], cq.at[i, c], sems, base + 4 + i, "c") for i in range(2)]
         for i in range(2):
             cq[i, c] = zq[block(i, c)]
@@ -823,14 +893,16 @@
         line_s.step(3)
         s_line[z] = s_sum[2]
         total_ref[...] = (s_line[0] + s_line[1]) + (s_line[2] + s_line[3])
-        for half in range(2):
-            done2(half)
-
-            def sum_of(rows):
-                total = wide(op_ref[0, 0, rows]) + wide(rc2[0, rows]) + wide(rx2[rows]) + wide(ry2[rows])
-                out_ref[rows] = (resid_ref[rows] + total).astype(bf16)
-
-            tiles(half * (n // 2), n // 2, sum_of)
+        down_swap.wait_recv()
+        for i in range(2):
+            gd_ref[i * down.shape[0] : (i + 1) * down.shape[0]] = wide(fd[i])
+        gu_swaps[3].wait_recv()
+        for i in range(2):
+            for k in range(4):
+                for m in range(8):
+                    col = 256 * (4 * (m % 4) + k) + 128 * i
+                    dst = gate_ref if m < 4 else up_ref
+                    dst[:, col : col + 128] = wide(fg[i, k // 2, k % 2, :, m * 128 : (m + 1) * 128])
         swaps[3].wait_recv()
         go_ref[...] = wide(ro[0]) + wide(ro[1])
         swaps[4].wait_recv()
@@ -841,37 +913,154 @@
                     col = (m // 2) * MODEL_WIDTH + (2 * pair + m % 2) * E
                     gq_ref[:, col : col + E] = wide(fq[i, k // 2, k % 2, :, m * EP : m * EP + E])
         line_s.finish()
-        for copy in swaps + hops + [to_c]:
+        for copy in swaps + hops + gu_swaps + [to_c, down_swap]:
             copy.wait_send()
 
     stages = [pltpu.VMEM((2, rows_o, w), bf16), pltpu.VMEM((3,) + small.shape, f32), pltpu.VMEM((3,) + small.shape, f32),
               pltpu.VMEM((4,) + small.shape, f32)]
     return comm_call(
-        body, "end", ident, (da_parts, out_parts, qkv, wo, small, x, resid, dresid, gain), [VM] * 9,
-        [shape((n, w), bf16), shape((n, w), f32), shape((rows_q, 3 * MODEL_WIDTH), f32), shape((rows_o, w), f32), shape(small.shape, f32)],
-        [VM] * 5,
-        scatter_scratch(n, w) * 2 + line_scratch(*qkv.shape[1:]) + line_scratch(rows_o, w)
+        body, "end", ident, (da_parts, qkv, wo, gu, down, small, x, dresid, gain), [VM] * 9,
+        [shape((n, w), f32), shape((rows_q, 3 * MODEL_WIDTH), f32), shape((rows_o, w), f32),
+         shape((rows_q, FF), f32), shape((rows_q, FF), f32), shape((2 * down.shape[0], w), f32), shape(small.shape, f32)],
+        [VM] * 7,
+        scatter_scratch(n, w) + line_scratch(*qkv.shape[1:]) + line_scratch(rows_o, w)
         + [pltpu.VMEM(qkv.shape[1:], bf16), pltpu.VMEM((2, 2, rows_q, 6 * EP), bf16), pltpu.VMEM((2, 2, 2, rows_q, 6 * EP), bf16),
+           pltpu.VMEM((2, 2, rows_q, FF // 4), bf16), pltpu.VMEM((2, 2, 2, rows_q, FF // 4), bf16), pltpu.VMEM((2,) + down.shape, bf16),
            pltpu.VMEM((4, rows_o, w), bf16)]
-        + stages + dma_sems(2 * SCATTER_COPIES + 18 + 9),
+        + stages + dma_sems(SCATTER_COPIES + 18 + 14),
     )
 
 
-def place_gu(pieces):
-    rows = pieces.shape[3]
-
-    def body(p_ref, gate_ref, up_ref):
-        for i in range(2):
-            for k in range(4):
-                for m in range(8):
-                    col = 256 * (4 * (m % 4) + k) + 128 * i
-                    dst = gate_ref if m < 4 else up_ref
-                    dst[:, col : col + 128] = wide(p_ref[i, k // 2, k % 2, :, m * 128 : (m + 1) * 128])
-
+def back_call(mix, qkv, dcol, drow, tt, gain, dattn, xhat, s, p, z, normed, a1, out_w, qkv_w, out_parts, gu, resid, ident):
+    rows, t, _ = qkv.shape
+    n, w = out_parts.shape[2:]
+
+    def body(mix_ref, qkv_ref, dcol_ref, drow_ref, tt_ref, gain_ref, dattn_ref, xhat_ref, s_ref, p_ref, z_ref, normed_ref, a1_ref,
+             ow_ref, qw_ref, op_ref, gu_ref, resid_ref,
+             da_ref, gq_ref, go_ref, gconv_ref, gmix_ref, gg_ref, out_ref, gu_out,
+             m_ref, dq, rc, rd, rx, ry, td, tx, ty, g_got, g_made, send, recv):
+        net = Net()
+        sems = (send, recv)
+        step = pl.program_id(0)
+        line = ScatterLine(net, gu_ref, g_got, g_made, sems, SCATTER_COPIES)
+        scatter = scatter_steps(net, op_ref, rc, rd, rx, ry, td, tx, ty, sems, 0)
+
+        @pl.when(step == 0)
+        def _():
+            net.greet("xyc")
+            line.step(0)
+            next(scatter)
+            m_ref[...] = jnp.zeros_like(m_ref)
+            gmix_ref[...] = jnp.zeros_like(gmix_ref)
+            gg_ref[...] = jnp.zeros_like(gg_ref)
+            gq_ref[...] = jnp.zeros_like(gq_ref)
+            go_ref[...] = jnp.zeros_like(go_ref)
+
+        allowed = allowed_mask(dcol_ref[0], drow_ref[0])
+        scale = 1.0 / math.sqrt(E)
+        lane = lax.broadcasted_iota(jnp.int32, (1, EP), 1)
+        prob = [p_ref[0, 0], p_ref[0, 1]]
+        go_ref[...] += dot(normed_ref[0], dattn_ref[0], 0, 0)
+        dmixed = []
+        for h in range(2):
+            cols = slice(h * EP, (h + 1) * EP)
+            dn, xh = dot(dattn_ref[0], ow_ref[cols], 1, 1), xhat_ref[0, :, cols]
+            gg_ref[0:1, cols] += jnp.sum(dn * xh, axis=0, keepdims=True)
+            dc = dn * gain_ref[0:1, cols]
+            m1 = jnp.sum(dc, axis=1, keepdims=True) / E
+            m2 = jnp.sum(dc * xh, axis=1, keepdims=True) / E
+            dh = jnp.where(lane < E, s_ref[0, :, cols] * (dc - m1 - xh * m2), 0.0).astype(bf16)
+            v = qkv_ref[0, :, (4 + h) * EP : (5 + h) * EP]
+            mixed = (mix_ref[h, 0] * prob[0] + mix_ref[h, 1] * prob[1]).astype(bf16)
+            dmixed.append(dot(dh, v, 1, 1))
+            dq[:, (4 + h) * EP : (5 + h) * EP] = dot(mixed, dh, 0, 0).astype(bf16)
+        for h in range(2):
+            for c in range(2):
+                r = 2 * h + c
+                gmix_ref[r : r + 1, :] += jnp.sum(dmixed[h] * prob[c], axis=0, keepdims=True)
+        for c in range(2):
+            dp = mix_ref[0, c] * dmixed[0] + mix_ref[1, c] * dmixed[1]
+            dconv = prob[c] * (dp - jnp.sum(dp * prob[c], axis=1, keepdims=True))
+            ahead = jnp.concatenate([up(dconv, a).astype(bf16) for a in range(QWIN)], 1)
+            m_ref[c] += dot(z_ref[0, c], ahead, 0, 0)
+            ds = jnp.where(allowed, dot(ahead, tt_ref[c]), 0.0).astype(bf16)
+            q = qkv_ref[0, :, c * EP : (c + 1) * EP]
+            k = qkv_ref[0, :, (2 + c) * EP : (3 + c) * EP]
+            dq[:, c * EP : (c + 1) * EP] = (dot(ds, k) * scale).astype(bf16)
+            dq[:, (2 + c) * EP : (3 + c) * EP] = (dot(ds, q, 0, 0) * scale).astype(bf16)
+        da_ref[0] = dot(dq[...], qw_ref[...], 1, 1).astype(bf16)
+        for i in range(0, w, 384):
+            gq_ref[i : i + 384] += dot(a1_ref[0, :, i : i + 384], dq[...], 0, 0)
+
+        @pl.when(step == 1)
+        def _():
+            next(scatter)
+
+        @pl.when(step == 3)
+        def _():
+            line.step(1)
+
+        done = []
+
+        @pl.when(step == 2)
+        def _():
+            done.append(next(scatter))
+
+        @pl.when(step == 5)
+        def _():
+            line.step(2)
+
+        @pl.when(step == rows - 1)
+        def _():
+            lanes = lax.broadcasted_iota(jnp.int32, (8, t), 1)
+            for h in range(2):
+                for a in range(QWIN):
+                    total = jnp.zeros((8, t), f32)
+                    for first in range(0, t, 8):
+                        part = m_ref[h, first : first + 8, a * t : (a + 1) * t]
+                        turned = pltpu.roll(part, t - first, 1) if first else part
+                        total = total + jnp.where(lanes < t - first, turned, 0.0)
+                    gconv_ref[h, a] = total[:, :EP]
+            for half in range(2):
+                done[0](half)
+
+                def sum_of(at):
+                    total = wide(op_ref[0, 0, at]) + wide(rc[0, at]) + wide(rx[at]) + wide(ry[at])
+                    out_ref[at] = (resid_ref[at] + total).astype(bf16)
+
+                tiles(half * (n // 2), n // 2, sum_of)
+
+            def put(at, total):
+                gu_out[at] = total.astype(bf16)
+
+            line.finish(put)
+
+    row = lambda *sh: pl.BlockSpec((1,) + sh, lambda i: (i,) + (0,) * len(sh))
+    full = lambda v: pl.BlockSpec(v.shape, lambda i: (0,) * v.ndim, pipeline_mode=pl.Buffered(1))
+    keep = lambda *sh: pl.BlockSpec(sh, lambda i: (0,) * len(sh))
     return pl.pallas_call(
-        body, in_specs=[VM], out_specs=[VM] * 2, out_shape=[shape((rows, FF), f32)] * 2, name="place_gu",
-        compiler_params=pltpu.CompilerParams(vmem_limit_bytes=16 << 20),
-    )(pieces)
+        body,
+        grid=(rows,),
+        in_specs=[pl.BlockSpec(memory_space=pltpu.SMEM), row(t, 6 * EP), row(t, 1), row(1, t), full(tt), full(gain),
+                  row(t, w), row(t, 2 * EP), row(t, 2 * EP), row(2, t, t), row(2, t, t), row(t, 2 * EP), row(t, w),
+                  full(out_w), full(qkv_w), full(out_parts), full(gu), full(resid)],
+        out_specs=[row(t, w), keep(w, 6 * EP), keep(2 * EP, w), keep(2, QWIN, 8, EP), keep(8, t), keep(8, 2 * EP), keep(n, w),
+                   keep(*gu.shape[1:])],
+        out_shape=[
+            shape((rows, t, w), bf16),
+            shape((w, 6 * EP), f32),
+            shape((2 * EP, w), f32),
+            shape((2, QWIN, 8, EP), f32),
+            shape((8, t), f32),
+            shape((8, 2 * EP), f32),
+            shape((n, w), bf16),
+            shape(gu.shape[1:], bf16),
+        ],
+        scratch_shapes=[pltpu.VMEM((2, t, QWIN * t), f32), pltpu.VMEM((t, 6 * EP), bf16)] + scatter_scratch(n, w)
+        + line_scratch(*gu.shape[1:]) + dma_sems(SCATTER_COPIES + LINE_COPIES),
+        compiler_params=pltpu.CompilerParams(collective_id=ident, has_side_effects=True, vmem_limit_bytes=63 << 20),
+        name="back",
+    )(mix, qkv, dcol, drow, tt, gain, dattn, xhat, s, p, z, normed, a1, out_w, qkv_w, out_parts, gu, resid)
 
 
 def rms_scale(values):
@@ -1222,28 +1411,26 @@
     x, dy = x_in[0], cotangent[0]
     rows = w_qkv.shape[0]
 
+    kernel = lax.dynamic_slice_in_dim(conv_kernel, 2 * pair, 2, 0)
+    mix = lax.dynamic_slice_in_dim(head_mix, 2 * pair, 2, 0)
     gains = jnp.pad(jnp.stack([gain_attn, gain_group, gain_ffn]), ((0, 13), (0, 128 - rows)))
     docs = jnp.broadcast_to(doc_ids, (8, tokens))
-    x_all, dffn_all, docs, gains, qkv_w, gu_plane, out_w = start_call(x, dy, docs, gains, w_qkv, w_gate, w_up, w_out, 1)
+    a1, dffn_all, docs, gains, qkv_w, gu_plane, out_w, th, tl, tt = start_call(
+        x, dy, docs, gains, kernel.reshape(-1), w_qkv, w_gate, w_up, w_out, 1
+    )
     docs = docs.reshape(8, 8, tokens)[:, 0]
-    gains = gains.reshape(16, 16, 128)[:, :3, :rows].astype(f32).transpose(1, 0, 2).reshape(3, MODEL_WIDTH)
     gain_a, gain_g, gain_f = gains[0:1], gains[1], gains[2:3]
     qkv_w = qkv_w.reshape(MODEL_WIDTH, 6 * EP)
     keep = lax.dynamic_index_in_dim(out_w, 2 * links.x + links.c, 0, keepdims=False)
     other = links.across("c", lax.dynamic_index_in_dim(out_w, 2 * links.x + 1 - links.c, 0, keepdims=False))
     out_w = jnp.pad(join(links.c, keep, other, 0), ((0, 0), (0, EP - E), (0, 0))).reshape(2 * EP, MODEL_WIDTH)
 
-    kernel = lax.dynamic_slice_in_dim(conv_kernel, 2 * pair, 2, 0)
-    mix = lax.dynamic_slice_in_dim(head_mix, 2 * pair, 2, 0)
-    th, tl, tt = bands(kernel, tokens)
     group = lax.dynamic_slice_in_dim(gain_g.reshape(8, 2, E), pair, 1, 0)
     group = jnp.pad(group, ((0, 0), (0, 0), (0, EP - E))).reshape(1, 2 * EP)
     doc_col, doc_row = docs[:, :, None], docs[:, None, :]
 
-    x_all = x_all.reshape(8 * tokens, MODEL_WIDTH)
     dffn_all = dffn_all.reshape(8 * tokens, MODEL_WIDTH)
-    xf_all = x_all.astype(f32)
-    a1 = (xf_all * rms_scale(xf_all) * gain_a).astype(bf16)
+    a1 = a1.reshape(8 * tokens, MODEL_WIDTH)
     qkv = dot(a1, qkv_w).astype(bf16).reshape(8, tokens, 6 * EP)
     normed, xhat, s, probs, zeroed = attend(mix, qkv, doc_col, doc_row, th, tl, group)
     normed = normed.reshape(8 * tokens, 2 * EP)
@@ -1266,26 +1453,14 @@
     grad_gu = dot(a2, dgu, 0, 0).astype(bf16).reshape(4, 4 * rows, FF // 4)
     grad_down = dot(hidden, dffn_all, 0, 0).astype(bf16).reshape(4, FF // 32, MODEL_WIDTH)
     out_parts = by_chip(dot(hidden, down_w))
-    dresid, dattn, sum_f, grad_gu, grad_down = mid_back_call(
-        by_chip(dot(dgu, gu_w, 1, 1)), dy, resid, gain_f, grad_gu, grad_down, 3
+    dresid, dattn, sum_f, grad_down = mid_back_call(by_chip(dot(dgu, gu_w, 1, 1)), dy, resid, gain_f, grad_down, 3)
+    by_row = lambda v: v.reshape(8, tokens, -1)
+    da_parts, grad_qkv, grad_out, conv_tiles, mix_sums, group_sums, out, grad_gu = back_call(
+        mix, qkv, doc_col, doc_row, tt, group, by_row(dattn), xhat, s, probs, zeroed, by_row(normed), by_row(a1), out_w, qkv_w,
+        out_parts, grad_gu, resid, 5
     )
-    v = grad_gu.reshape(2, 2, rows, FF // 4)
-    sent = links.across("c", lax.dynamic_index_in_dim(v, 1 - links.c, 1, keepdims=False))
-    v = join(links.c, lax.dynamic_index_in_dim(v, links.c, 1, keepdims=False), sent, 1)
-    sent = links.across("y", lax.dynamic_index_in_dim(v, 1 - links.y, 0, keepdims=False))
-    v = join(links.y, lax.dynamic_index_in_dim(v, links.y, 0, keepdims=False), sent, 0)
-    grad_gate, grad_up = place_gu(join(links.x, v, links.across("x", v), 0))
-    grad_down = join(links.x, grad_down, links.across("x", grad_down), 0).reshape(-1, MODEL_WIDTH).astype(f32)
-
-    dattn = dattn.reshape(8 * tokens, MODEL_WIDTH)
-    dnormed = dot(dattn, out_w, 1, 1).reshape(8, tokens, 2 * EP)
-    dqkv, conv_tiles, mix_sums, group_sums = attend_back(
-        mix, qkv, doc_col, doc_row, tt, group, dnormed, xhat, s, probs, zeroed
-    )
-    dqkv = dqkv.reshape(8 * tokens, 6 * EP)
-    grad_qkv = dot(a1, dqkv, 0, 0)
     sum_a = jnp.sum(grad_qkv * qkv_w.astype(f32), axis=1) / gain_a[0]
-    grad_out = dot(normed, dattn, 0, 0).astype(bf16).reshape(2, EP, MODEL_WIDTH)[:, :rows]
+    grad_out = grad_out.astype(bf16).reshape(2, EP, MODEL_WIDTH)[:, :rows]
     place = lambda v: lax.dynamic_update_index_in_dim(jnp.zeros((8,) + v.shape, f32), v, pair, 0)
     small = [
         sum_a,
@@ -1299,14 +1474,14 @@
         cut.append(cut[-1] + v.size)
     room = 48 * 128
     flat = jnp.concatenate([v.reshape(-1) for v in small] + [jnp.zeros((room - cut[-1],), f32)]).reshape(48, 128)
-    out, grad_x, grad_qkv, grad_out, total = end_call(
-        by_chip(dot(dqkv, qkv_w, 1, 1)),
-        out_parts,
+    grad_x, grad_qkv, grad_out, grad_gate, grad_up, grad_down, total = end_call(
+        by_chip(da_parts),
         grad_qkv.astype(bf16).reshape(4, 4 * rows, 6 * EP),
         grad_out,
+        grad_gu,
+        grad_down,
         flat,
         x,
-        resid,
         dresid,
         gain_a,
         4,

time: 566 us -> 537 us (0.949)
  Pallas kernels: 396 us -> 426 us
  matrix products: 85.5 us -> 61.4 us
  other arithmetic: 27.7 us -> 9.45 us
  waiting for transfers between devices: 17.7 us -> 0.01 us
    pallas_call x2 -> x1, Pallas kernels: 23.6 us -> 74.1 us  [back_call(): pl.pallas_call(body, grid=(rows,), in_specs=[pl.BlockSpec(memory_space=pl...]
    dot_general x12 -> x8, matrix products: 85.5 us -> 61.4 us  [dot(): lax.dot_general(a, b, (((ca,), (cb,)), ((), ())), preferred_element_type=...]
    pallas_call x4, Pallas kernels: 352 us -> 331 us  [comm_call(): pl.pallas_call(body, in_specs=in_specs, out_specs=out_specs, out_shape=ou...]
    convert_element_type x4 -> x1, other arithmetic: 18.9 us -> 0.08 us  [fast(): grad_out = grad_out.astype(bf16).reshape(2, EP, MODEL_WIDTH)[:, :rows]]
    ppermute x2 -> x0, waiting for transfers between devices: 17.7 us -> none  [across(): return lax.ppermute(v, 'rep', [(0, 1), (1, 0)])]
    unnamed x83 -> x48, local copies, waits for them, and re-layouts: 7.13 us -> 13.2 us
  transfers between devices with their start and end apart: 5 -> 1, of which waited for: 1 -> 0; matrix products, arithmetic and copies ran while one was open for 10% -> 3% of each run, Pallas kernels for 20% -> 4%
where the time goes in v3:
time: 537 us; the launch traced here: 530 us
  Pallas kernels  426 us (79%)
  matrix products  61.4 us (11%)
  local copies, waits for them, and re-layouts  30.7 us (6%)
  other arithmetic  9.45 us (2%)
    pallas_call x4, Pallas kernels, comm_call(): pl.pallas_call(body, in_specs=in_specs, out_specs=out_specs, out_shape=ou...  331 us
    pallas_call x1, Pallas kernels, back_call(): pl.pallas_call(body, grid=(rows,), in_specs=[pl.BlockSpec(memory_space=pl...  74.1 us
    dot_general x8, matrix products, dot(): lax.dot_general(a, b, (((ca,), (cb,)), ((), ())), preferred_element_type=...  61.4 us
    pallas_call x1, Pallas kernels, attend(): pl.pallas_call(fwd_kernel, grid=(n,), in_specs=[pl.BlockSpec(memory_space...  20.7 us
    unnamed x48, local copies, waits for them, and re-layouts  13.2 us
  transfers between devices with their start and end apart: 1, of which 0 were waited for; matrix products, arithmetic and copies ran while one was open for 3% of the time, Pallas kernels for 4%

profile of v3, /device:TPU:16, one launch (start us, length us, event | category | flops | bytes accessed | tf_op | source)
XLA Modules:
  0.0 529.5 jit_solution(7097834228442184494)
XLA Ops:
  0.6 0.0 copy-start
  0.7 0.7 copy-done
  1.4 0.1 constant_dynamic-slice_fusion.1
  1.5 0.1 copy.30
  1.7 0.7 reshape.194.taps_ref
  2.3 1.3 fusion.14.g_ref
  3.6 1.3 broadcast_in_dim.36.docs_ref
  4.9 77.5 %start.1 = (bf16[4,2,256,1536]{3,2,1,0:T(8,128)(2,1)}, bf16[4,2,256,1536]{3,2,1,0:T(8,128)(2,1)}, s32[4,2,8,256]{3,2,1,0:T(8,128)}, f32[8,1536]{1,0:T(8,128)}, b...) custom-call(bf16[256,1536]{1,0:T(8,128)(2,1)} %bitcast.76, ...), custom_call_target="tpu_custom_call" | custom-call | tf_op jit(solution)/shard_map/start/pallas_call | solution.py:536
  82.4 1.0 dynamic-slice_bitcast_fusion
  83.4 0.6 collective-permute-start
  84.0 0.1 constant_dynamic-slice_fusion.2
  84.1 0.7 copy.36.mix_ref
  84.7 1.4 fusion.17
  86.1 1.3 copy.32.dcol_ref
  87.5 1.5 fusion.18
  89.0 0.1 reshape_squeeze.6
  89.1 9.0 %convolution_convert_fusion.4 = bf16[2048,768]{1,0:T(8,128)(2,1)} fusion(bf16[2048,1536]{1,0:T(8,128)(2,1)} %bitcast.82, bf16[1536,768]{1,0:T(8,128)(2,1)} %bitcast.73), kind=kOutput, calls=%fused_computation.11 | convolution fusion | flops 4833411072 | bytes 11796480 | tf_op jit(solution)/shard_map/dot_general | solution.py:42
  98.1 0.6 pad.13
  98.7 20.7 %attend.1 = (bf16[8,256,256]{2,1,0:T(8,128)(2,1)}, f32[8,256,256]{2,1,0:T(8,128)}, f32[8,256,256]{2,1,0:T(8,128)}, f32[8,2,256,256]{3,2,1,0:T(8,128)}, bf16[8,2,256,256]{3,2,1,0:T(8,128)(2,1)}) custom-call(f32[2,2]{1,0:T(2,128)} %copy.36.mix_ref, bf16[8,256,768]{2,1,0:T(8,128)(2,1)} %bitcast.88, s32[8,256,1]{2,1,0:T(8,128)} %copy.32.dcol_ref, ...), custom_call_target="tpu_custom_call" | custom-call | flops 9663676416 | bytes 10485760 | tf_op jit(solution)/shard_map/attend/pallas_call | solution.py:91
  119.3 0.0 copy-start.3
  119.4 1.1 fusion.4
  120.5 0.1 fusion.3
  120.5 0.0 copy-start.2
  120.6 0.1 copy-done.3
  120.7 4.5 convolution_convert_fusion
  125.1 83.3 %mid.1 = (f32[256,1536]{1,0:T(8,128)}, bf16[4,2,256,1536]{3,2,1,0:T(8,128)(2,1)}, bf16[4,4,96,1024]{3,2,1,0:T(8,128)(2,1)}, bf16[4,128,1536]{2,1,0:T(8,128)(2,1)}) custom-call(bf16[4,2,256,1536]{3,2,1,0:T(8,128)(2,1)} %bitcast.72, bf16[256,1536]{1,0:T(8,128)(2,1)} %bitcast.77, f32[1,1536]{1,0:T(1,128)} %get-tuple-element.112.g_ref, ...), custom_call_target="tpu_custom_call" | custom-call | tf_op jit(solution)/shard_map/mid/pallas_call | solution.py:536
  208.5 11.9 %fusion.19 = f32[2048,1024]{0,1:T(8,128)} fusion(bf16[2048,1536]{1,0:T(8,128)(2,1)} %bitcast.112, bf16[1536,1024]{1,0:T(8,128)(2,1)} %bitcast.116), kind=kOutput, calls=%fused_computation.50 | convolution fusion | flops 6442450944 | bytes 17825792 | tf_op jit(solution)/shard_map/dot_general | solution.py:42
  220.4 7.3 %multiply_convert_fusion.2 = (bf16[2048,512]{0,1:T(8,128)(2,1)S(1)}, bf16[2048,512]{0,1:T(8,128)(2,1)S(1)}, bf16[2048,512]{0,1:T(8,128)(2,1)S(1)}) fusion(f32[2048,1024]{0,1:T(8,128)} %fusion.19, bf16[2048,1536]{1,0:T(8,128)(2,1)S(1)} %bitcast.110, bf16[512,1536]{1,0:T(8,128)(2,1)S(1)} %bitcast.118), kind=kOutput, calls=%fused_computation.7 | convolution fusion | flops 3236954112 | bytes 22544384 | tf_op jit(solution)/shard_map/dot_general | solution.py:42
  227.8 4.5 convolution_convert_fusion.5
  232.3 5.3 %convolution_convert_fusion.1 = bf16[2048,1536]{1,0:T(8,128)(2,1)} fusion(bf16[2048,512]{0,1:T(8,128)(2,1)S(1)} %get-tuple-element.104, bf16[512,1536]{1,0:T(8,128)(2,1)S(1)} %bitcast.119), kind=kOutput, calls=%fused_computation.1 | convolution fusion | flops 3224371200 | bytes 9961472 | tf_op jit(solution)/shard_map/dot_general | solution.py:42
  237.6 9.3 %convolution_convert_fusion.2 = bf16[2048,1536]{1,0:T(8,128)(2,1)} fusion(bf16[1536,1024]{1,0:T(8,128)(2,1)S(1)} %bitcast.117, bf16[2048,512]{0,1:T(8,128)(2,1)S(1)} %get-tuple-element.103, bf16[2048,512]{0,1:T(8,128)(2,1)S(1)} %get-tuple-element.102), kind=kOutput, calls=%fused_computation.2 | convolution fusion | flops 6453985280 | bytes 13631488 | tf_op jit(solution)/shard_map/dot_general | solution.py:42
  246.9 9.5 %convolution_convert_fusion.3 = bf16[1536,1024]{1,0:T(8,128)(2,1)} fusion(bf16[2048,1536]{1,0:T(8,128)(2,1)S(1)} %bitcast.115, bf16[2048,512]{0,1:T(8,128)(2,1)S(1)} %get-tuple-element.103, bf16[2048,512]{0,1:T(8,128)(2,1)S(1)} %get-tuple-element.102), kind=kOutput, calls=%fused_computation.10 | convolution fusion | flops 6452412416 | bytes 13631488 | tf_op jit(solution)/shard_map/dot_general | solution.py:42
  256.4 70.3 %mid_back.1 = (f32[256,1536]{1,0:T(8,128)}, bf16[4,2,256,1536]{3,2,1,0:T(8,128)(2,1)}, f32[8,1536]{1,0:T(8,128)}, bf16[128,1536]{1,0:T(8,128)(2,1)}) custom-call(bf16[4,2,256,1536]{3,2,1,0:T(8,128)(2,1)} %bitcast.87, bf16[256,1536]{1,0:T(8,128)(2,1)} %bitcast.92, f32[256,1536]{1,0:T(8,128)} %get-tuple-element.64.r_ref.resid_ref, ...), custom_call_target="tpu_custom_call" | custom-call | tf_op jit(solution)/shard_map/mid_back/pallas_call | solution.py:536
  326.7 74.1 %back.1 = (bf16[8,256,1536]{2,1,0:T(8,128)(2,1)}, f32[1536,768]{1,0:T(8,128)}, f32[256,1536]{1,0:T(8,128)}, f32[2,6,8,128]{3,2,1,0:T(8,128)}, f32[8,256]{1,0:T(8...) custom-call(f32[2,2]{1,0:T(2,128)} %copy.36.mix_ref, ...), custom_call_target="tpu_custom_call" | custom-call | tf_op jit(solution)/shard_map/back/pallas_call | solution.py:1041
  400.8 6.7 %multiply_reduce_fusion = (f32[1536]{0:T(1024)S(1)}, bf16[1536,768]{1,0:T(8,128)(2,1)}) fusion(f32[1536,768]{1,0:T(8,128)} %get-tuple-element.72, bf16[4,4,96,768]{3,2,1,0:T(8,128)(2,1)} %get-tuple-element.51), kind=kLoop, calls=%fused_computation.3 | loop fusion | flops 4717056 | bytes 9443328 | tf_op jit(solution)/shard_map/reduce_sum | solution.py:1462
  407.5 0.1 convert_element_type.52
  407.6 0.9 slice.115.wo_ref
  408.5 0.8 slice_reduce_fusion
  409.3 0.7 slice.92
  410.0 0.1 broadcast_in_dim.39
  410.1 0.1 reshape.215
  410.2 0.2 add_bitcast_fusion
  410.4 0.2 reshape.216
  410.5 0.1 slice_reduce_fusion.2
  410.7 0.1 reshape.217
  410.8 0.7 concatenate.7
  411.5 100.1 %end.1 = (f32[256,1536]{1,0:T(8,128)}, f32[96,4608]{1,0:T(8,128)}, f32[96,1536]{1,0:T(8,128)}, f32[96,4096]{1,0:T(8,128)}, f32[96,4096]{1,0:T(8,128)}, /*index=5*/f32[256,1536]{1,0:T(8,128)}, f32[48,128]{1,0:T(8,128)}) custom-call(bf16[4,2,256,1536]{3,2,1,0:T(8,128)(2,1)} %bitcast.86, bf16[4,384,768]{2,1,0:T(8,128)(2,1)} %bitcast.75, ...), custom_call_target="tpu_custom_call" | custom-call | tf_op jit(solution)/shard_map/end/pallas_call | solution.py:536
  511.6 0.8 slice_bitcast_fusion
  512.4 2.4 slice.108
  514.8 0.6 dynamic_slice.30
  515.4 0.6 dynamic_slice.31
  516.0 0.7 slice.116
  516.7 0.2 reshape.220
  516.8 0.8 copy.34
  517.6 0.6 copy.35
  518.2 0.6 dynamic_slice.32
  518.8 2.1 copy.48
  520.9 2.7 copy.49
  523.6 1.2 copy.50
  524.8 0.8 copy.51
  525.6 0.0 copy-done.7
  525.6 1.1 copy.52
  526.8 1.1 copy.53
  527.9 1.1 copy.54
  (45 shorter events, 0.2 us)
Async XLA Ops:
  0.6 0.8 copy-start
  0.7 83.3 %copy-start.12 = (f32[16,2]{0,1:T(2,128)S(1)}, f32[16,2]{0,1:T(2,128)}, u32[]{:S(2)}) copy-start(f32[16,2]{0,1:T(2,128)} %param.20) | copy-start | bytes 388
  83.4 36.0 %collective-permute-start = (bf16[96,1536]{1,0:T(8,128)(2,1)S(1)}, bf16[96,1536]{1,0:T(8,128)(2,1)S(1)}, u32[]{:S(2)}, u32[]{:S(2)}) collective-permute-start(bf16[96,1536]{1,0:T(8,128)(2,1)S(1)} %dynamic-slice_bitcast_fusion), channel_id=1, source_target_pairs={{0,1},{1,0},{2,3},{3,2},{4,5},{5,4},{6,7},{7,6},{8,9},{9,8},{10,11... | collective-permute-start | bytes 884744 | tf_op jit(solution)/shard_map/ppermute | solution.py:1081
  119.3 1.3 copy-start.3
  120.5 4.6 copy-start.2
  125.1 95.3 %slice-start = ((s8[6291456]{0:T(1024)(128)(4,1)}), s8[2097152]{0:T(1024)(128)(4,1)S(1)}, s32[]{:S(2)}) async-start(s8[6291456]{0:T(1024)(128)(4,1)} %bitcast.108), calls=%async_computation | async-start | bytes 4194304
  208.5 11.9 %slice-start.1 = ((s8[6291456]{0:T(1024)(128)(4,1)}), s8[4194304]{0:T(1024)(128)(4,1)S(1)}, s32[]{:S(2)}) async-start(s8[6291456]{0:T(1024)(128)(4,1)} %bitcast.108), calls=%async_computation.1 | async-start | bytes 8388608
  208.5 11.9 %copy-start.14 = (bf16[4,128,1536]{2,1,0:T(8,128)(2,1)S(1)}, bf16[4,128,1536]{2,1,0:T(8,128)(2,1)}, u32[]{:S(2)}) copy-start(bf16[4,128,1536]{2,1,0:T(8,128)(2,1)} %get-tuple-element.61) | copy-start | bytes 4718596
  232.3 5.3 %copy-start.13 = (bf16[4,4,96,1024]{3,2,1,0:T(8,128)(2,1)S(1)}, bf16[4,4,96,1024]{3,2,1,0:T(8,128)(2,1)}, u32[]{:S(2)}) copy-start(bf16[4,4,96,1024]{3,2,1,0:T(8,128)(2,1)} %get-tuple-element.63) | copy-start | bytes 9437188
  232.3 14.6 %slice-start.2 = ((s8[6291456]{0:T(1024)(128)(4,1)}), s8[4194304]{0:T(1024)(128)(4,1)S(1)}, s32[]{:S(2)}) async-start(s8[6291456]{0:T(1024)(128)(4,1)} %bitcast.113), calls=%async_computation.2 | async-start | bytes 8388608
  237.6 9.3 %slice-start.3 = ((s8[6291456]{0:T(1024)(128)(4,1)}), s8[2097152]{0:T(1024)(128)(4,1)S(1)}, s32[]{:S(2)}) async-start(s8[6291456]{0:T(1024)(128)(4,1)} %bitcast.113), calls=%async_computation.3 | async-start | bytes 4194304
  400.8 6.7 %copy-start.8 = (f32[256,1536]{1,0:T(8,128)S(1)}, f32[256,1536]{1,0:T(8,128)}, u32[]{:S(2)}) copy-start(f32[256,1536]{1,0:T(8,128)} %get-tuple-element.73) | copy-start | bytes 4718596
  407.5 2.7 copy-start.10
  407.5 3.0 copy-start.11
  512.4 11.2 %copy-start.4 = (f32[96,4608]{1,0:T(8,128)S(1)}, f32[96,4608]{1,0:T(8,128)}, u32[]{:S(2)}) copy-start(f32[96,4608]{1,0:T(8,128)} %get-tuple-element.132) | copy-start | bytes 5308420
  520.9 3.9 copy-start.9
  523.6 2.0 copy-start.7
  523.6 3.2 copy-start.6
  525.6 2.3 copy-start.5
  525.6 3.4 copy-start.1
